TPU v7x, 32 devices: a whole 2x2x4 slice. The times are simulated.
32 devices in a mesh: freq: 2 (over x), panel: 16 (over z, y, core).
Axes of the slice: x: 2, y: 2, z: 4, core: 2. Of those that a mesh axis runs over, the one named last changes fastest.
Arguments:
- recorded: float32 [2, 2, 2048, 2048], P('freq', None, 'panel'), parts along dimension 0, may hold values from -60 to 60
- receiver_kernel: bfloat16 [2, 2, 4095], P('freq'), parts along dimension 0, may hold values from -1.5 to 1.5
- source_kernel: bfloat16 [2, 2, 4095], P('freq'), parts along dimension 0, may hold values from -1.5 to 1.5
Outputs:
- primaries: float32 [2, 2, 2048, 2048], P('freq', None, 'panel'), parts along dimension 0
- multiples: bfloat16 [2, 2, 2048, 2048], P('freq', None, 'panel'), parts along dimension 0
There are 2 independent parts, one for each index of `freq`. A program takes and returns all parts, laid end to end along the dimension named above; each array names one. Nothing has to cross between parts.
All inputs are finite; a program needn't handle non-finite values.
Results may differ from a plain program's by a relative error of at most 0.0057.
Values may be sent and summed in bfloat16 or wider, within the bound.
No kernel may reach another device: no remote copies, remote signals or barrier semaphores. Data moves between devices by JAX's collectives and lax.ppermute only.
A program may use at most 320 MiB of HBM per device.

v0:
```python
import jax
import jax.numpy as jnp
from jax import lax
from jax.sharding import PartitionSpec as P


def band(kernel, base, nrows, ncols):
    length = nrows + ncols - 1
    piece = lax.dynamic_slice_in_dim(kernel, base - nrows + 1, length, 1)
    rolled = jnp.roll(piece, -(nrows - 1), axis=1)
    flat = jnp.tile(rolled, (1, nrows))[:, : nrows * (length - 1)]
    return flat.reshape(2, nrows, length - 1)[:, :, :ncols]


def complex_dot(left, right):
    real_part = jnp.dot(left[0], right[0], preferred_element_type=jnp.float32) - jnp.dot(
        left[1], right[1], preferred_element_type=jnp.float32
    )
    imag_part = jnp.dot(left[0], right[1], preferred_element_type=jnp.float32) + jnp.dot(
        left[1], right[0], preferred_element_type=jnp.float32
    )
    return jnp.stack([real_part, imag_part])


def per_device(recorded, receiver_kernel, source_kernel):
    freqs, rows, width = (recorded.shape[0], recorded.shape[2], recorded.shape[3])
    panels = lax.axis_size("panel")
    sources = rows * panels
    data_b = recorded.astype(jnp.bfloat16)
    focused = jnp.stack(
        [complex_dot(data_b[0], band(receiver_kernel[0], width - 1, width, width))]
    ).astype(jnp.bfloat16)
    row_first = lax.axis_index("panel") * rows
    local_oper = jnp.stack([band(source_kernel[0], sources - 1 - row_first, rows, sources)])
    oper = local_oper[0]
    parts = [complex_dot(oper, lax.all_gather(focused, "panel", axis=2, tiled=True)[0])]
    summed = jnp.stack(parts)
    mult = summed.astype(jnp.bfloat16)
    mfl = mult.astype(jnp.float32)
    num_re = jnp.sum(mfl[:, 0] * recorded[:, 0] + mfl[:, 1] * recorded[:, 1], axis=(1, 2))
    num_im = jnp.sum(mfl[:, 0] * recorded[:, 1] - mfl[:, 1] * recorded[:, 0], axis=(1, 2))
    energy = jnp.sum(mfl[:, 0] * mfl[:, 0] + mfl[:, 1] * mfl[:, 1], axis=(1, 2))
    num_re, num_im, energy = lax.psum((num_re, num_im, energy), "panel")
    den = energy + 1e-06
    fit_re = (num_re / den)[:, None, None]
    fit_im = (num_im / den)[:, None, None]
    prim_re = recorded[:, 0] - (fit_re * mfl[:, 0] - fit_im * mfl[:, 1])
    prim_im = recorded[:, 1] - (fit_re * mfl[:, 1] + fit_im * mfl[:, 0])
    return (jnp.stack([prim_re, prim_im], axis=1), mult)


def solution(mesh):
    placed = (P("freq", None, "panel", None), P("freq", None, None), P("freq", None, None))
    return jax.shard_map(
        per_device,
        mesh=mesh,
        in_specs=placed,
        out_specs=(P("freq", None, "panel", None), P("freq", None, "panel", None)),
        check_vma=False,
    )
```

profile of v0, /device:TPU:0, one launch (start us, length us, event | category | flops | bytes accessed | tf_op | source)
XLA Modules:
  0.0 487.0 jit_solution(3146243379102983382)
XLA Ops:
  7.2 0.0 copy-start
  7.2 0.0 all-gather.2.cloned.1.call-start
  7.2 0.8 slice.112
  8.0 0.7 slice.113
  8.7 11.0 %tile.20 = bf16[2,2048,4095]{2,1,0:T(8,128)(2,1)} broadcast(bf16[2,4095]{1,0:T(2,128)(2,1)S(1)} %pad_maximum_fusion.3), dimensions={0,2} | broadcast | bytes 33562620 | tf_op jit(solution)/shard_map/tile | solution.py:11
  19.7 69.5 %reshape.271 = bf16[16773120]{0:T(1024)(128)(2,1)} reshape(bf16[2,2048,4095]{2,1,0:T(8,128)(2,1)} %tile.20) | data formatting | bytes 67092480
  89.2 39.9 %tile.21 = bf16[2,8386560]{1,0:T(2,128)(2,1)} reshape(bf16[16773120]{0:T(1024)(128)(2,1)} %reshape.271) | data formatting | bytes 67092480 | tf_op jit(solution)/shard_map/tile | solution.py:11
  129.2 27.0 %slice.114 = bf16[2,8384512]{1,0:T(2,128)(2,1)} slice(bf16[2,8386560]{1,0:T(2,128)(2,1)} %tile.21), slice={[0:2], [0:8384512]} | slice | bytes 67076096 | tf_op jit(solution)/shard_map/slice | solution.py:11
  156.2 52.8 %reshape.273 = bf16[16769024]{0:T(1024)(128)(2,1)} reshape(bf16[2,8384512]{1,0:T(2,128)(2,1)} %slice.114) | data formatting | bytes 67076096
  209.0 0.0 copy-start.1
  209.0 53.4 %reshape.270 = bf16[2,2048,4094]{2,1,0:T(8,128)(2,1)} reshape(bf16[16769024]{0:T(1024)(128)(2,1)} %reshape.273) | data formatting | bytes 67076096 | tf_op jit(solution)/shard_map/reshape | solution.py:12
  262.3 0.0 copy-done.1
  262.4 0.1 convert_element_type.36
  262.5 5.8 %fusion.1 = f32[2048,128]{1,0:T(8,128)S(1)} fusion(bf16[2,2048,4094]{2,1,0:T(8,128)(2,1)} %reshape.270, bf16[1,2,128,2048]{3,2,1,0:T(8,128)(2,1)S(1)} %convert_element_type.36), kind=kOutput, calls=%fused_computation.5 | convolution fusion | flops 1073741824 | bytes 9961472 | tf_op jit(solution)/shard_map/dot_general | solution.py:16
  268.3 5.8 %fusion = f32[2048,128]{1,0:T(8,128)S(1)} fusion(bf16[2,2048,4094]{2,1,0:T(8,128)(2,1)} %reshape.270, bf16[1,2,128,2048]{3,2,1,0:T(8,128)(2,1)S(1)} %convert_element_type.36), kind=kOutput, calls=%fused_computation.4 | convolution fusion | flops 1073741824 | bytes 9961472 | tf_op jit(solution)/shard_map/dot_general | solution.py:19
  274.2 5.8 %fusion.18 = bf16[1,1,128,2048]{2,3,1,0:T(8,128)(2,1)S(1)} fusion(f32[2048,128]{1,0:T(8,128)S(1)} %fusion.1, bf16[2,2048,4094]{2,1,0:T(8,128)(2,1)} %reshape.270, bf16[1,2,128,2048]{3,2,1,0:T(8,128)(2,1)S(1)} %convert_element_type.36), kind=kOutput, calls=%fused_computation.22 | convolution fusion | flops 1074266112 | bytes 10485760 | tf_op jit(solution)/shard_map/dot_general | solution.py:16
  280.0 5.8 %fusion.19 = bf16[1,1,128,2048]{2,3,1,0:T(8,128)(2,1)S(1)} fusion(f32[2048,128]{1,0:T(8,128)S(1)} %fusion, bf16[2,2048,4094]{2,1,0:T(8,128)(2,1)} %reshape.270, bf16[1,2,128,2048]{3,2,1,0:T(8,128)(2,1)S(1)} %convert_element_type.36), kind=kOutput, calls=%fused_computation.23 | convolution fusion | flops 1074266112 | bytes 10485760 | tf_op jit(solution)/shard_map/dot_general | solution.py:19
  285.8 1.1 pad_maximum_fusion.1
  286.9 0.0 all-gather.2.cloned.1.call-update
  286.9 0.0 copy-done
  286.9 0.1 dynamic-slice_bitcast_fusion
  287.0 0.1 slice.108
  287.1 0.1 tile.8
  287.2 2.5 reshape.275
  289.7 3.0 tile.9
  292.7 2.0 slice.110
  294.7 3.1 reshape.277
  297.8 3.0 reshape.269
  300.8 0.0 copy-start.3
  300.8 118.8 %all-gather.2.cloned.1.call-done = bf16[1,2,2048,2048]{2,3,1,0:T(8,128)(2,1)} async-done(((bf16[1,2,128,2048]{2,3,1,0:T(8,128)(2,1)}), bf16[1,2,2048,2048]{2,3,1,0:T(8,128)(2,1)}) %all-gather.2.cloned.1.call-update) | async-done | bytes 16777232 | tf_op jit(solution)/shard_map/all_gather | solution.py:36
  419.7 0.0 copy-start.4
  419.7 6.6 %fusion.5 = f32[128,2048]{1,0:T(8,128)S(1)} fusion(bf16[1,2,2048,2048]{2,3,1,0:T(8,128)(2,1)} %all-gather.2.cloned.1.call-done, bf16[2,128,2174]{2,1,0:T(8,128)(2,1)} %reshape.269), kind=kOutput, calls=%fused_computation.9 | convolution fusion | flops 1073741824 | bytes 9961472 | tf_op jit(solution)/shard_map/dot_general | solution.py:16
  426.2 0.0 copy-done.3
  426.3 7.0 %fusion.4 = f32[128,2048]{1,0:T(8,128)S(1)} fusion(bf16[1,2,2048,2048]{2,3,1,0:T(8,128)(2,1)} %all-gather.2.cloned.1.call-done, bf16[2,128,2174]{2,1,0:T(8,128)(2,1)S(1)} %copy-done.3), kind=kOutput, calls=%fused_computation.8 | convolution fusion | flops 1073741824 | bytes 9961472 | tf_op jit(solution)/shard_map/dot_general | solution.py:19
  433.3 0.0 copy-done.4
  433.3 2.9 fusion.16
  436.2 2.9 fusion.17
  439.1 1.2 fusion.20
  440.3 0.0 copy-start.2
  440.3 1.3 copy-done.2
  441.6 1.6 add_reduce_fusion.1
  443.2 31.4 %all-reduce = (f32[1]{0:T(128)}, f32[1]{0:T(128)}, f32[1]{0:T(128)}) all-reduce(f32[1]{0:T(128)} %bitcast.19, f32[1]{0:T(128)} %bitcast.17, f32[1]{0:T(128)} %bitcast.16), channel_id=1, replica_groups=mesh['freq'=2,'panel'=16] {'panel'}, use_global_device_ids=true, to_apply=%region_5.6 | all-reduce | flops 3 | bytes 24 | tf_op jit(solution)/shard_map/psum | solution.py:43
  476.4 1.9 subtract_subtract_fusion
  478.3 1.5 pad_maximum_fusion
  (3 shorter events, 0.0 us)
Async XLA Ops:
  7.2 279.7 %copy-start = (bf16[1,2,4095]{2,1,0:T(2,128)(2,1)S(1)}, bf16[1,2,4095]{2,1,0:T(2,128)(2,1)}, u32[]{:S(2)}) copy-start(bf16[1,2,4095]{2,1,0:T(2,128)(2,1)} %param.5) | copy-start | bytes 49144
  7.2 412.5 %all-gather.2.cloned.1.call-start = ((), (), s32[]{:S(2)}) async-start(), calls=%async_computation | async-start | bytes 17825792 | tf_op jit(solution)/shard_map/all_gather | solution.py:36
  209.0 53.4 %copy-start.1 = (f32[1,2,128,2048]{3,2,1,0:T(8,128)S(1)}, f32[1,2,128,2048]{3,2,1,0:T(8,128)}, u32[]{:S(2)}) copy-start(f32[1,2,128,2048]{3,2,1,0:T(8,128)} %param.3) | copy-start | bytes 6291460
  300.8 125.4 %copy-start.3 = (bf16[2,128,2174]{2,1,0:T(8,128)(2,1)S(1)}, bf16[2,128,2174]{2,1,0:T(8,128)(2,1)}, u32[]{:S(2)}) copy-start(bf16[2,128,2174]{2,1,0:T(8,128)(2,1)} %reshape.269) | copy-start | bytes 3339268
  419.7 13.6 %copy-start.4 = (bf16[1,2,2048,2048]{2,3,1,0:T(8,128)(2,1)S(1)}, bf16[1,2,2048,2048]{2,3,1,0:T(8,128)(2,1)}, u32[]{:S(2)}) copy-start(bf16[1,2,2048,2048]{2,3,1,0:T(8,128)(2,1)} %all-gather.2.cloned.1.call-done) | copy-start | bytes 50331652
  440.3 1.3 copy-start.2
Sparse Core Ops, SparseCore 0:
  287.0 132.6 all-gather.1
where the time goes:
time: 496 us; the launch traced here: 487 us
  local copies, waits for them, and re-layouts  270 us (54%)
  waiting for transfers between devices  119 us (24%)
  matrix products  42.7 us (9%)
  blocking collectives  31.4 us (6%)
  between operations  16.4 us (3%)
  other arithmetic  7.4 us (1%)
    unnamed x14, local copies, waits for them, and re-layouts  129 us
    all_gather x1, waiting for transfers between devices, per_device(): lax.all_gather(focused, 'panel', axis=2, tiled=True)[0]  119 us
    reshape x2, local copies, waits for them, and re-layouts, band(): return flat.reshape(2, nrows, length - 1)[:, :, :ncols]  56.4 us
    another operation x4, local copies, waits for them, and re-layouts, band(): flat = jnp.tile(rolled, (1, nrows))[:, :nrows * (length - 1)]  54 us
    psum x1, blocking collectives, per_device(): num_re, num_im, energy = lax.psum((num_re, num_im, energy), 'panel')  31.4 us
    slice x2, local copies, waits for them, and re-layouts, band(): flat = jnp.tile(rolled, (1, nrows))[:, :nrows * (length - 1)]  29 us
    dot_general x2, matrix products, complex_dot(): jnp.dot(left[1], right[0], preferred_element_type=jnp.float32)  12.8 us
    dot_general x2, matrix products, complex_dot(): jnp.dot(left[0], right[0], preferred_element_type=jnp.float32)  12.4 us
  transfers between devices with their start and end apart: 1, of which 1 were waited for; matrix products, arithmetic and copies ran while one was open for 3% of the time, Pallas kernels for 0%

commit v1 on v0

v1 whole, which is shorter than its diff:
```python
import jax
import jax.numpy as jnp
from jax import lax
from jax.experimental import pallas as pl
from jax.experimental.pallas import tpu as pltpu
from jax.sharding import PartitionSpec as P

F32 = jnp.float32
BF16 = jnp.bfloat16
TILE = 256
VMEM_LIMIT = 56 * 1024 * 1024


def build_slab(kernel_ref, row_ref, slab_ref):
    taps = kernel_ref.shape[-1]
    length = taps + 1
    row_ref[:, :taps] = kernel_ref[0].astype(F32)
    for part in range(2):
        base = jnp.broadcast_to(row_ref[part : part + 1, :], (8, length))
        top = pltpu.roll(base, 1, 1, stride=1, stride_axis=0)
        for step in range(128 // 16):
            low = pltpu.roll(top, 16 * step, 1) if step else top
            high = pltpu.roll(top, 16 * step + 8, 1)
            slab_ref[part, 16 * step : 16 * step + 16, :] = jnp.concatenate([low, high], axis=0).astype(BF16)
        slab_ref[part, 128:256, 128:] = slab_ref[part, 0:128, : length - 128]


def focus_body(data_ref, kernel_ref, out_ref, row_ref, slab_ref, lhs_ref):
    rows, width = data_ref.shape[2], data_ref.shape[3]
    cols = out_ref.shape[2] // 2
    build_slab(kernel_ref, row_ref, slab_ref)
    lhs_ref[:rows] = data_ref[0, 0].astype(BF16)
    lhs_ref[rows:] = data_ref[0, 1].astype(BF16)
    lhs = lhs_ref[...]
    blocks = width // TILE
    for c in range(blocks):
        prods = []
        for part in range(2):
            rhs = jnp.concatenate(
                [slab_ref[part, :, width + TILE * (c - b) : width + TILE * (c - b) + TILE] for b in range(blocks)], axis=0
            )
            prods.append(jnp.dot(lhs, rhs, preferred_element_type=F32))
        re = (prods[0][:rows] - prods[1][rows:]).astype(BF16)
        im = (prods[1][:rows] + prods[0][rows:]).astype(BF16)
        for k in range(TILE // cols):
            dest = c * (TILE // cols) + k
            out_ref[dest, :, :cols] = re[:, k * cols : (k + 1) * cols]
            out_ref[dest, :, cols:] = im[:, k * cols : (k + 1) * cols]


def spread_body(kernel_ref, x_ref, out_ref, row_ref, slab_ref):
    sources, cols = x_ref.shape[0], x_ref.shape[1] // 2
    build_slab(kernel_ref, row_ref, slab_ref)
    for b in range(sources // TILE):
        first = sources - TILE * b
        pr = jnp.dot(slab_ref[0, :, first : first + sources], x_ref[...], preferred_element_type=F32)
        pi = jnp.dot(slab_ref[1, :, first : first + sources], x_ref[...], preferred_element_type=F32)
        out_ref[TILE * b : TILE * b + TILE, :cols] = (pr[:, :cols] - pi[:, cols:]).astype(BF16)
        out_ref[TILE * b : TILE * b + TILE, cols:] = (pr[:, cols:] + pi[:, :cols]).astype(BF16)


def fold(x):
    rows, width = x.shape
    x = x.reshape(rows // 8, 8, width).sum(axis=0)
    out = x[:, :128]
    for k in range(1, width // 128):
        out = out + x[:, 128 * k : 128 * k + 128]
    return out


def fit_body(data_ref, y_ref, mult_ref, sums_ref):
    panels, cols = y_ref.shape[0], y_ref.shape[2] // 2
    for q in range(panels):
        mult_ref[0, 0, :, q * cols : (q + 1) * cols] = y_ref[q, :, :cols]
        mult_ref[0, 1, :, q * cols : (q + 1) * cols] = y_ref[q, :, cols:]
    mr, mi = mult_ref[0, 0].astype(F32), mult_ref[0, 1].astype(F32)
    pr, pi = data_ref[0, 0], data_ref[0, 1]
    part = (fold(mr * pr + mi * pi), fold(mr * pi - mi * pr), fold(mr * mr + mi * mi))
    first = pl.program_id(0) == 0

    @pl.when(first)
    def _():
        for k in range(3):
            sums_ref[k] = part[k]

    @pl.when(jnp.logical_not(first))
    def _():
        for k in range(3):
            sums_ref[k] += part[k]


def subtract_body(data_ref, mult_ref, sums_ref, out_ref):
    num_re, num_im, energy = (jnp.sum(sums_ref[k], keepdims=True) for k in range(3))
    den = energy + 1e-6
    fit_re, fit_im = num_re / den, num_im / den
    mr, mi = mult_ref[0, 0].astype(F32), mult_ref[0, 1].astype(F32)
    out_ref[0, 0] = data_ref[0, 0] - (fit_re * mr - fit_im * mi)
    out_ref[0, 1] = data_ref[0, 1] - (fit_re * mi + fit_im * mr)


def params(**kw):
    return pltpu.CompilerParams(vmem_limit_bytes=VMEM_LIMIT, **kw)


def total(x, axis):
    n = lax.axis_size(axis)
    if n & (n - 1):
        return lax.psum(x, axis)
    step = n // 2
    while step:
        x = x + lax.ppermute(x, axis, [(k, k ^ step) for k in range(n)])
        step //= 2
    return x


def per_device(recorded, receiver_kernel, source_kernel):
    rows, width = recorded.shape[2], recorded.shape[3]
    panels = lax.axis_size("panel")
    sources = rows * panels
    cols = width // panels
    shape = jax.ShapeDtypeStruct

    focused = pl.pallas_call(
        focus_body,
        out_shape=shape((panels, rows, 2 * cols), BF16),
        scratch_shapes=[
            pltpu.VMEM((2, 2 * width), F32),
            pltpu.VMEM((2, TILE, 2 * width), BF16),
            pltpu.VMEM((2 * rows, width), BF16),
        ],
        compiler_params=params(),
        name="focus",
    )(recorded, receiver_kernel)
    columns = lax.all_to_all(focused, "panel", 0, 0, tiled=True).reshape(sources, 2 * cols)
    spread = pl.pallas_call(
        spread_body,
        out_shape=shape((sources, 2 * cols), BF16),
        scratch_shapes=[pltpu.VMEM((2, 2 * sources), F32), pltpu.VMEM((2, TILE, 2 * sources), BF16)],
        compiler_params=params(),
        name="spread",
    )(source_kernel, columns)
    back = lax.all_to_all(spread.reshape(panels, rows, 2 * cols), "panel", 0, 0, tiled=True)

    bm = 32
    data_spec = pl.BlockSpec((1, 2, bm, width), lambda i: (0, 0, i, 0))
    mult, sums = pl.pallas_call(
        fit_body,
        grid=(rows // bm,),
        in_specs=[data_spec, pl.BlockSpec((panels, bm, 2 * cols), lambda i: (0, i, 0))],
        out_specs=[data_spec, pl.BlockSpec((3, 8, 128), lambda i: (0, 0, 0))],
        out_shape=[shape((1, 2, rows, width), BF16), shape((3, 8, 128), F32)],
        compiler_params=params(),
        name="fit",
    )(recorded, back)
    sums = total(sums, "panel")
    prim = pl.pallas_call(
        subtract_body,
        grid=(rows // bm,),
        in_specs=[data_spec, data_spec, pl.BlockSpec((3, 8, 128), lambda i: (0, 0, 0))],
        out_specs=data_spec,
        out_shape=shape((1, 2, rows, width), F32),
        compiler_params=params(),
        name="subtract",
    )(recorded, mult, sums)
    return prim, mult


def solution(mesh):
    placed = (P("freq", None, "panel", None), P("freq", None, None), P("freq", None, None))
    return jax.shard_map(
        per_device,
        mesh=mesh,
        in_specs=placed,
        out_specs=(P("freq", None, "panel", None), P("freq", None, "panel", None)),
        check_vma=False,
    )
```

time: 496 us -> 102 us (0.21); the launches traced: 487 us -> 102 us
  local copies, waits for them, and re-layouts: 270 us -> 0 us
  waiting for transfers between devices: 119 us -> 7.73 us
  matrix products: 42.7 us -> 0 us
  blocking collectives: 31.4 us -> 62 us
  Pallas kernels: 0 us -> 24 us
  between operations: 16.4 us -> 0.64 us
  other arithmetic: 7.4 us -> 1.32 us
  starting transfers between devices: 0.04 us -> 5.97 us
    unnamed x14 -> x0, local copies, waits for them, and re-layouts: 129 us -> none
    all_gather x1 -> x0, waiting for transfers between devices: 119 us -> none  [per_device(): lax.all_gather(focused, 'panel', axis=2, tiled=True)[0]]
    all_to_all x0 -> x2, blocking collectives: none -> 62 us  [the longest x1 32.2 us: per_device(): lax.all_to_all(focused, 'panel', 0, 0, tiled=True)]
    reshape x2 -> x0, local copies, waits for them, and re-layouts: 56.4 us -> none  [band(): return flat.reshape(2, nrows, length - 1)[:, :, :ncols]]
    another operation x4 -> x0, local copies, waits for them, and re-layouts: 54 us -> none  [band(): flat = jnp.tile(rolled, (1, nrows))[:, :nrows * (length - 1)]]
    dot_general x8 -> x0, matrix products: 42.7 us -> none  [the longest x2 12.8 us: complex_dot(): jnp.dot(left[1], right[0], preferred_element_type=jnp.float32)]
    psum x1 -> x0, blocking collectives: 31.4 us -> none  [per_device(): num_re, num_im, energy = lax.psum((num_re, num_im, energy), 'panel')]
    slice x6 -> x0, local copies, waits for them, and re-layouts: 30.6 us -> none  [the longest x2 29 us: band(): flat = jnp.tile(rolled, (1, nrows))[:, :nrows * (length - 1)]]
  transfers between devices with their start and end apart: 1 -> 4, of which waited for: 1 -> 4; matrix products, arithmetic and copies ran while one was open for 3% -> 0% of each run, Pallas kernels for 0% -> 0%
where the time goes in v1:
time: 102 us
  blocking collectives  62 us (61%)
  Pallas kernels  24 us (24%)
  waiting for transfers between devices  7.73 us (8%)
  starting transfers between devices  5.97 us (6%)
  other arithmetic  1.32 us (1%)
    all_to_all x1, blocking collectives, per_device(): lax.all_to_all(focused, 'panel', 0, 0, tiled=True)  32.2 us
    all_to_all x1, blocking collectives, per_device(): lax.all_to_all(spread.reshape(panels, rows, 2 * cols), 'panel', 0, 0, til...  29.8 us
    pallas_call x1, Pallas kernels, per_device(): pl.pallas_call(focus_body, out_shape=shape((panels, rows, 2 * cols), BF16...  8.09 us
    ppermute x4, waiting for transfers between devices, total(): x = x + lax.ppermute(x, axis, [(k, k ^ step) for k in range(n)])  7.73 us
    pallas_call x1, Pallas kernels, per_device(): pl.pallas_call(spread_body, out_shape=shape((sources, 2 * cols), BF16), s...  7.27 us
    ppermute x4, starting transfers between devices, total(): x = x + lax.ppermute(x, axis, [(k, k ^ step) for k in range(n)])  5.97 us
    pallas_call x1, Pallas kernels, per_device(): pl.pallas_call(subtract_body, grid=(rows // bm,), in_specs=[data_spec, da...  4.4 us
    pallas_call x1, Pallas kernels, per_device(): pl.pallas_call(fit_body, grid=(rows // bm,), in_specs=[data_spec, pl.Bloc...  4.21 us
  transfers between devices with their start and end apart: 4, of which 4 were waited for; matrix products, arithmetic and copies ran while one was open for 0% of the time, Pallas kernels for 0%

profile of v1, /device:TPU:0, one launch (start us, length us, event | category | flops | bytes accessed | tf_op | source)
XLA Modules:
  0.0 101.6 jit_solution(17351877947858069526)
XLA Ops:
  0.6 8.1 %focus.1 = bf16[16,128,256]{2,1,0:T(8,128)(2,1)} custom-call(f32[1,2,128,2048]{3,2,1,0:T(8,128)} %data_ref.5, bf16[1,2,4095]{2,1,0:T(2,128)(2,1)} %kernel_ref.2), custom_call_target="tpu_custom_call" | custom-call | tf_op jit(solution)/shard_map/focus/pallas_call | solution.py:123
  8.7 32.2 %all_to_all.10 = bf16[16,128,256]{2,1,0:T(8,128)(2,1)} all-to-all(bf16[16,128,256]{2,1,0:T(8,128)(2,1)} %focus.1), channel_id=1, replica_groups=mesh['freq'=2,'panel'=16] {'panel'}, dimensions={0} | all-to-all | bytes 2097152 | tf_op jit(solution)/shard_map/all_to_all | solution.py:134
  40.9 7.3 %spread.1 = bf16[2048,256]{1,0:T(8,128)(2,1)} custom-call(bf16[1,2,4095]{2,1,0:T(2,128)(2,1)} %kernel_ref.3, bf16[2048,256]{1,0:T(8,128)(2,1)} %bitcast.2), custom_call_target="tpu_custom_call" | custom-call | tf_op jit(solution)/shard_map/spread/pallas_call | solution.py:135
  48.2 29.8 %all_to_all.11.y_ref = bf16[16,128,256]{2,1,0:T(8,128)(2,1)} all-to-all(bf16[16,128,256]{2,1,0:T(8,128)(2,1)} %bitcast.3), channel_id=1, replica_groups=mesh['freq'=2,'panel'=16] {'panel'}, dimensions={0} | all-to-all | bytes 2097152 | tf_op jit(solution)/shard_map/all_to_all | solution.py:142
  78.0 4.2 %fit.1 = (bf16[1,2,128,2048]{3,2,1,0:T(8,128)(2,1)}, f32[3,8,128]{2,1,0:T(8,128)}) custom-call(f32[1,2,128,2048]{3,2,1,0:T(8,128)} %data_ref.5, bf16[16,128,256]{2,1,0:T(8,128)(2,1)} %all_to_all.11.y_ref), custom_call_target="tpu_custom_call" | custom-call | tf_op jit(solution)/shard_map/fit/pallas_call | solution.py:146
  82.2 3.2 %collective-permute-start = (f32[3,8,128]{2,1,0:T(8,128)}, f32[3,8,128]{2,1,0:T(8,128)S(1)}, u32[]{:S(2)}, u32[]{:S(2)}) collective-permute-start(f32[3,8,128]{2,1,0:T(8,128)} %get-tuple-element.5), channel_id=1, source_target_pairs={{0,8},{1,9},{2,10},{3,11},{4,12},{5,13},{6,14},{7,15},{8,0},{9,1},... | collective-permute-start | bytes 36872 | tf_op jit(solution)/shard_map/ppermute | solution.py:111
  85.5 1.9 %collective-permute-done = f32[3,8,128]{2,1,0:T(8,128)S(1)} collective-permute-done((f32[3,8,128]{2,1,0:T(8,128)}, f32[3,8,128]{2,1,0:T(8,128)S(1)}, u32[]{:S(2)}, u32[]{:S(2)}) %collective-permute-start) | collective-permute-done | bytes 12320 | tf_op jit(solution)/shard_map/ppermute | solution.py:111
  87.3 0.7 add.12
  88.1 1.6 %collective-permute-start.1 = (f32[3,8,128]{2,1,0:T(8,128)S(1)}, f32[3,8,128]{2,1,0:T(8,128)S(1)}, u32[]{:S(2)}, u32[]{:S(2)}) collective-permute-start(f32[3,8,128]{2,1,0:T(8,128)S(1)} %add.12), channel_id=1, source_target_pairs={{0,4},{1,5},{2,6},{3,7},{4,0},{5,1},{6,2},{7,3},{8,12},{9,13},{10,... | collective-permute-start | bytes 36872 | tf_op jit(solution)/shard_map/ppermute | solution.py:111
  89.7 2.0 %collective-permute-done.1 = f32[3,8,128]{2,1,0:T(8,128)S(1)} collective-permute-done((f32[3,8,128]{2,1,0:T(8,128)S(1)}, f32[3,8,128]{2,1,0:T(8,128)S(1)}, u32[]{:S(2)}, u32[]{:S(2)}) %collective-permute-start.1) | collective-permute-done | bytes 12320 | tf_op jit(solution)/shard_map/ppermute | solution.py:111
  91.8 1.1 %collective-permute-start.2 = (f32[3,8,128]{2,1,0:T(8,128)S(1)}, f32[3,8,128]{2,1,0:T(8,128)S(1)}, u32[]{:S(2)}, u32[]{:S(2)}) collective-permute-start(f32[3,8,128]{2,1,0:T(8,128)S(1)} %add.13), channel_id=1, source_target_pairs={{0,2},{1,3},{2,0},{3,1},{4,6},{5,7},{6,4},{7,5},{8,10},{9,11},{10,... | collective-permute-start | bytes 36872 | tf_op jit(solution)/shard_map/ppermute | solution.py:111
  92.8 2.6 %collective-permute-done.2 = f32[3,8,128]{2,1,0:T(8,128)S(1)} collective-permute-done((f32[3,8,128]{2,1,0:T(8,128)S(1)}, f32[3,8,128]{2,1,0:T(8,128)S(1)}, u32[]{:S(2)}, u32[]{:S(2)}) %collective-permute-start.2) | collective-permute-done | bytes 12320 | tf_op jit(solution)/shard_map/ppermute | solution.py:111
  95.5 0.0 collective-permute-start.3
  95.5 1.2 %collective-permute-done.3 = f32[3,8,128]{2,1,0:T(8,128)S(1)} collective-permute-done((f32[3,8,128]{2,1,0:T(8,128)S(1)}, f32[3,8,128]{2,1,0:T(8,128)S(1)}, u32[]{:S(2)}, u32[]{:S(2)}) %collective-permute-start.3) | collective-permute-done | bytes 12320 | tf_op jit(solution)/shard_map/ppermute | solution.py:111
  96.6 0.6 add.15.sums_ref
  97.2 4.4 %subtract.1 = f32[1,2,128,2048]{3,2,1,0:T(8,128)} custom-call(f32[1,2,128,2048]{3,2,1,0:T(8,128)} %data_ref.5, bf16[1,2,128,2048]{3,2,1,0:T(8,128)(2,1)} %get-tuple-element.3.mult_ref, f32[3,8,128]{2,1,0:T(8,128)} %add.15.sums_ref), custom_call_target="tpu_custom_call" | custom-call | tf_op jit(solution)/shard_map/subtract/pallas_call | solution.py:156
  (2 shorter events, 0.0 us)
Async XLA Ops:
  82.2 5.1 %collective-permute-start = (f32[3,8,128]{2,1,0:T(8,128)}, f32[3,8,128]{2,1,0:T(8,128)S(1)}, u32[]{:S(2)}, u32[]{:S(2)}) collective-permute-start(f32[3,8,128]{2,1,0:T(8,128)} %get-tuple-element.5), channel_id=1, source_target_pairs={{0,8},{1,9},{2,10},{3,11},{4,12},{5,13},{6,14},{7,15},{8,0},{9,1},... | collective-permute-start | bytes 36872 | tf_op jit(solution)/shard_map/ppermute | solution.py:111
  88.1 3.7 %collective-permute-start.1 = (f32[3,8,128]{2,1,0:T(8,128)S(1)}, f32[3,8,128]{2,1,0:T(8,128)S(1)}, u32[]{:S(2)}, u32[]{:S(2)}) collective-permute-start(f32[3,8,128]{2,1,0:T(8,128)S(1)} %add.12), channel_id=1, source_target_pairs={{0,4},{1,5},{2,6},{3,7},{4,0},{5,1},{6,2},{7,3},{8,12},{9,13},{10,... | collective-permute-start | bytes 36872 | tf_op jit(solution)/shard_map/ppermute | solution.py:111
  91.8 3.7 %collective-permute-start.2 = (f32[3,8,128]{2,1,0:T(8,128)S(1)}, f32[3,8,128]{2,1,0:T(8,128)S(1)}, u32[]{:S(2)}, u32[]{:S(2)}) collective-permute-start(f32[3,8,128]{2,1,0:T(8,128)S(1)} %add.13), channel_id=1, source_target_pairs={{0,2},{1,3},{2,0},{3,1},{4,6},{5,7},{6,4},{7,5},{8,10},{9,11},{10,... | collective-permute-start | bytes 36872 | tf_op jit(solution)/shard_map/ppermute | solution.py:111
  95.5 1.2 %collective-permute-start.3 = (f32[3,8,128]{2,1,0:T(8,128)S(1)}, f32[3,8,128]{2,1,0:T(8,128)S(1)}, u32[]{:S(2)}, u32[]{:S(2)}) collective-permute-start(f32[3,8,128]{2,1,0:T(8,128)S(1)} %add.14), channel_id=1, source_target_pairs={{0,1},{1,0},{2,3},{3,2},{4,5},{5,4},{6,7},{7,6},{8,9},{9,8},{10,11... | collective-permute-start | bytes 36872 | tf_op jit(solution)/shard_map/ppermute | solution.py:111

commit v2 on v1

--- a/solution.py
+++ b/solution.py
@@ -68,49 +68,65 @@
     return out
 
 
-def fit_body(data_ref, y_ref, mult_ref, sums_ref):
-    panels, cols = y_ref.shape[0], y_ref.shape[2] // 2
-    for q in range(panels):
-        mult_ref[0, 0, :, q * cols : (q + 1) * cols] = y_ref[q, :, :cols]
-        mult_ref[0, 1, :, q * cols : (q + 1) * cols] = y_ref[q, :, cols:]
-    mr, mi = mult_ref[0, 0].astype(F32), mult_ref[0, 1].astype(F32)
-    pr, pi = data_ref[0, 0], data_ref[0, 1]
-    part = (fold(mr * pr + mi * pi), fold(mr * pi - mi * pr), fold(mr * mr + mi * mi))
-    first = pl.program_id(0) == 0
-
-    @pl.when(first)
-    def _():
-        for k in range(3):
-            sums_ref[k] = part[k]
-
-    @pl.when(jnp.logical_not(first))
-    def _():
-        for k in range(3):
-            sums_ref[k] += part[k]
+def fit_body(data_ref, y_ref, sums_ref):
+    panels, rows, cols = y_ref.shape[0], y_ref.shape[1], y_ref.shape[2] // 2
+    strip = max(1, 128 // cols)
+    acc = [jnp.zeros((8, 128), F32)] * 3
+    for q in range(0, panels, strip):
+        at = slice(q * cols, (q + strip) * cols)
+        mr = jnp.concatenate([y_ref[q + k, :, :cols] for k in range(strip)], axis=1).astype(F32)
+        mi = jnp.concatenate([y_ref[q + k, :, cols:] for k in range(strip)], axis=1).astype(F32)
+        pr, pi = data_ref[0, 0, :, at], data_ref[0, 1, :, at]
+        acc[0] += fold(mr * pr + mi * pi)
+        acc[1] += fold(mr * pi - mi * pr)
+        acc[2] += fold(mr * mr + mi * mi)
+    for k in range(3):
+        sums_ref[k] = acc[k]
 
 
-def subtract_body(data_ref, mult_ref, sums_ref, out_ref):
-    num_re, num_im, energy = (jnp.sum(sums_ref[k], keepdims=True) for k in range(3))
+def subtract_body(data_ref, y_ref, *refs):
+    sums_refs, (out_ref, mult_ref) = refs[:-2], refs[-2:]
+    panels, cols = y_ref.shape[0], y_ref.shape[2] // 2
+    bm = out_ref.shape[2]
+    sums = sums_refs[0][...]
+    for ref in sums_refs[1:]:
+        sums = sums + ref[...]
+    num_re, num_im, energy = (jnp.sum(sums[k], keepdims=True) for k in range(3))
     den = energy + 1e-6
     fit_re, fit_im = num_re / den, num_im / den
+    at = pl.ds(pl.multiple_of(pl.program_id(0) * bm, bm), bm)
+    for q in range(panels):
+        lanes = slice(q * cols, (q + 1) * cols)
+        mult_ref[0, 0, :, lanes] = y_ref[q, at, :cols]
+        mult_ref[0, 1, :, lanes] = y_ref[q, at, cols:]
     mr, mi = mult_ref[0, 0].astype(F32), mult_ref[0, 1].astype(F32)
-    out_ref[0, 0] = data_ref[0, 0] - (fit_re * mr - fit_im * mi)
-    out_ref[0, 1] = data_ref[0, 1] - (fit_re * mi + fit_im * mr)
+    out_ref[0, 0] = data_ref[0, 0, at] - (fit_re * mr - fit_im * mi)
+    out_ref[0, 1] = data_ref[0, 1, at] - (fit_re * mi + fit_im * mr)
 
 
 def params(**kw):
     return pltpu.CompilerParams(vmem_limit_bytes=VMEM_LIMIT, **kw)
 
 
-def total(x, axis):
+def small():
+    return pltpu.CompilerParams(vmem_limit_bytes=16 * 1024 * 1024)
+
+
+def partials(x, axis):
     n = lax.axis_size(axis)
     if n & (n - 1):
-        return lax.psum(x, axis)
-    step = n // 2
-    while step:
-        x = x + lax.ppermute(x, axis, [(k, k ^ step) for k in range(n)])
-        step //= 2
-    return x
+        return [lax.psum(x, axis)]
+    terms, span = [x], n
+    while span > 1:
+        radix = min(4, span)
+        span //= radix
+        x = terms[0]
+        for term in terms[1:]:
+            x = x + term
+        terms = [x] + [
+            lax.ppermute(x, axis, [(k, k ^ (span * d)) for k in range(n)]) for d in range(1, radix)
+        ]
+    return terms
 
 
 def per_device(recorded, receiver_kernel, source_kernel):
@@ -141,28 +157,26 @@
     )(source_kernel, columns)
     back = lax.all_to_all(spread.reshape(panels, rows, 2 * cols), "panel", 0, 0, tiled=True)
 
-    bm = 32
-    data_spec = pl.BlockSpec((1, 2, bm, width), lambda i: (0, 0, i, 0))
-    mult, sums = pl.pallas_call(
+    resident = pl.BlockSpec(memory_space=pltpu.VMEM)
+    sums = pl.pallas_call(
         fit_body,
-        grid=(rows // bm,),
-        in_specs=[data_spec, pl.BlockSpec((panels, bm, 2 * cols), lambda i: (0, i, 0))],
-        out_specs=[data_spec, pl.BlockSpec((3, 8, 128), lambda i: (0, 0, 0))],
-        out_shape=[shape((1, 2, rows, width), BF16), shape((3, 8, 128), F32)],
-        compiler_params=params(),
+        in_specs=[resident, resident],
+        out_shape=shape((3, 8, 128), F32),
+        compiler_params=small(),
         name="fit",
     )(recorded, back)
-    sums = total(sums, "panel")
-    prim = pl.pallas_call(
+    terms = partials(sums, "panel")
+    bm = 32
+    block = pl.BlockSpec((1, 2, bm, width), lambda i: (0, 0, i, 0))
+    return pl.pallas_call(
         subtract_body,
         grid=(rows // bm,),
-        in_specs=[data_spec, data_spec, pl.BlockSpec((3, 8, 128), lambda i: (0, 0, 0))],
-        out_specs=data_spec,
-        out_shape=shape((1, 2, rows, width), F32),
-        compiler_params=params(),
+        in_specs=[resident, resident] + [pl.BlockSpec((3, 8, 128), lambda i: (0, 0, 0))] * len(terms),
+        out_specs=[block, block],
+        out_shape=[shape((1, 2, rows, width), F32), shape((1, 2, rows, width), BF16)],
+        compiler_params=small(),
         name="subtract",
-    )(recorded, mult, sums)
-    return prim, mult
+    )(recorded, back, *terms)
 
 
 def solution(mesh):

time: 102 us -> 92.8 us (0.910)
  Pallas kernels: 24 us -> 18.7 us
  waiting for transfers between devices: 7.73 us -> 4.89 us
  other arithmetic: 1.32 us -> 0.01 us
    pallas_call x2, Pallas kernels: 8.62 us -> 3.18 us  [the longest x1 2.59 us: per_device(): pl.pallas_call(subtract_body, grid=(rows // bm,), in_specs=[resident, res...]
    ppermute x4 -> x6, waiting for transfers between devices: 7.73 us -> 4.89 us  [partials(): lax.ppermute(x, axis, [(k, k ^ span * d) for k in range(n)])]
    add x4 -> x1, other arithmetic: 1.32 us -> 0.01 us  [partials(): x = x + term]
    ppermute x4 -> x6, starting transfers between devices: 5.97 us -> 6.32 us  [partials(): lax.ppermute(x, axis, [(k, k ^ span * d) for k in range(n)])]
  transfers between devices with their start and end apart: 4 -> 6, of which waited for: 4 -> 5; matrix products, arithmetic and copies ran while one was open for 0% -> 0% of each run, Pallas kernels for 0% -> 0%
where the time goes in v2:
time: 92.8 us; the launch traced here: 92.5 us
  blocking collectives  61.9 us (67%)
  Pallas kernels  18.7 us (20%)
  starting transfers between devices  6.32 us (7%)
  waiting for transfers between devices  4.89 us (5%)
    all_to_all x1, blocking collectives, per_device(): lax.all_to_all(focused, 'panel', 0, 0, tiled=True)  32.2 us
    all_to_all x1, blocking collectives, per_device(): lax.all_to_all(spread.reshape(panels, rows, 2 * cols), 'panel', 0, 0, til...  29.7 us
    pallas_call x1, Pallas kernels, per_device(): pl.pallas_call(focus_body, out_shape=shape((panels, rows, 2 * cols), BF16...  8.09 us
    pallas_call x1, Pallas kernels, per_device(): pl.pallas_call(spread_body, out_shape=shape((sources, 2 * cols), BF16), s...  7.42 us
    ppermute x6, starting transfers between devices, partials(): lax.ppermute(x, axis, [(k, k ^ span * d) for k in range(n)])  6.32 us
    ppermute x6, waiting for transfers between devices, partials(): lax.ppermute(x, axis, [(k, k ^ span * d) for k in range(n)])  4.89 us
    pallas_call x1, Pallas kernels, per_device(): pl.pallas_call(subtract_body, grid=(rows // bm,), in_specs=[resident, res...  2.59 us
  transfers between devices with their start and end apart: 6, of which 5 were waited for; matrix products, arithmetic and copies ran while one was open for 0% of the time, Pallas kernels for 0%

profile of v2, /device:TPU:0, one launch (start us, length us, event | category | flops | bytes accessed | tf_op | source)
XLA Modules:
  0.0 92.5 jit_solution(335323116988043462)
XLA Ops:
  0.6 8.1 %focus.1 = bf16[16,128,256]{2,1,0:T(8,128)(2,1)} custom-call(f32[1,2,128,2048]{3,2,1,0:T(8,128)} %data_ref.5, bf16[1,2,4095]{2,1,0:T(2,128)(2,1)} %kernel_ref.2), custom_call_target="tpu_custom_call" | custom-call | tf_op jit(solution)/shard_map/focus/pallas_call | solution.py:139
  8.7 32.2 %all_to_all.10 = bf16[16,128,256]{2,1,0:T(8,128)(2,1)} all-to-all(bf16[16,128,256]{2,1,0:T(8,128)(2,1)} %focus.1), channel_id=1, replica_groups=mesh['freq'=2,'panel'=16] {'panel'}, dimensions={0} | all-to-all | bytes 2097152 | tf_op jit(solution)/shard_map/all_to_all | solution.py:150
  40.9 0.0 copy-start
  40.9 7.4 %spread.1 = bf16[2048,256]{1,0:T(8,128)(2,1)} custom-call(bf16[1,2,4095]{2,1,0:T(2,128)(2,1)} %kernel_ref.3, bf16[2048,256]{1,0:T(8,128)(2,1)} %bitcast.2), custom_call_target="tpu_custom_call" | custom-call | tf_op jit(solution)/shard_map/spread/pallas_call | solution.py:151
  48.3 29.7 %all_to_all.11.y_ref = bf16[16,128,256]{2,1,0:T(8,128)(2,1)S(1)} all-to-all(bf16[16,128,256]{2,1,0:T(8,128)(2,1)} %bitcast.3), channel_id=1, replica_groups=mesh['freq'=2,'panel'=16] {'panel'}, dimensions={0} | all-to-all | bytes 2097152 | tf_op jit(solution)/shard_map/all_to_all | solution.py:158
  78.0 0.0 copy-done
  78.1 0.6 fit.1
  78.6 2.4 %collective-permute-start.2 = (f32[3,8,128]{2,1,0:T(8,128)S(1)}, f32[3,8,128]{2,1,0:T(8,128)S(1)}, u32[]{:S(2)}, u32[]{:S(2)}) collective-permute-start(f32[3,8,128]{2,1,0:T(8,128)S(1)} %fit.1), channel_id=1, source_target_pairs={{0,12},{1,13},{2,14},{3,15},{4,8},{5,9},{6,10},{7,11},{8,4},{9,5},... | collective-permute-start | bytes 36872 | tf_op jit(solution)/shard_map/ppermute | solution.py:127
  81.0 1.1 %collective-permute-start.1 = (f32[3,8,128]{2,1,0:T(8,128)S(1)}, f32[3,8,128]{2,1,0:T(8,128)S(1)}, u32[]{:S(2)}, u32[]{:S(2)}) collective-permute-start(f32[3,8,128]{2,1,0:T(8,128)S(1)} %fit.1), channel_id=1, source_target_pairs={{0,8},{1,9},{2,10},{3,11},{4,12},{5,13},{6,14},{7,15},{8,0},{9,1},... | collective-permute-start | bytes 36872 | tf_op jit(solution)/shard_map/ppermute | solution.py:127
  82.1 1.0 %collective-permute-start = (f32[3,8,128]{2,1,0:T(8,128)S(1)}, f32[3,8,128]{2,1,0:T(8,128)S(1)}, u32[]{:S(2)}, u32[]{:S(2)}) collective-permute-start(f32[3,8,128]{2,1,0:T(8,128)S(1)} %fit.1), channel_id=1, source_target_pairs={{0,4},{1,5},{2,6},{3,7},{4,0},{5,1},{6,2},{7,3},{8,12},{9,13},{10,... | collective-permute-start | bytes 36872 | tf_op jit(solution)/shard_map/ppermute | solution.py:127
  83.1 1.2 %collective-permute-done.2 = f32[3,8,128]{2,1,0:T(8,128)S(1)} collective-permute-done((f32[3,8,128]{2,1,0:T(8,128)S(1)}, f32[3,8,128]{2,1,0:T(8,128)S(1)}, u32[]{:S(2)}, u32[]{:S(2)}) %collective-permute-start.2) | collective-permute-done | bytes 12320 | tf_op jit(solution)/shard_map/ppermute | solution.py:127
  84.3 1.3 %collective-permute-done.1 = f32[3,8,128]{2,1,0:T(8,128)S(1)} collective-permute-done((f32[3,8,128]{2,1,0:T(8,128)S(1)}, f32[3,8,128]{2,1,0:T(8,128)S(1)}, u32[]{:S(2)}, u32[]{:S(2)}) %collective-permute-start.1) | collective-permute-done | bytes 12320 | tf_op jit(solution)/shard_map/ppermute | solution.py:127
  85.6 0.2 collective-permute-done
  85.8 0.3 collective-permute-start.5
  86.2 1.5 %collective-permute-start.4 = (f32[3,8,128]{2,1,0:T(8,128)S(1)}, f32[3,8,128]{2,1,0:T(8,128)S(1)}, u32[]{:S(2)}, u32[]{:S(2)}) collective-permute-start(f32[3,8,128]{2,1,0:T(8,128)S(1)} %add_add_fusion.refs_0_), channel_id=1, source_target_pairs={{0,2},{1,3},{2,0},{3,1},{4,6},{5,7},{6,4},{7,5},{8,10},{9,11},{10,... | collective-permute-start | bytes 36872 | tf_op jit(solution)/shard_map/ppermute | solution.py:127
  87.7 0.0 collective-permute-start.3
  87.7 1.3 %collective-permute-done.5.refs_3_ = f32[3,8,128]{2,1,0:T(8,128)S(1)} collective-permute-done((f32[3,8,128]{2,1,0:T(8,128)S(1)}, f32[3,8,128]{2,1,0:T(8,128)S(1)}, u32[]{:S(2)}, u32[]{:S(2)}) %collective-permute-start.5) | collective-permute-done | bytes 12320 | tf_op jit(solution)/shard_map/ppermute | solution.py:127
  89.0 0.9 collective-permute-done.4.refs_2_
  89.9 0.0 collective-permute-done.3.refs_1_
  89.9 2.6 %subtract.1 = (f32[1,2,128,2048]{3,2,1,0:T(8,128)}, bf16[1,2,128,2048]{3,2,1,0:T(8,128)(2,1)}) custom-call(f32[1,2,128,2048]{3,2,1,0:T(8,128)S(1)} %copy-done, bf16[16,128,256]{2,1,0:T(8,128)(2,1)S(1)} %all_to_all.11.y_ref, f32[3,8,128]{2,1,0:T(8,128)S(1)} %add_add_fusion.refs_0_, f32[3,8,128]{2,1,0:T(8,128)S(1)} %collective-permute-done.3.refs_1_, ...), custom_call_target="tpu_custom_call" | custom-call | tf_op jit(solution)/shard_map/subtract/pallas_call | solution.py:171
  (1 shorter events, 0.0 us)
Async XLA Ops:
  40.9 37.1 %copy-start = (f32[1,2,128,2048]{3,2,1,0:T(8,128)S(1)}, f32[1,2,128,2048]{3,2,1,0:T(8,128)}, u32[]{:S(2)}) copy-start(f32[1,2,128,2048]{3,2,1,0:T(8,128)} %data_ref.5) | copy-start | bytes 6291460
  78.6 5.7 %collective-permute-start.2 = (f32[3,8,128]{2,1,0:T(8,128)S(1)}, f32[3,8,128]{2,1,0:T(8,128)S(1)}, u32[]{:S(2)}, u32[]{:S(2)}) collective-permute-start(f32[3,8,128]{2,1,0:T(8,128)S(1)} %fit.1), channel_id=1, source_target_pairs={{0,12},{1,13},{2,14},{3,15},{4,8},{5,9},{6,10},{7,11},{8,4},{9,5},... | collective-permute-start | bytes 36872 | tf_op jit(solution)/shard_map/ppermute | solution.py:127
  81.0 4.6 %collective-permute-start.1 = (f32[3,8,128]{2,1,0:T(8,128)S(1)}, f32[3,8,128]{2,1,0:T(8,128)S(1)}, u32[]{:S(2)}, u32[]{:S(2)}) collective-permute-start(f32[3,8,128]{2,1,0:T(8,128)S(1)} %fit.1), channel_id=1, source_target_pairs={{0,8},{1,9},{2,10},{3,11},{4,12},{5,13},{6,14},{7,15},{8,0},{9,1},... | collective-permute-start | bytes 36872 | tf_op jit(solution)/shard_map/ppermute | solution.py:127
  82.1 3.7 %collective-permute-start = (f32[3,8,128]{2,1,0:T(8,128)S(1)}, f32[3,8,128]{2,1,0:T(8,128)S(1)}, u32[]{:S(2)}, u32[]{:S(2)}) collective-permute-start(f32[3,8,128]{2,1,0:T(8,128)S(1)} %fit.1), channel_id=1, source_target_pairs={{0,4},{1,5},{2,6},{3,7},{4,0},{5,1},{6,2},{7,3},{8,12},{9,13},{10,... | collective-permute-start | bytes 36872 | tf_op jit(solution)/shard_map/ppermute | solution.py:127
  85.8 3.1 %collective-permute-start.5 = (f32[3,8,128]{2,1,0:T(8,128)S(1)}, f32[3,8,128]{2,1,0:T(8,128)S(1)}, u32[]{:S(2)}, u32[]{:S(2)}) collective-permute-start(f32[3,8,128]{2,1,0:T(8,128)S(1)} %add_add_fusion.refs_0_), channel_id=1, source_target_pairs={{0,3},{1,2},{2,1},{3,0},{4,7},{5,6},{6,5},{7,4},{8,11},{9,10},{10,... | collective-permute-start | bytes 36872 | tf_op jit(solution)/shard_map/ppermute | solution.py:127
  86.2 3.7 %collective-permute-start.4 = (f32[3,8,128]{2,1,0:T(8,128)S(1)}, f32[3,8,128]{2,1,0:T(8,128)S(1)}, u32[]{:S(2)}, u32[]{:S(2)}) collective-permute-start(f32[3,8,128]{2,1,0:T(8,128)S(1)} %add_add_fusion.refs_0_), channel_id=1, source_target_pairs={{0,2},{1,3},{2,0},{3,1},{4,6},{5,7},{6,4},{7,5},{8,10},{9,11},{10,... | collective-permute-start | bytes 36872 | tf_op jit(solution)/shard_map/ppermute | solution.py:127
  87.7 2.2 %collective-permute-start.3 = (f32[3,8,128]{2,1,0:T(8,128)S(1)}, f32[3,8,128]{2,1,0:T(8,128)S(1)}, u32[]{:S(2)}, u32[]{:S(2)}) collective-permute-start(f32[3,8,128]{2,1,0:T(8,128)S(1)} %add_add_fusion.refs_0_), channel_id=1, source_target_pairs={{0,1},{1,0},{2,3},{3,2},{4,5},{5,4},{6,7},{7,6},{8,9},{9,8},{10,11... | collective-permute-start | bytes 36872 | tf_op jit(solution)/shard_map/ppermute | solution.py:127

commit v3 on v2

--- a/solution.py
+++ b/solution.py
@@ -1,9 +1,12 @@
+import functools
+
 import jax
 import jax.numpy as jnp
 from jax import lax
 from jax.experimental import pallas as pl
 from jax.experimental.pallas import tpu as pltpu
 from jax.sharding import PartitionSpec as P
+
 
 F32 = jnp.float32
 BF16 = jnp.bfloat16
@@ -69,7 +72,7 @@
 
 
 def fit_body(data_ref, y_ref, sums_ref):
-    panels, rows, cols = y_ref.shape[0], y_ref.shape[1], y_ref.shape[2] // 2
+    panels, cols = y_ref.shape[0], y_ref.shape[2] // 2
     strip = max(1, 128 // cols)
     acc = [jnp.zeros((8, 128), F32)] * 3
     for q in range(0, panels, strip):
@@ -108,6 +111,10 @@
     return pltpu.CompilerParams(vmem_limit_bytes=VMEM_LIMIT, **kw)
 
 
+def medium():
+    return pltpu.CompilerParams(vmem_limit_bytes=32 * 1024 * 1024)
+
+
 def small():
     return pltpu.CompilerParams(vmem_limit_bytes=16 * 1024 * 1024)
 
@@ -129,7 +136,7 @@
     return terms
 
 
-def per_device(recorded, receiver_kernel, source_kernel):
+def plain(recorded, receiver_kernel, source_kernel):
     rows, width = recorded.shape[2], recorded.shape[3]
     panels = lax.axis_size("panel")
     sources = rows * panels
@@ -179,6 +186,283 @@
     )(recorded, back, *terms)
 
 
+def narrow_slab(kernel_ref, row_ref, slab_ref):
+    taps = kernel_ref.shape[-1]
+    row_ref[:, :taps] = kernel_ref[0].astype(F32)
+    for part in range(2):
+        base = jnp.broadcast_to(row_ref[part : part + 1, :], (8, taps + 1))
+        top = pltpu.roll(base, 1, 1, stride=1, stride_axis=0)
+        for step in range(8):
+            low = pltpu.roll(top, 16 * step, 1) if step else top
+            high = pltpu.roll(top, 16 * step + 8, 1)
+            slab_ref[part, 16 * step : 16 * step + 16, :] = jnp.concatenate([low, high], axis=0).astype(BF16)
+
+
+def lane_half(shape):
+    return lax.broadcasted_iota(jnp.int32, shape, 1) < shape[1] // 2
+
+
+def interleave(re, im):
+    low = lane_half(re.shape)
+    return jnp.where(low, re, pltpu.roll(im, 64, 1)), jnp.where(low, pltpu.roll(re, 64, 1), im)
+
+
+def load_lhs(data_ref, lhs_ref):
+    rows = data_ref.shape[2]
+    lhs_ref[:rows] = data_ref[0, 0].astype(BF16)
+    lhs_ref[rows:] = data_ref[0, 1].astype(BF16)
+    return lhs_ref[...]
+
+
+def chip_lane(offset):
+    return 128 * ((lax.axis_index("panel") // 2) ^ offset)
+
+
+def aligned(start, size):
+    return pl.ds(pl.multiple_of(start, 128), size)
+
+
+def focus_b_body(data_ref, kernel_ref, out_ref, row_ref, slab_ref, lhs_ref):
+    rows, width = data_ref.shape[2], data_ref.shape[3]
+    narrow_slab(kernel_ref, row_ref, slab_ref)
+    lhs = load_lhs(data_ref, lhs_ref)
+    for c in range(width // TILE // 2):
+        first = width + width // 2 + TILE * c
+        prods = []
+        for part in range(2):
+            rhs = [slab_ref[part, :, first - 128 * r : first - 128 * r + TILE] for r in range(width // 128)]
+            prods.append(jnp.dot(lhs, jnp.concatenate(rhs, axis=0), preferred_element_type=F32))
+        re, im = prods[0][:rows] - prods[1][rows:], prods[1][:rows] + prods[0][rows:]
+        for k in range(2):
+            pair = interleave(re[:, 128 * k : 128 * k + 128], im[:, 128 * k : 128 * k + 128])
+            out_ref[4 * c + 2 * k] = pair[0].astype(BF16)
+            out_ref[4 * c + 2 * k + 1] = pair[1].astype(BF16)
+
+
+def focus_a_body(data_ref, kernel_ref, *refs):
+    out_refs, (row_ref, slab_ref, lhs_ref) = refs[:-3], refs[-3:]
+    rows, width = data_ref.shape[2], data_ref.shape[3]
+    narrow_slab(kernel_ref, row_ref, slab_ref)
+    lhs = load_lhs(data_ref, lhs_ref)
+    for o in range(len(out_refs) - 2, -1, -2):
+        prods = []
+        for part in range(2):
+            cols = []
+            for k in range(2):
+                first = width + chip_lane(o + k)
+                cols.append(
+                    jnp.concatenate(
+                        [slab_ref[part, :, aligned(first - 128 * r, 128)] for r in range(width // 128)], axis=0
+                    )
+                )
+            prods.append(jnp.dot(lhs, jnp.concatenate(cols, axis=1), preferred_element_type=F32))
+        re = (prods[0][:rows] - prods[1][rows:]).astype(BF16)
+        im = (prods[1][:rows] + prods[0][rows:]).astype(BF16)
+        for k in range(2):
+            out_refs[o + k][:, :128] = re[:, 128 * k : 128 * k + 128]
+            out_refs[o + k][:, 128:] = im[:, 128 * k : 128 * k + 128]
+
+
+def spread_b_body(kernel_ref, x_ref, out_ref, row_ref, slab_ref, cat_ref):
+    sources = x_ref.shape[0]
+    narrow_slab(kernel_ref, row_ref, slab_ref)
+    zeros = jnp.zeros((128, 128), BF16)
+    cat_ref[:128, :128] = zeros
+    cat_ref[128:, :128] = x_ref[...]
+    cat_ref[:sources, 128:] = x_ref[...]
+    cat_ref[sources:, 128:] = zeros
+    cat = cat_ref[...]
+    for b in range(0, sources // 128, 4):
+        prods = []
+        for part in range(2):
+            lhs = []
+            for k in range(2):
+                first = sources - 128 * (b + 2 * k) - 128
+                lhs.append(slab_ref[part, :, first : first + sources + 128])
+            prods.append(jnp.dot(jnp.concatenate(lhs, axis=0), cat, preferred_element_type=F32))
+        for k in range(2):
+            real, imag = prods[0][:, 128 * k : 128 * k + 128], prods[1][:, 128 * k : 128 * k + 128]
+            turned = pltpu.roll(imag, 64, 1)
+            both = (real + jnp.where(lane_half(turned.shape), -turned, turned)).astype(BF16)
+            for h in range(2):
+                row = 128 * (b + 2 * h + k)
+                out_ref[row : row + 128] = both[128 * h : 128 * h + 128]
+
+
+def spread_a_body(kernel_ref, peer_ref, *refs):
+    chips = peer_ref.shape[0]
+    own_refs, out_refs, (row_ref, slab_ref, x_ref) = refs[:chips], refs[chips : 2 * chips], refs[2 * chips :]
+    sources = 2 * chips * 128
+    narrow_slab(kernel_ref, row_ref, slab_ref)
+    for o in range(chips):
+        x_ref[128 * o : 128 * o + 128] = own_refs[o][...]
+        x_ref[128 * (chips + o) : 128 * (chips + o) + 128] = peer_ref[o]
+    x = x_ref[...]
+    me = lax.axis_index("panel")
+    chip, turn = me // 2, 128 - 256 * (me % 2)
+    for out in range(chips - 2, -1, -2):
+        prods = []
+        for part in range(2):
+            lhs = []
+            for k in range(2):
+                here = sources - 256 * (chip ^ (out + k))
+                blocks = [
+                    slab_ref[part, :, aligned(here + 256 * (chip ^ o) + shift, 128)]
+                    for shift in (0, turn)
+                    for o in range(chips)
+                ]
+                lhs.append(jnp.concatenate(blocks, axis=1))
+            prods.append(jnp.dot(jnp.concatenate(lhs, axis=0), x, preferred_element_type=F32))
+        re = (prods[0][:, :128] - prods[1][:, 128:]).astype(BF16)
+        im = (prods[0][:, 128:] + prods[1][:, :128]).astype(BF16)
+        for k in range(2):
+            out_refs[out + k][:, :128] = re[128 * k : 128 * k + 128]
+            out_refs[out + k][:, 128:] = im[128 * k : 128 * k + 128]
+
+
+def stack_body(after_ref, *refs):
+    for o, ref in enumerate(refs[:-1]):
+        refs[-1][o] = ref[...]
+
+
+def fit_two_body(data_ref, b_ref, *refs):
+    a_refs, sums_ref = refs[:-1], refs[-1]
+    panels, width = b_ref.shape[0], data_ref.shape[3]
+    acc = [jnp.zeros((8, 128), F32)] * 3
+
+    def add(mr, mi, at):
+        pr, pi = data_ref[0, 0, :, at], data_ref[0, 1, :, at]
+        acc[0] += fold(mr * pr + mi * pi)
+        acc[1] += fold(mr * pi - mi * pr)
+        acc[2] += fold(mr * mr + mi * mi)
+
+    for q in range(0, panels, 2):
+        mr, mi = interleave(b_ref[q].astype(F32), b_ref[q + 1].astype(F32))
+        add(mr, mi, pl.ds(width // 2 + 64 * q, 128))
+    for o, a_ref in enumerate(a_refs):
+        add(a_ref[:, :128].astype(F32), a_ref[:, 128:].astype(F32), aligned(chip_lane(o), 128))
+    for k in range(3):
+        sums_ref[k] = acc[k]
+
+
+def subtract_two_body(chips, data_ref, b_ref, *refs):
+    a_refs, sums_refs, (out_ref, mult_ref) = refs[:chips], refs[chips:-2], refs[-2:]
+    panels, width = b_ref.shape[0], data_ref.shape[3]
+    bm = out_ref.shape[2]
+    sums = sums_refs[0][...]
+    for ref in sums_refs[1:]:
+        sums = sums + ref[...]
+    num_re, num_im, energy = (jnp.sum(sums[k], keepdims=True) for k in range(3))
+    den = energy + 1e-6
+    fit_re, fit_im = num_re / den, num_im / den
+    rows = pl.ds(pl.multiple_of(pl.program_id(0) * bm, bm), bm)
+
+    def finish(mr, mi, at):
+        mult_ref[0, 0, :, at] = mr.astype(BF16)
+        mult_ref[0, 1, :, at] = mi.astype(BF16)
+        out_ref[0, 0, :, at] = data_ref[0, 0, rows, at] - (fit_re * mr - fit_im * mi)
+        out_ref[0, 1, :, at] = data_ref[0, 1, rows, at] - (fit_re * mi + fit_im * mr)
+
+    for q in range(0, panels, 2):
+        mr, mi = interleave(b_ref[q, rows].astype(F32), b_ref[q + 1, rows].astype(F32))
+        finish(mr, mi, pl.ds(width // 2 + 64 * q, 128))
+    for o, a_ref in enumerate(a_refs):
+        finish(a_ref[rows, :128].astype(F32), a_ref[rows, 128:].astype(F32), aligned(chip_lane(o), 128))
+
+
+def piped(recorded, receiver_kernel, source_kernel):
+    rows, width = recorded.shape[2], recorded.shape[3]
+    panels = lax.axis_size("panel")
+    chips = panels // 2
+    sources = rows * panels
+    shape = jax.ShapeDtypeStruct
+    resident = pl.BlockSpec(memory_space=pltpu.VMEM)
+    piece = shape((rows, 256), BF16)
+
+    def slabs(length):
+        return [pltpu.VMEM((2, 2 * length), F32), pltpu.VMEM((2, 128, 2 * length), BF16)]
+
+    def exchange(pieces):
+        return [pieces[0]] + [
+            lax.ppermute(pieces[o], "panel", [(k, k ^ (2 * o)) for k in range(panels)]) for o in range(1, chips)
+        ]
+
+    focused_b = pl.pallas_call(
+        focus_b_body,
+        out_shape=shape((panels, rows, 128), BF16),
+        scratch_shapes=slabs(width) + [pltpu.VMEM((2 * rows, width), BF16)],
+        compiler_params=medium(),
+        name="focus_b",
+    )(recorded, receiver_kernel)
+    columns_b = lax.all_to_all(focused_b, "panel", 0, 0, tiled=True).reshape(sources, 128)
+    focused_a = pl.pallas_call(
+        focus_a_body,
+        out_shape=[piece] * chips,
+        scratch_shapes=slabs(width) + [pltpu.VMEM((2 * rows, width), BF16)],
+        compiler_params=medium(),
+        name="focus_a",
+    )(recorded, receiver_kernel)
+    own = exchange(focused_a)
+    spread_b = pl.pallas_call(
+        spread_b_body,
+        in_specs=[pl.BlockSpec(), resident],
+        out_shape=shape((sources, 128), BF16),
+        scratch_shapes=slabs(sources) + [pltpu.VMEM((sources + 128, 256), BF16)],
+        compiler_params=medium(),
+        name="spread_b",
+    )(source_kernel, columns_b)
+    back_b = lax.all_to_all(spread_b.reshape(panels, rows, 128), "panel", 0, 0, tiled=True)
+    stacked = pl.pallas_call(
+        stack_body,
+        in_specs=[pl.BlockSpec(memory_space=pl.ANY)] + [resident] * chips,
+        out_shape=shape((chips, rows, 256), BF16),
+        compiler_params=small(),
+        name="stack",
+    )(spread_b, *own)
+    peer = lax.ppermute(stacked, "panel", [(k, k ^ 1) for k in range(panels)])
+    spread_a = pl.pallas_call(
+        spread_a_body,
+        in_specs=[pl.BlockSpec()] + [resident] * (1 + chips),
+        out_shape=[piece] * chips,
+        scratch_shapes=slabs(sources) + [pltpu.VMEM((sources, 256), BF16)],
+        compiler_params=medium(),
+        name="spread_a",
+    )(source_kernel, peer, *own)
+    back_a = exchange(spread_a)
+
+    sums = pl.pallas_call(
+        fit_two_body,
+        in_specs=[resident] * (2 + chips),
+        out_shape=shape((3, 8, 128), F32),
+        compiler_params=small(),
+        name="fit",
+    )(recorded, back_b, *back_a)
+    terms = partials(sums, "panel")
+    bm = 32
+    block = pl.BlockSpec((1, 2, bm, width), lambda i: (0, 0, i, 0))
+    return pl.pallas_call(
+        functools.partial(subtract_two_body, chips),
+        grid=(rows // bm,),
+        in_specs=[resident] * (2 + chips) + [pl.BlockSpec((3, 8, 128), lambda i: (0, 0, 0))] * len(terms),
+        out_specs=[block, block],
+        out_shape=[shape((1, 2, rows, width), F32), shape((1, 2, rows, width), BF16)],
+        compiler_params=small(),
+        name="subtract",
+    )(recorded, back_b, *back_a, *terms)
+
+
+def overlapping(panels):
+    return panels >= 4 and panels & (panels - 1) == 0
+
+
+def per_device(recorded, receiver_kernel, source_kernel):
+    rows, width = recorded.shape[2], recorded.shape[3]
+    panels = lax.axis_size("panel")
+    if rows == 128 and width == 128 * panels and overlapping(panels):
+        return piped(recorded, receiver_kernel, source_kernel)
+    return plain(recorded, receiver_kernel, source_kernel)
+
+
 def solution(mesh):
     placed = (P("freq", None, "panel", None), P("freq", None, None), P("freq", None, None))
     return jax.shard_map(

time: 92.8 us -> 98.7 us (1.064)
  blocking collectives: 61.9 us -> 21.6 us
  starting transfers between devices: 6.32 us -> 34.6 us
  waiting for transfers between devices: 4.89 us -> 21.4 us
  local copies, waits for them, and re-layouts: 0.01 us -> 2.32 us
  Pallas kernels: 18.7 us -> 17.6 us
    all_to_all x2 -> x1, blocking collectives: 61.9 us -> 21.6 us  [piped(): lax.all_to_all(focused_b, 'panel', 0, 0, tiled=True).reshape(sources, 128)]
    ppermute x0 -> x15, starting transfers between devices: none -> 24 us  [the longest x14 23.9 us: exchange(): lax.ppermute(pieces[o], 'panel', [(k, k ^ 2 * o) for k in range(panels)])]
    ppermute x0 -> x15, waiting for transfers between devices: none -> 15.8 us  [the longest x14 13.9 us: exchange(): lax.ppermute(pieces[o], 'panel', [(k, k ^ 2 * o) for k in range(panels)])]
    all_to_all x0 -> x1, starting transfers between devices: none -> 4.17 us  [piped(): lax.all_to_all(spread_b.reshape(panels, rows, 128), 'panel', 0, 0, tiled=...]
    unnamed x2 -> x10, local copies, waits for them, and re-layouts: 0.01 us -> 2.32 us
    pallas_call x4 -> x7, Pallas kernels: 18.7 us -> 17.6 us  [the longest x1 3.95 us: piped(): pl.pallas_call(focus_a_body, out_shape=[piece] * chips, scratch_shapes=sl...]
  transfers between devices with their start and end apart: 6 -> 22, of which waited for: 5 -> 10; matrix products, arithmetic and copies ran while one was open for 0% -> 0% of each run, Pallas kernels for 0% -> 7%
where the time goes in v3:
time: 98.7 us; the launch traced here: 98.4 us
  starting transfers between devices  34.6 us (35%)
  blocking collectives  21.6 us (22%)
  waiting for transfers between devices  21.4 us (22%)
  Pallas kernels  17.6 us (18%)
  local copies, waits for them, and re-layouts  2.32 us (2%)
    ppermute x14, starting transfers between devices, exchange(): lax.ppermute(pieces[o], 'panel', [(k, k ^ 2 * o) for k in range(panels)])  23.9 us
    all_to_all x1, blocking collectives, piped(): lax.all_to_all(focused_b, 'panel', 0, 0, tiled=True).reshape(sources, 128)  21.6 us
    ppermute x14, waiting for transfers between devices, exchange(): lax.ppermute(pieces[o], 'panel', [(k, k ^ 2 * o) for k in range(panels)])  13.9 us
    ppermute x6, starting transfers between devices, partials(): lax.ppermute(x, axis, [(k, k ^ span * d) for k in range(n)])  6.47 us
    ppermute x6, waiting for transfers between devices, partials(): lax.ppermute(x, axis, [(k, k ^ span * d) for k in range(n)])  5.6 us
    all_to_all x1, starting transfers between devices, piped(): lax.all_to_all(spread_b.reshape(panels, rows, 128), 'panel', 0, 0, tiled=...  4.17 us
    pallas_call x1, Pallas kernels, piped(): pl.pallas_call(focus_a_body, out_shape=[piece] * chips, scratch_shapes=sl...  3.95 us
    pallas_call x1, Pallas kernels, piped(): pl.pallas_call(spread_b_body, in_specs=[pl.BlockSpec(), resident], out_sh...  3.93 us
  transfers between devices with their start and end apart: 22, of which 10 were waited for; matrix products, arithmetic and copies ran while one was open for 0% of the time, Pallas kernels for 7%

profile of v3, /device:TPU:0, one launch (start us, length us, event | category | flops | bytes accessed | tf_op | source)
XLA Modules:
  0.0 98.4 jit_solution(3722255925200265852)
XLA Ops:
  0.6 0.0 copy-start
  0.6 1.6 %copy-done = f32[1,2,128,2048]{3,2,1,0:T(8,128)S(1)} copy-done((f32[1,2,128,2048]{3,2,1,0:T(8,128)S(1)}, f32[1,2,128,2048]{3,2,1,0:T(8,128)}, u32[]{:S(2)}) %copy-start) | copy-done | bytes 2097176
  2.2 0.7 copy-done.2
  2.9 3.3 %focus_b.1 = bf16[16,128,128]{2,1,0:T(8,128)(2,1)S(1)} custom-call(f32[1,2,128,2048]{3,2,1,0:T(8,128)S(1)} %copy-done, bf16[1,2,4095]{2,1,0:T(2,128)(2,1)S(1)} %copy-done.2), custom_call_target="tpu_custom_call" | custom-call | tf_op jit(solution)/shard_map/focus_b/pallas_call | solution.py:390
  6.3 0.0 copy-start.1
  6.3 0.0 copy-start.3
  6.3 21.6 %all_to_all.10 = bf16[16,128,128]{2,1,0:T(8,128)(2,1)S(1)} all-to-all(bf16[16,128,128]{2,1,0:T(8,128)(2,1)S(1)} %focus_b.1), channel_id=1, replica_groups=mesh['freq'=2,'panel'=16] {'panel'}, dimensions={0} | all-to-all | bytes 1048576 | tf_op jit(solution)/shard_map/all_to_all | solution.py:397
  27.9 3.9 %spread_b.1.after_ref = bf16[2048,128]{1,0:T(8,128)(2,1)} custom-call(bf16[1,2,4095]{2,1,0:T(2,128)(2,1)S(1)} %copy-done.4, bf16[2048,128]{1,0:T(8,128)(2,1)S(1)} %bitcast.2), custom_call_target="tpu_custom_call" | custom-call | tf_op jit(solution)/shard_map/spread_b/pallas_call | solution.py:406
  31.9 4.2 %all-to-all-start.1 = ((bf16[16,128,128]{2,1,0:T(8,128)(2,1)}), bf16[16,128,128]{2,1,0:T(8,128)(2,1)S(1)}, u32[]{:S(2)}, u32[]{:S(2)}) async-start(bf16[16,128,128]{2,1,0:T(8,128)(2,1)} %bitcast.1), calls=%async_computation.1 | async-start | bytes 1048576 | tf_op jit(solution)/shard_map/all_to_all | solution.py:414
  36.0 4.0 %focus_a.1 = (bf16[128,256]{1,0:T(8,128)(2,1)S(1)}, bf16[128,256]{1,0:T(8,128)(2,1)S(1)}, bf16[128,256]{1,0:T(8,128)(2,1)S(1)}, bf16[128,256]{1,0:T(8,128)(2,1)S...) custom-call(f32[1,2,128,2048]{3,2,1,0:T(8,128)S(1)} %copy-done.1, ...), custom_call_target="tpu_custom_call" | custom-call | tf_op jit(solution)/shard_map/focus_a/pallas_call | solution.py:398
  40.0 2.0 %collective-permute-start = (bf16[128,256]{1,0:T(8,128)(2,1)S(1)}, bf16[128,256]{1,0:T(8,128)(2,1)S(1)}, u32[]{:S(2)}, u32[]{:S(2)}) collective-permute-start(bf16[128,256]{1,0:T(8,128)(2,1)S(1)} %get-tuple-element.19), channel_id=1, source_target_pairs={{0,2},{1,3},{2,0},{3,1},{4,6},{5,7},{6,4},{7,5},{8,10},{9,11},{10,... | collective-permute-start | bytes 196616 | tf_op jit(solution)/shard_map/ppermute | solution.py:387
  42.0 1.5 %collective-permute-start.1 = (bf16[128,256]{1,0:T(8,128)(2,1)S(1)}, bf16[128,256]{1,0:T(8,128)(2,1)S(1)}, u32[]{:S(2)}, u32[]{:S(2)}) collective-permute-start(bf16[128,256]{1,0:T(8,128)(2,1)S(1)} %get-tuple-element.20), channel_id=1, source_target_pairs={{0,4},{1,5},{2,6},{3,7},{4,0},{5,1},{6,2},{7,3},{8,12},{9,13},{10,... | collective-permute-start | bytes 196616 | tf_op jit(solution)/shard_map/ppermute | solution.py:387
  43.5 0.1 collective-permute-start.2
  43.6 2.8 %collective-permute-start.3 = (bf16[128,256]{1,0:T(8,128)(2,1)S(1)}, bf16[128,256]{1,0:T(8,128)(2,1)S(1)}, u32[]{:S(2)}, u32[]{:S(2)}) collective-permute-start(bf16[128,256]{1,0:T(8,128)(2,1)S(1)} %get-tuple-element.22), channel_id=1, source_target_pairs={{0,8},{1,9},{2,10},{3,11},{4,12},{5,13},{6,14},{7,15},{8,0},{9,1},... | collective-permute-start | bytes 196616 | tf_op jit(solution)/shard_map/ppermute | solution.py:387
  46.4 1.5 %collective-permute-start.4 = (bf16[128,256]{1,0:T(8,128)(2,1)S(1)}, bf16[128,256]{1,0:T(8,128)(2,1)S(1)}, u32[]{:S(2)}, u32[]{:S(2)}) collective-permute-start(bf16[128,256]{1,0:T(8,128)(2,1)S(1)} %get-tuple-element.23), channel_id=1, source_target_pairs={{0,10},{1,11},{2,8},{3,9},{4,14},{5,15},{6,12},{7,13},{8,2},{9,3},... | collective-permute-start | bytes 196616 | tf_op jit(solution)/shard_map/ppermute | solution.py:387
  47.8 0.0 collective-permute-done.refs_1_
  47.8 3.3 %collective-permute-start.5 = (bf16[128,256]{1,0:T(8,128)(2,1)S(1)}, bf16[128,256]{1,0:T(8,128)(2,1)S(1)}, u32[]{:S(2)}, u32[]{:S(2)}) collective-permute-start(bf16[128,256]{1,0:T(8,128)(2,1)S(1)} %get-tuple-element.24), channel_id=1, source_target_pairs={{0,12},{1,13},{2,14},{3,15},{4,8},{5,9},{6,10},{7,11},{8,4},{9,5},... | collective-permute-start | bytes 196616 | tf_op jit(solution)/shard_map/ppermute | solution.py:387
  51.1 0.0 collective-permute-done.1.refs_2_
  51.1 0.8 collective-permute-start.6
  51.9 0.0 collective-permute-done.2.refs_3_
  51.9 6.9 %collective-permute-done.3.refs_4_ = bf16[128,256]{1,0:T(8,128)(2,1)S(1)} collective-permute-done((bf16[128,256]{1,0:T(8,128)(2,1)S(1)}, bf16[128,256]{1,0:T(8,128)(2,1)S(1)}, u32[]{:S(2)}, u32[]{:S(2)}) %collective-permute-start.3) | collective-permute-done | bytes 65568 | tf_op jit(solution)/shard_map/ppermute | solution.py:387
  58.8 2.3 %collective-permute-done.4.refs_5_ = bf16[128,256]{1,0:T(8,128)(2,1)S(1)} collective-permute-done((bf16[128,256]{1,0:T(8,128)(2,1)S(1)}, bf16[128,256]{1,0:T(8,128)(2,1)S(1)}, u32[]{:S(2)}, u32[]{:S(2)}) %collective-permute-start.4) | collective-permute-done | bytes 65568 | tf_op jit(solution)/shard_map/ppermute | solution.py:387
  61.1 0.0 collective-permute-done.5.refs_6_
  61.2 0.0 collective-permute-done.6.refs_7_
  61.2 0.1 collective-permute-start.7
  61.3 1.9 %collective-permute-done.7.peer_ref = bf16[8,128,256]{2,1,0:T(8,128)(2,1)S(1)} collective-permute-done((bf16[8,128,256]{2,1,0:T(8,128)(2,1)S(1)}, bf16[8,128,256]{2,1,0:T(8,128)(2,1)S(1)}, u32[]{:S(2)}, u32[]{:S(2)}) %collective-permute-start.7) | collective-permute-done | bytes 524320 | tf_op jit(solution)/shard_map/ppermute | solution.py:422
  63.2 3.1 %spread_a.1 = (bf16[128,256]{1,0:T(8,128)(2,1)S(1)}, bf16[128,256]{1,0:T(8,128)(2,1)S(1)}, bf16[128,256]{1,0:T(8,128)(2,1)S(1)}, bf16[128,256]{1,0:T(8,128)(2,1)...) custom-call(bf16[1,2,4095]{2,1,0:T(2,128)(2,1)S(1)} %copy-done.4, ...), custom_call_target="tpu_custom_call" | custom-call | tf_op jit(solution)/shard_map/spread_a/pallas_call | solution.py:423
  66.3 0.6 collective-permute-start.8
  66.9 2.8 %collective-permute-start.9 = (bf16[128,256]{1,0:T(8,128)(2,1)S(1)}, bf16[128,256]{1,0:T(8,128)(2,1)S(1)}, u32[]{:S(2)}, u32[]{:S(2)}) collective-permute-start(bf16[128,256]{1,0:T(8,128)(2,1)S(1)} %get-tuple-element.28), channel_id=1, source_target_pairs={{0,4},{1,5},{2,6},{3,7},{4,0},{5,1},{6,2},{7,3},{8,12},{9,13},{10,... | collective-permute-start | bytes 196616 | tf_op jit(solution)/shard_map/ppermute | solution.py:387
  69.7 0.9 collective-permute-start.10
  70.6 2.0 %collective-permute-start.11 = (bf16[128,256]{1,0:T(8,128)(2,1)S(1)}, bf16[128,256]{1,0:T(8,128)(2,1)S(1)}, u32[]{:S(2)}, u32[]{:S(2)}) collective-permute-start(bf16[128,256]{1,0:T(8,128)(2,1)S(1)} %get-tuple-element.30), channel_id=1, source_target_pairs={{0,8},{1,9},{2,10},{3,11},{4,12},{5,13},{6,14},{7,15},{8,0},{9,1},... | collective-permute-start | bytes 196616 | tf_op jit(solution)/shard_map/ppermute | solution.py:387
  72.6 0.9 collective-permute-start.12
  73.5 1.5 %collective-permute-start.13 = (bf16[128,256]{1,0:T(8,128)(2,1)S(1)}, bf16[128,256]{1,0:T(8,128)(2,1)S(1)}, u32[]{:S(2)}, u32[]{:S(2)}) collective-permute-start(bf16[128,256]{1,0:T(8,128)(2,1)S(1)} %get-tuple-element.32), channel_id=1, source_target_pairs={{0,12},{1,13},{2,14},{3,15},{4,8},{5,9},{6,10},{7,11},{8,4},{9,5},... | collective-permute-start | bytes 196616 | tf_op jit(solution)/shard_map/ppermute | solution.py:387
  75.1 0.0 collective-permute-done.9.refs_2_
  75.1 3.2 %collective-permute-start.14 = (bf16[128,256]{1,0:T(8,128)(2,1)S(1)}, bf16[128,256]{1,0:T(8,128)(2,1)S(1)}, u32[]{:S(2)}, u32[]{:S(2)}) collective-permute-start(bf16[128,256]{1,0:T(8,128)(2,1)S(1)} %get-tuple-element.33), channel_id=1, source_target_pairs={{0,14},{1,15},{2,12},{3,13},{4,10},{5,11},{6,8},{7,9},{8,6},{9,7},... | collective-permute-start | bytes 196616 | tf_op jit(solution)/shard_map/ppermute | solution.py:387
  78.3 2.9 %collective-permute-done.11.refs_4_ = bf16[128,256]{1,0:T(8,128)(2,1)S(1)} collective-permute-done((bf16[128,256]{1,0:T(8,128)(2,1)S(1)}, bf16[128,256]{1,0:T(8,128)(2,1)S(1)}, u32[]{:S(2)}, u32[]{:S(2)}) %collective-permute-start.11) | collective-permute-done | bytes 65568 | tf_op jit(solution)/shard_map/ppermute | solution.py:387
  81.1 1.8 %collective-permute-done.12.refs_5_ = bf16[128,256]{1,0:T(8,128)(2,1)S(1)} collective-permute-done((bf16[128,256]{1,0:T(8,128)(2,1)S(1)}, bf16[128,256]{1,0:T(8,128)(2,1)S(1)}, u32[]{:S(2)}, u32[]{:S(2)}) %collective-permute-start.12) | collective-permute-done | bytes 65568 | tf_op jit(solution)/shard_map/ppermute | solution.py:387
  83.0 0.7 fit.1
  83.7 1.9 %collective-permute-start.17 = (f32[3,8,128]{2,1,0:T(8,128)S(1)}, f32[3,8,128]{2,1,0:T(8,128)S(1)}, u32[]{:S(2)}, u32[]{:S(2)}) collective-permute-start(f32[3,8,128]{2,1,0:T(8,128)S(1)} %fit.1), channel_id=1, source_target_pairs={{0,12},{1,13},{2,14},{3,15},{4,8},{5,9},{6,10},{7,11},{8,4},{9,5},... | collective-permute-start | bytes 36872 | tf_op jit(solution)/shard_map/ppermute | solution.py:134
  85.6 2.7 %collective-permute-start.16 = (f32[3,8,128]{2,1,0:T(8,128)S(1)}, f32[3,8,128]{2,1,0:T(8,128)S(1)}, u32[]{:S(2)}, u32[]{:S(2)}) collective-permute-start(f32[3,8,128]{2,1,0:T(8,128)S(1)} %fit.1), channel_id=1, source_target_pairs={{0,8},{1,9},{2,10},{3,11},{4,12},{5,13},{6,14},{7,15},{8,0},{9,1},... | collective-permute-start | bytes 36872 | tf_op jit(solution)/shard_map/ppermute | solution.py:134
  88.3 0.9 collective-permute-done.17
  89.3 0.9 collective-permute-done.16
  90.2 1.8 %collective-permute-done.15 = f32[3,8,128]{2,1,0:T(8,128)S(1)} collective-permute-done((f32[3,8,128]{2,1,0:T(8,128)S(1)}, f32[3,8,128]{2,1,0:T(8,128)S(1)}, u32[]{:S(2)}, u32[]{:S(2)}) %collective-permute-start.15) | collective-permute-done | bytes 12320 | tf_op jit(solution)/shard_map/ppermute | solution.py:134
  92.0 1.4 %collective-permute-start.19 = (f32[3,8,128]{2,1,0:T(8,128)S(1)}, f32[3,8,128]{2,1,0:T(8,128)S(1)}, u32[]{:S(2)}, u32[]{:S(2)}) collective-permute-start(f32[3,8,128]{2,1,0:T(8,128)S(1)} %add_add_fusion.refs_8_), channel_id=1, source_target_pairs={{0,2},{1,3},{2,0},{3,1},{4,6},{5,7},{6,4},{7,5},{8,10},{9,11},{10,... | collective-permute-start | bytes 36872 | tf_op jit(solution)/shard_map/ppermute | solution.py:134
  93.4 0.4 collective-permute-start.18
  93.9 1.3 %collective-permute-done.20.refs_11_ = f32[3,8,128]{2,1,0:T(8,128)S(1)} collective-permute-done((f32[3,8,128]{2,1,0:T(8,128)S(1)}, f32[3,8,128]{2,1,0:T(8,128)S(1)}, u32[]{:S(2)}, u32[]{:S(2)}) %collective-permute-start.20) | collective-permute-done | bytes 12320 | tf_op jit(solution)/shard_map/ppermute | solution.py:134
  95.2 0.6 collective-permute-done.19.refs_10_
  95.8 2.6 %subtract.1 = (f32[1,2,128,2048]{3,2,1,0:T(8,128)}, bf16[1,2,128,2048]{3,2,1,0:T(8,128)(2,1)}) custom-call(f32[1,2,128,2048]{3,2,1,0:T(8,128)S(1)} %copy-done.1, bf16[16,128,128]{2,1,0:T(8,128)(2,1)S(1)} %all-to-all-done.1.b_ref, bf16[128,256]{1,0:T(8,128)(2,1)S(1)} %get-tuple-element.26.refs_0_, bf16[128,256]{1,0:T(8,128)(2,1)S(1)} %collective-permute-done.8.refs_1_, ...), custom_call_target="tpu_custom_call" | custom-call | tf_op jit(solution)/shard_map/subtract/pallas_call | solution.py:443
  (15 shorter events, 0.1 us)
Async XLA Ops:
  0.6 1.6 %copy-start = (f32[1,2,128,2048]{3,2,1,0:T(8,128)S(1)}, f32[1,2,128,2048]{3,2,1,0:T(8,128)}, u32[]{:S(2)}) copy-start(f32[1,2,128,2048]{3,2,1,0:T(8,128)} %data_ref.7) | copy-start | bytes 6291460
  2.2 0.7 copy-start.2
  2.9 25.0 %copy-start.4 = (bf16[1,2,4095]{2,1,0:T(2,128)(2,1)S(1)}, bf16[1,2,4095]{2,1,0:T(2,128)(2,1)}, u32[]{:S(2)}) copy-start(bf16[1,2,4095]{2,1,0:T(2,128)(2,1)} %kernel_ref.7) | copy-start | bytes 49144
  6.3 29.8 %copy-start.1 = (f32[1,2,128,2048]{3,2,1,0:T(8,128)S(1)}, f32[1,2,128,2048]{3,2,1,0:T(8,128)}, u32[]{:S(2)}) copy-start(f32[1,2,128,2048]{3,2,1,0:T(8,128)} %data_ref.7) | copy-start | bytes 6291460
  6.3 29.8 %copy-start.3 = (bf16[1,2,4095]{2,1,0:T(2,128)(2,1)S(1)}, bf16[1,2,4095]{2,1,0:T(2,128)(2,1)}, u32[]{:S(2)}) copy-start(bf16[1,2,4095]{2,1,0:T(2,128)(2,1)} %kernel_ref.6) | copy-start | bytes 49144
  31.9 51.1 %all-to-all-start.1 = ((bf16[16,128,128]{2,1,0:T(8,128)(2,1)}), bf16[16,128,128]{2,1,0:T(8,128)(2,1)S(1)}, u32[]{:S(2)}, u32[]{:S(2)}) async-start(bf16[16,128,128]{2,1,0:T(8,128)(2,1)} %bitcast.1), calls=%async_computation.1 | async-start | bytes 1048576 | tf_op jit(solution)/shard_map/all_to_all | solution.py:414
  40.0 7.8 %collective-permute-start = (bf16[128,256]{1,0:T(8,128)(2,1)S(1)}, bf16[128,256]{1,0:T(8,128)(2,1)S(1)}, u32[]{:S(2)}, u32[]{:S(2)}) collective-permute-start(bf16[128,256]{1,0:T(8,128)(2,1)S(1)} %get-tuple-element.19), channel_id=1, source_target_pairs={{0,2},{1,3},{2,0},{3,1},{4,6},{5,7},{6,4},{7,5},{8,10},{9,11},{10,... | collective-permute-start | bytes 196616 | tf_op jit(solution)/shard_map/ppermute | solution.py:387
  42.0 9.1 %collective-permute-start.1 = (bf16[128,256]{1,0:T(8,128)(2,1)S(1)}, bf16[128,256]{1,0:T(8,128)(2,1)S(1)}, u32[]{:S(2)}, u32[]{:S(2)}) collective-permute-start(bf16[128,256]{1,0:T(8,128)(2,1)S(1)} %get-tuple-element.20), channel_id=1, source_target_pairs={{0,4},{1,5},{2,6},{3,7},{4,0},{5,1},{6,2},{7,3},{8,12},{9,13},{10,... | collective-permute-start | bytes 196616 | tf_op jit(solution)/shard_map/ppermute | solution.py:387
  43.5 8.5 %collective-permute-start.2 = (bf16[128,256]{1,0:T(8,128)(2,1)S(1)}, bf16[128,256]{1,0:T(8,128)(2,1)S(1)}, u32[]{:S(2)}, u32[]{:S(2)}) collective-permute-start(bf16[128,256]{1,0:T(8,128)(2,1)S(1)} %get-tuple-element.21), channel_id=1, source_target_pairs={{0,6},{1,7},{2,4},{3,5},{4,2},{5,3},{6,0},{7,1},{8,14},{9,15},{10,... | collective-permute-start | bytes 196616 | tf_op jit(solution)/shard_map/ppermute | solution.py:387
  43.6 15.3 %collective-permute-start.3 = (bf16[128,256]{1,0:T(8,128)(2,1)S(1)}, bf16[128,256]{1,0:T(8,128)(2,1)S(1)}, u32[]{:S(2)}, u32[]{:S(2)}) collective-permute-start(bf16[128,256]{1,0:T(8,128)(2,1)S(1)} %get-tuple-element.22), channel_id=1, source_target_pairs={{0,8},{1,9},{2,10},{3,11},{4,12},{5,13},{6,14},{7,15},{8,0},{9,1},... | collective-permute-start | bytes 196616 | tf_op jit(solution)/shard_map/ppermute | solution.py:387
  46.4 14.8 %collective-permute-start.4 = (bf16[128,256]{1,0:T(8,128)(2,1)S(1)}, bf16[128,256]{1,0:T(8,128)(2,1)S(1)}, u32[]{:S(2)}, u32[]{:S(2)}) collective-permute-start(bf16[128,256]{1,0:T(8,128)(2,1)S(1)} %get-tuple-element.23), channel_id=1, source_target_pairs={{0,10},{1,11},{2,8},{3,9},{4,14},{5,15},{6,12},{7,13},{8,2},{9,3},... | collective-permute-start | bytes 196616 | tf_op jit(solution)/shard_map/ppermute | solution.py:387
  47.8 13.3 %collective-permute-start.5 = (bf16[128,256]{1,0:T(8,128)(2,1)S(1)}, bf16[128,256]{1,0:T(8,128)(2,1)S(1)}, u32[]{:S(2)}, u32[]{:S(2)}) collective-permute-start(bf16[128,256]{1,0:T(8,128)(2,1)S(1)} %get-tuple-element.24), channel_id=1, source_target_pairs={{0,12},{1,13},{2,14},{3,15},{4,8},{5,9},{6,10},{7,11},{8,4},{9,5},... | collective-permute-start | bytes 196616 | tf_op jit(solution)/shard_map/ppermute | solution.py:387
  51.1 10.0 %collective-permute-start.6 = (bf16[128,256]{1,0:T(8,128)(2,1)S(1)}, bf16[128,256]{1,0:T(8,128)(2,1)S(1)}, u32[]{:S(2)}, u32[]{:S(2)}) collective-permute-start(bf16[128,256]{1,0:T(8,128)(2,1)S(1)} %get-tuple-element.25), channel_id=1, source_target_pairs={{0,14},{1,15},{2,12},{3,13},{4,10},{5,11},{6,8},{7,9},{8,6},{9,7},... | collective-permute-start | bytes 196616 | tf_op jit(solution)/shard_map/ppermute | solution.py:387
  61.2 2.0 %collective-permute-start.7 = (bf16[8,128,256]{2,1,0:T(8,128)(2,1)S(1)}, bf16[8,128,256]{2,1,0:T(8,128)(2,1)S(1)}, u32[]{:S(2)}, u32[]{:S(2)}) collective-permute-start(bf16[8,128,256]{2,1,0:T(8,128)(2,1)S(1)} %stack.1), channel_id=1, source_target_pairs={{0,1},{1,0},{2,3},{3,2},{4,5},{5,4},{6,7},{7,6},{8,9},{9,8},{10,11... | collective-permute-start | bytes 1572872 | tf_op jit(solution)/shard_map/ppermute | solution.py:422
  66.3 7.3 %collective-permute-start.8 = (bf16[128,256]{1,0:T(8,128)(2,1)S(1)}, bf16[128,256]{1,0:T(8,128)(2,1)S(1)}, u32[]{:S(2)}, u32[]{:S(2)}) collective-permute-start(bf16[128,256]{1,0:T(8,128)(2,1)S(1)} %get-tuple-element.27), channel_id=1, source_target_pairs={{0,2},{1,3},{2,0},{3,1},{4,6},{5,7},{6,4},{7,5},{8,10},{9,11},{10,... | collective-permute-start | bytes 196616 | tf_op jit(solution)/shard_map/ppermute | solution.py:387
  66.9 8.2 %collective-permute-start.9 = (bf16[128,256]{1,0:T(8,128)(2,1)S(1)}, bf16[128,256]{1,0:T(8,128)(2,1)S(1)}, u32[]{:S(2)}, u32[]{:S(2)}) collective-permute-start(bf16[128,256]{1,0:T(8,128)(2,1)S(1)} %get-tuple-element.28), channel_id=1, source_target_pairs={{0,4},{1,5},{2,6},{3,7},{4,0},{5,1},{6,2},{7,3},{8,12},{9,13},{10,... | collective-permute-start | bytes 196616 | tf_op jit(solution)/shard_map/ppermute | solution.py:387
  69.7 8.6 %collective-permute-start.10 = (bf16[128,256]{1,0:T(8,128)(2,1)S(1)}, bf16[128,256]{1,0:T(8,128)(2,1)S(1)}, u32[]{:S(2)}, u32[]{:S(2)}) collective-permute-start(bf16[128,256]{1,0:T(8,128)(2,1)S(1)} %get-tuple-element.29), channel_id=1, source_target_pairs={{0,6},{1,7},{2,4},{3,5},{4,2},{5,3},{6,0},{7,1},{8,14},{9,15},{10,... | collective-permute-start | bytes 196616 | tf_op jit(solution)/shard_map/ppermute | solution.py:387
  70.6 10.5 %collective-permute-start.11 = (bf16[128,256]{1,0:T(8,128)(2,1)S(1)}, bf16[128,256]{1,0:T(8,128)(2,1)S(1)}, u32[]{:S(2)}, u32[]{:S(2)}) collective-permute-start(bf16[128,256]{1,0:T(8,128)(2,1)S(1)} %get-tuple-element.30), channel_id=1, source_target_pairs={{0,8},{1,9},{2,10},{3,11},{4,12},{5,13},{6,14},{7,15},{8,0},{9,1},... | collective-permute-start | bytes 196616 | tf_op jit(solution)/shard_map/ppermute | solution.py:387
  72.6 10.3 %collective-permute-start.12 = (bf16[128,256]{1,0:T(8,128)(2,1)S(1)}, bf16[128,256]{1,0:T(8,128)(2,1)S(1)}, u32[]{:S(2)}, u32[]{:S(2)}) collective-permute-start(bf16[128,256]{1,0:T(8,128)(2,1)S(1)} %get-tuple-element.31), channel_id=1, source_target_pairs={{0,10},{1,11},{2,8},{3,9},{4,14},{5,15},{6,12},{7,13},{8,2},{9,3},... | collective-permute-start | bytes 196616 | tf_op jit(solution)/shard_map/ppermute | solution.py:387
  73.5 9.4 %collective-permute-start.13 = (bf16[128,256]{1,0:T(8,128)(2,1)S(1)}, bf16[128,256]{1,0:T(8,128)(2,1)S(1)}, u32[]{:S(2)}, u32[]{:S(2)}) collective-permute-start(bf16[128,256]{1,0:T(8,128)(2,1)S(1)} %get-tuple-element.32), channel_id=1, source_target_pairs={{0,12},{1,13},{2,14},{3,15},{4,8},{5,9},{6,10},{7,11},{8,4},{9,5},... | collective-permute-start | bytes 196616 | tf_op jit(solution)/shard_map/ppermute | solution.py:387
  75.1 7.9 %collective-permute-start.14 = (bf16[128,256]{1,0:T(8,128)(2,1)S(1)}, bf16[128,256]{1,0:T(8,128)(2,1)S(1)}, u32[]{:S(2)}, u32[]{:S(2)}) collective-permute-start(bf16[128,256]{1,0:T(8,128)(2,1)S(1)} %get-tuple-element.33), channel_id=1, source_target_pairs={{0,14},{1,15},{2,12},{3,13},{4,10},{5,11},{6,8},{7,9},{8,6},{9,7},... | collective-permute-start | bytes 196616 | tf_op jit(solution)/shard_map/ppermute | solution.py:387
  83.7 5.6 %collective-permute-start.17 = (f32[3,8,128]{2,1,0:T(8,128)S(1)}, f32[3,8,128]{2,1,0:T(8,128)S(1)}, u32[]{:S(2)}, u32[]{:S(2)}) collective-permute-start(f32[3,8,128]{2,1,0:T(8,128)S(1)} %fit.1), channel_id=1, source_target_pairs={{0,12},{1,13},{2,14},{3,15},{4,8},{5,9},{6,10},{7,11},{8,4},{9,5},... | collective-permute-start | bytes 36872 | tf_op jit(solution)/shard_map/ppermute | solution.py:134
  85.6 4.6 %collective-permute-start.16 = (f32[3,8,128]{2,1,0:T(8,128)S(1)}, f32[3,8,128]{2,1,0:T(8,128)S(1)}, u32[]{:S(2)}, u32[]{:S(2)}) collective-permute-start(f32[3,8,128]{2,1,0:T(8,128)S(1)} %fit.1), channel_id=1, source_target_pairs={{0,8},{1,9},{2,10},{3,11},{4,12},{5,13},{6,14},{7,15},{8,0},{9,1},... | collective-permute-start | bytes 36872 | tf_op jit(solution)/shard_map/ppermute | solution.py:134
  88.3 3.7 %collective-permute-start.15 = (f32[3,8,128]{2,1,0:T(8,128)S(1)}, f32[3,8,128]{2,1,0:T(8,128)S(1)}, u32[]{:S(2)}, u32[]{:S(2)}) collective-permute-start(f32[3,8,128]{2,1,0:T(8,128)S(1)} %fit.1), channel_id=1, source_target_pairs={{0,4},{1,5},{2,6},{3,7},{4,0},{5,1},{6,2},{7,3},{8,12},{9,13},{10,... | collective-permute-start | bytes 36872 | tf_op jit(solution)/shard_map/ppermute | solution.py:134
  92.0 3.2 %collective-permute-start.20 = (f32[3,8,128]{2,1,0:T(8,128)S(1)}, f32[3,8,128]{2,1,0:T(8,128)S(1)}, u32[]{:S(2)}, u32[]{:S(2)}) collective-permute-start(f32[3,8,128]{2,1,0:T(8,128)S(1)} %add_add_fusion.refs_8_), channel_id=1, source_target_pairs={{0,3},{1,2},{2,1},{3,0},{4,7},{5,6},{6,5},{7,4},{8,11},{9,10},{10,... | collective-permute-start | bytes 36872 | tf_op jit(solution)/shard_map/ppermute | solution.py:134
  92.0 3.8 %collective-permute-start.19 = (f32[3,8,128]{2,1,0:T(8,128)S(1)}, f32[3,8,128]{2,1,0:T(8,128)S(1)}, u32[]{:S(2)}, u32[]{:S(2)}) collective-permute-start(f32[3,8,128]{2,1,0:T(8,128)S(1)} %add_add_fusion.refs_8_), channel_id=1, source_target_pairs={{0,2},{1,3},{2,0},{3,1},{4,6},{5,7},{6,4},{7,5},{8,10},{9,11},{10,... | collective-permute-start | bytes 36872 | tf_op jit(solution)/shard_map/ppermute | solution.py:134
  93.4 2.3 %collective-permute-start.18 = (f32[3,8,128]{2,1,0:T(8,128)S(1)}, f32[3,8,128]{2,1,0:T(8,128)S(1)}, u32[]{:S(2)}, u32[]{:S(2)}) collective-permute-start(f32[3,8,128]{2,1,0:T(8,128)S(1)} %add_add_fusion.refs_8_), channel_id=1, source_target_pairs={{0,1},{1,0},{2,3},{3,2},{4,5},{5,4},{6,7},{7,6},{8,9},{9,8},{10,11... | collective-permute-start | bytes 36872 | tf_op jit(solution)/shard_map/ppermute | solution.py:134

commit v4 on v2

--- a/solution.py
+++ b/solution.py
@@ -1,9 +1,12 @@
+import functools
+
 import jax
 import jax.numpy as jnp
 from jax import lax
 from jax.experimental import pallas as pl
 from jax.experimental.pallas import tpu as pltpu
 from jax.sharding import PartitionSpec as P
+
 
 F32 = jnp.float32
 BF16 = jnp.bfloat16
@@ -25,7 +28,7 @@
         slab_ref[part, 128:256, 128:] = slab_ref[part, 0:128, : length - 128]
 
 
-def focus_body(data_ref, kernel_ref, out_ref, row_ref, slab_ref, lhs_ref):
+def focus_all_body(data_ref, kernel_ref, out_ref, row_ref, slab_ref, lhs_ref):
     rows, width = data_ref.shape[2], data_ref.shape[3]
     cols = out_ref.shape[2] // 2
     build_slab(kernel_ref, row_ref, slab_ref)
@@ -69,7 +72,7 @@
 
 
 def fit_body(data_ref, y_ref, sums_ref):
-    panels, rows, cols = y_ref.shape[0], y_ref.shape[1], y_ref.shape[2] // 2
+    panels, cols = y_ref.shape[0], y_ref.shape[2] // 2
     strip = max(1, 128 // cols)
     acc = [jnp.zeros((8, 128), F32)] * 3
     for q in range(0, panels, strip):
@@ -108,6 +111,10 @@
     return pltpu.CompilerParams(vmem_limit_bytes=VMEM_LIMIT, **kw)
 
 
+def medium():
+    return pltpu.CompilerParams(vmem_limit_bytes=32 * 1024 * 1024)
+
+
 def small():
     return pltpu.CompilerParams(vmem_limit_bytes=16 * 1024 * 1024)
 
@@ -129,7 +136,7 @@
     return terms
 
 
-def per_device(recorded, receiver_kernel, source_kernel):
+def plain(recorded, receiver_kernel, source_kernel):
     rows, width = recorded.shape[2], recorded.shape[3]
     panels = lax.axis_size("panel")
     sources = rows * panels
@@ -137,7 +144,7 @@
     shape = jax.ShapeDtypeStruct
 
     focused = pl.pallas_call(
-        focus_body,
+        focus_all_body,
         out_shape=shape((panels, rows, 2 * cols), BF16),
         scratch_shapes=[
             pltpu.VMEM((2, 2 * width), F32),
@@ -179,6 +186,280 @@
     )(recorded, back, *terms)
 
 
+def narrow_slab(kernel_ref, row_ref, slab_ref):
+    taps = kernel_ref.shape[-1]
+    row_ref[:, :taps] = kernel_ref[0].astype(F32)
+    for part in range(2):
+        base = jnp.broadcast_to(row_ref[part : part + 1, :], (8, taps + 1))
+        top = pltpu.roll(base, 1, 1, stride=1, stride_axis=0)
+        for step in range(8):
+            low = pltpu.roll(top, 16 * step, 1) if step else top
+            high = pltpu.roll(top, 16 * step + 8, 1)
+            slab_ref[part, 16 * step : 16 * step + 16, :] = jnp.concatenate([low, high], axis=0).astype(BF16)
+
+
+def aligned(start, size):
+    return pl.ds(pl.multiple_of(start, 128), size)
+
+
+def turns(chips, parity, home=False):
+    half = chips // 2
+    near, far = [*range(2, half), 1], [*range(half, chips)]
+    return far + near if bool(parity) != home else near + far
+
+
+def chip_at(chips, position, other=False, home=False):
+    me = lax.axis_index("panel")
+    if position == chips - 1:
+        return me // 2
+    even, odd = turns(chips, 0, home)[position], turns(chips, 1, home)[position]
+    parity = 1 - me % 2 if other else me % 2
+    return (me // 2) ^ (even + parity * (odd - even))
+
+
+def focus_columns(chips, offsets, slab_ref, lhs_ref, out_refs):
+    rows, width = lhs_ref.shape[0] // 2, lhs_ref.shape[1]
+    lhs = lhs_ref[...]
+    for offset, out_ref in zip(offsets, out_refs):
+        first = width + 256 * chip_at(chips, offset)
+        prods = []
+        for part in range(2):
+            rhs = [slab_ref[part, :, aligned(first - 128 * r, 256)] for r in range(width // 128)]
+            prods.append(jnp.dot(lhs, jnp.concatenate(rhs, axis=0), preferred_element_type=F32))
+        out_ref[:, :256] = (prods[0][:rows] - prods[1][rows:]).astype(BF16)
+        out_ref[:, 256:] = (prods[1][:rows] + prods[0][rows:]).astype(BF16)
+
+
+def focus_first_body(chips, offsets, data_hbm, kernel_hbm, *refs):
+    out_refs, (slab_ref, lhs_ref, row_ref, data_ref, kernel_ref, sems) = refs[: len(offsets)], refs[len(offsets) :]
+    rows = data_ref.shape[2]
+    taps_in = pltpu.make_async_copy(kernel_hbm, kernel_ref, sems.at[0])
+    data_in = pltpu.make_async_copy(data_hbm, data_ref, sems.at[1])
+    taps_in.start()
+    data_in.start()
+    taps_in.wait()
+    narrow_slab(kernel_ref, row_ref, slab_ref)
+    data_in.wait()
+    lhs_ref[:rows] = data_ref[0, 0].astype(BF16)
+    lhs_ref[rows:] = data_ref[0, 1].astype(BF16)
+    focus_columns(chips, offsets, slab_ref, lhs_ref, out_refs)
+
+
+def focus_rest_body(chips, offsets, slab_ref, lhs_ref, *out_refs):
+    focus_columns(chips, offsets, slab_ref, lhs_ref, out_refs)
+
+
+def stack_body(*refs):
+    for k, ref in enumerate(refs[:-1]):
+        refs[-1][k] = ref[...]
+
+
+def source_products(chips, slab_ref, stacks, outs):
+    length = slab_ref.shape[2] // 2
+    turn = 128 - 256 * (lax.axis_index("panel") % 2)
+    sides = [(refs[other], other, ins) for *refs, ins in stacks for other in (False, True)]
+    x = jnp.concatenate([ref[k] for ref, _, ins in sides for k in range(len(ins))], axis=0)
+    prods = []
+    for part in range(2):
+        lhs = []
+        for out in outs:
+            here = length - 256 * chip_at(chips, out, home=True)
+            blocks = [
+                slab_ref[part, :, aligned(here + 256 * chip_at(chips, k, other) + turn * other, 128)]
+                for _, other, ins in sides
+                for k in ins
+            ]
+            lhs.append(jnp.concatenate(blocks, axis=1))
+        prods.append(jnp.dot(jnp.concatenate(lhs, axis=0), x, preferred_element_type=F32))
+    return prods[0][:, :256] - prods[1][:, 256:], prods[0][:, 256:] + prods[1][:, :256]
+
+
+def slab_body(kernel_ref, slab_ref, row_ref):
+    narrow_slab(kernel_ref, row_ref, slab_ref)
+
+
+def begin_first_body(chips, outs, early, slab_ref, own_ref, peer_ref, acc_ref):
+    re, im = source_products(chips, slab_ref, [(own_ref, peer_ref, early)], outs)
+    for h in range(2):
+        acc_ref[h, :, :256] = re[128 * h : 128 * h + 128]
+        acc_ref[h, :, 256:] = im[128 * h : 128 * h + 128]
+
+
+def finish_first_body(chips, outs, late, slab_ref, own_ref, peer_ref, acc_ref, *out_refs):
+    re, im = source_products(chips, slab_ref, [(own_ref, peer_ref, late)], outs)
+    for h in range(2):
+        out_refs[h][:, :256] = (acc_ref[h, :, :256] + re[128 * h : 128 * h + 128]).astype(BF16)
+        out_refs[h][:, 256:] = (acc_ref[h, :, 256:] + im[128 * h : 128 * h + 128]).astype(BF16)
+
+
+def finish_rest_body(chips, outs, early, late, slab_ref, own_ref, peer_ref, late_own_ref, late_peer_ref, *out_refs):
+    stacks = [(own_ref, peer_ref, early), (late_own_ref, late_peer_ref, late)]
+    for k in range(0, len(outs), 2):
+        re, im = source_products(chips, slab_ref, stacks, outs[k : k + 2])
+        for h in range(2):
+            out_refs[k + h][:, :256] = re[128 * h : 128 * h + 128].astype(BF16)
+            out_refs[k + h][:, 256:] = im[128 * h : 128 * h + 128].astype(BF16)
+
+
+def fit_pieces_body(data_ref, *refs):
+    piece_refs, sums_ref = refs[:-1], refs[-1]
+    acc = [jnp.zeros((8, 128), F32)] * 3
+    for offset, ref in enumerate(piece_refs):
+        mr, mi = ref[:, :256].astype(F32), ref[:, 256:].astype(F32)
+        at = aligned(256 * chip_at(len(piece_refs), offset, home=True), 256)
+        pr, pi = data_ref[0, 0, :, at], data_ref[0, 1, :, at]
+        acc[0] += fold(mr * pr + mi * pi)
+        acc[1] += fold(mr * pi - mi * pr)
+        acc[2] += fold(mr * mr + mi * mi)
+    for k in range(3):
+        sums_ref[k] = acc[k]
+
+
+def subtract_pieces_body(chips, data_ref, *refs):
+    piece_refs, sums_refs, (out_ref, mult_ref) = refs[:chips], refs[chips:-2], refs[-2:]
+    bm = out_ref.shape[2]
+    sums = sums_refs[0][...]
+    for ref in sums_refs[1:]:
+        sums = sums + ref[...]
+    num_re, num_im, energy = (jnp.sum(sums[k], keepdims=True) for k in range(3))
+    den = energy + 1e-6
+    fit_re, fit_im = num_re / den, num_im / den
+    rows = pl.ds(pl.multiple_of(pl.program_id(0) * bm, bm), bm)
+    for offset, ref in enumerate(piece_refs):
+        at = aligned(256 * chip_at(len(piece_refs), offset, home=True), 256)
+        mult_ref[0, 0, :, at] = ref[rows, :256]
+        mult_ref[0, 1, :, at] = ref[rows, 256:]
+        mr, mi = ref[rows, :256].astype(F32), ref[rows, 256:].astype(F32)
+        out_ref[0, 0, :, at] = data_ref[0, 0, rows, at] - (fit_re * mr - fit_im * mi)
+        out_ref[0, 1, :, at] = data_ref[0, 1, rows, at] - (fit_re * mi + fit_im * mr)
+
+
+def piped(recorded, receiver_kernel, source_kernel):
+    rows, width = recorded.shape[2], recorded.shape[3]
+    panels = lax.axis_size("panel")
+    chips = panels // 2
+    own = chips - 1
+    first, rest = (0, 1), (own, *range(2, own))
+    early, late = (own, *range(chips // 2 - 1)), tuple(range(chips // 2 - 1, own))
+    sources = rows * panels
+    shape = jax.ShapeDtypeStruct
+    resident = pl.BlockSpec(memory_space=pltpu.VMEM)
+    in_hbm = pl.BlockSpec(memory_space=pltpu.HBM)
+    piece = shape((rows, 512), BF16)
+
+    def hbm(x):
+        return pltpu.with_memory_space_constraint(x, pltpu.HBM)
+
+    def exchange(pieces, positions, name):
+        got = {}
+        for x, p in zip(pieces, positions):
+            if p != own:
+                pairs = [(k, k ^ (2 * turns(chips, k % 2, name == "home")[p])) for k in range(panels)]
+                x = lax.ppermute(x, "panel", pairs)
+            got[p] = x
+        return got
+
+    def swap(pieces):
+        mine = pl.pallas_call(
+            stack_body,
+            in_specs=[resident] * len(pieces),
+            out_shape=pltpu.VMEM((len(pieces), rows, 512), BF16),
+            compiler_params=small(),
+        )(*pieces)
+        return mine, lax.ppermute(mine, "panel", [(k, k ^ 1) for k in range(panels)])
+
+    *pieces, slab_r, lhs = pl.pallas_call(
+        functools.partial(focus_first_body, chips, first),
+        in_specs=[in_hbm, in_hbm],
+        out_shape=[piece] * len(first)
+        + [pltpu.VMEM((2, 128, 2 * width), BF16), pltpu.VMEM((2 * rows, width), BF16)],
+        scratch_shapes=[
+            pltpu.VMEM((2, 2 * width), F32),
+            pltpu.VMEM(recorded.shape, F32),
+            pltpu.VMEM(receiver_kernel.shape, BF16),
+            pltpu.SemaphoreType.DMA((2,)),
+        ],
+        compiler_params=medium(),
+        name="focus_first",
+    )(hbm(recorded), hbm(receiver_kernel))
+    got = exchange(pieces, first, "away")
+    pieces = pl.pallas_call(
+        functools.partial(focus_rest_body, chips, rest),
+        in_specs=[resident] * 2,
+        out_shape=[piece] * len(rest),
+        compiler_params=medium(),
+        name="focus_rest",
+    )(slab_r, lhs)
+    got |= exchange(pieces, rest, "away")
+    early_own, early_peer = swap([got[o] for o in early])
+    slab_s = pl.pallas_call(
+        slab_body,
+        in_specs=[pl.BlockSpec()],
+        out_shape=pltpu.VMEM((2, 128, 2 * sources), BF16),
+        scratch_shapes=[pltpu.VMEM((2, 2 * sources), F32)],
+        compiler_params=medium(),
+        name="slab_source",
+    )(source_kernel)
+
+    acc_first = pl.pallas_call(
+        functools.partial(begin_first_body, chips, first, early),
+        in_specs=[resident] * 3,
+        out_shape=pltpu.VMEM((len(first), rows, 512), F32),
+        compiler_params=medium(),
+        name="begin_first",
+    )(slab_s, early_own, early_peer)
+    late_own, late_peer = swap([got[o] for o in late])
+    pieces = pl.pallas_call(
+        functools.partial(finish_first_body, chips, first, late),
+        in_specs=[resident] * 4,
+        out_shape=[piece] * len(first),
+        compiler_params=medium(),
+        name="finish_first",
+    )(slab_s, late_own, late_peer, acc_first)
+    home = exchange(pieces, first, "home")
+    pieces = pl.pallas_call(
+        functools.partial(finish_rest_body, chips, rest, early, late),
+        in_specs=[resident] * 5,
+        out_shape=[piece] * len(rest),
+        compiler_params=medium(),
+        name="finish_rest",
+    )(slab_s, early_own, early_peer, late_own, late_peer)
+    home |= exchange(pieces, rest, "home")
+    back = [home[o] for o in range(chips)]
+
+    sums = pl.pallas_call(
+        fit_pieces_body,
+        in_specs=[resident] * (1 + chips),
+        out_shape=shape((3, 8, 128), F32),
+        compiler_params=small(),
+        name="fit",
+    )(recorded, *back)
+    terms = partials(sums, "panel")
+    bm = 32
+    block = pl.BlockSpec((1, 2, bm, width), lambda i: (0, 0, i, 0))
+    return pl.pallas_call(
+        functools.partial(subtract_pieces_body, chips),
+        grid=(rows // bm,),
+        in_specs=[resident] * (1 + chips) + [pl.BlockSpec((3, 8, 128), lambda i: (0, 0, 0))] * len(terms),
+        out_specs=[block, block],
+        out_shape=[shape((1, 2, rows, width), F32), shape((1, 2, rows, width), BF16)],
+        compiler_params=small(),
+        name="subtract",
+    )(recorded, *back, *terms)
+
+
+def overlapping(panels):
+    return panels >= 8 and panels & (panels - 1) == 0
+
+
+def per_device(recorded, receiver_kernel, source_kernel):
+    rows, width = recorded.shape[2], recorded.shape[3]
+    panels = lax.axis_size("panel")
+    if rows == 128 and width == 128 * panels and overlapping(panels):
+        return piped(recorded, receiver_kernel, source_kernel)
+    return plain(recorded, receiver_kernel, source_kernel)
+
+
 def solution(mesh):
     placed = (P("freq", None, "panel", None), P("freq", None, None), P("freq", None, None))
     return jax.shard_map(

time: 92.8 us -> 85.1 us (0.917)
  blocking collectives: 61.9 us -> 0 us
  starting transfers between devices: 6.32 us -> 40.8 us
  waiting for transfers between devices: 4.89 us -> 27.7 us
  Pallas kernels: 18.7 us -> 15.5 us
    all_to_all x2 -> x0, blocking collectives: 61.9 us -> none  [the longest x1 32.2 us: per_device(): lax.all_to_all(focused, 'panel', 0, 0, tiled=True)]
    ppermute x0 -> x16, starting transfers between devices: none -> 34.5 us  [the longest x14 34.3 us: exchange(): x = lax.ppermute(x, 'panel', pairs)]
    ppermute x0 -> x16, waiting for transfers between devices: none -> 21.4 us  [the longest x14 20.2 us: exchange(): x = lax.ppermute(x, 'panel', pairs)]
    pallas_call x4 -> x10, Pallas kernels: 18.7 us -> 15.5 us  [the longest x1 3.57 us: piped(): pl.pallas_call(functools.partial(focus_rest_body, chips, rest), in_specs=...]
    ppermute x6, waiting for transfers between devices: 4.89 us -> 6.34 us  [partials(): lax.ppermute(x, axis, [(k, k ^ span * d) for k in range(n)])]
  transfers between devices with their start and end apart: 6 -> 22, of which waited for: 5 -> 10; matrix products, arithmetic and copies ran while one was open for 0% -> 0% of each run, Pallas kernels for 0% -> 3%
where the time goes in v4:
time: 85.1 us; the launch traced here: 84.8 us
  starting transfers between devices  40.8 us (48%)
  waiting for transfers between devices  27.7 us (33%)
  Pallas kernels  15.5 us (18%)
    ppermute x14, starting transfers between devices, exchange(): x = lax.ppermute(x, 'panel', pairs)  34.3 us
    ppermute x14, waiting for transfers between devices, exchange(): x = lax.ppermute(x, 'panel', pairs)  20.2 us
    ppermute x6, waiting for transfers between devices, partials(): lax.ppermute(x, axis, [(k, k ^ span * d) for k in range(n)])  6.34 us
    ppermute x6, starting transfers between devices, partials(): lax.ppermute(x, axis, [(k, k ^ span * d) for k in range(n)])  6.3 us
    pallas_call x1, Pallas kernels, piped(): pl.pallas_call(functools.partial(focus_rest_body, chips, rest), in_specs=...  3.57 us
    pallas_call x1, Pallas kernels, piped(): pl.pallas_call(functools.partial(finish_rest_body, chips, rest, early, la...  3.54 us
    pallas_call x1, Pallas kernels, piped(): pl.pallas_call(functools.partial(focus_first_body, chips, first), in_spec...  2.98 us
    pallas_call x1, Pallas kernels, piped(): pl.pallas_call(functools.partial(subtract_pieces_body, chips), grid=(rows...  2.47 us
  transfers between devices with their start and end apart: 22, of which 10 were waited for; matrix products, arithmetic and copies ran while one was open for 0% of the time, Pallas kernels for 3%

profile of v4, /device:TPU:0, one launch (start us, length us, event | category | flops | bytes accessed | tf_op | source)
XLA Modules:
  0.0 84.8 jit_solution(22150945378550060)
XLA Ops:
  0.6 3.0 %focus_first.1 = (bf16[128,512]{1,0:T(8,128)(2,1)S(1)}, bf16[128,512]{1,0:T(8,128)(2,1)S(1)}, bf16[2,128,4096]{2,1,0:T(8,128)(2,1)S(1)}, bf16[256,2048]{1,0:T(8,128)(2,1)S(1)}) custom-call(f32[1,2,128,2048]{3,2,1,0:T(8,128)} %data_ref.3, bf16[1,2,4095]{2,1,0:T(2,128)(2,1)} %kernel_hbm.1), custom_call_target="tpu_custom_call" | custom-call | tf_op jit(solution)/shard_map/focus_first/pallas_call | solution.py:371
  3.6 0.0 copy-start.1
  3.6 3.6 %focus_rest.1 = (bf16[128,512]{1,0:T(8,128)(2,1)S(1)}, bf16[128,512]{1,0:T(8,128)(2,1)S(1)}, bf16[128,512]{1,0:T(8,128)(2,1)S(1)}, bf16[128,512]{1,0:T(8,128)(2,...) custom-call(bf16[2,128,4096]{2,1,0:T(8,128)(2,1)S(1)} %get-tuple-element.20.slab_ref, ...), custom_call_target="tpu_custom_call" | custom-call | tf_op jit(solution)/shard_map/focus_rest/pallas_call | solution.py:386
  7.2 4.1 %collective-permute-start = (bf16[128,512]{1,0:T(8,128)(2,1)S(1)}, bf16[128,512]{1,0:T(8,128)(2,1)S(1)}, u32[]{:S(2)}, u32[]{:S(2)}) collective-permute-start(bf16[128,512]{1,0:T(8,128)(2,1)S(1)} %get-tuple-element.22), channel_id=1, source_target_pairs={{0,8},{1,15},{2,10},{3,13},{4,12},{5,11},{6,14},{7,9},{8,0},{9,7},... | collective-permute-start | bytes 393224 | tf_op jit(solution)/shard_map/ppermute | solution.py:358
  11.3 1.3 %collective-permute-start.1 = (bf16[128,512]{1,0:T(8,128)(2,1)S(1)}, bf16[128,512]{1,0:T(8,128)(2,1)S(1)}, u32[]{:S(2)}, u32[]{:S(2)}) collective-permute-start(bf16[128,512]{1,0:T(8,128)(2,1)S(1)} %get-tuple-element.23), channel_id=1, source_target_pairs={{0,10},{1,5},{2,8},{3,7},{4,14},{5,1},{6,12},{7,3},{8,2},{9,13},{1... | collective-permute-start | bytes 393224 | tf_op jit(solution)/shard_map/ppermute | solution.py:358
  12.6 3.6 %collective-permute-start.2 = (bf16[128,512]{1,0:T(8,128)(2,1)S(1)}, bf16[128,512]{1,0:T(8,128)(2,1)S(1)}, u32[]{:S(2)}, u32[]{:S(2)}) collective-permute-start(bf16[128,512]{1,0:T(8,128)(2,1)S(1)} %get-tuple-element.24), channel_id=1, source_target_pairs={{0,12},{1,7},{2,14},{3,5},{4,8},{5,3},{6,10},{7,1},{8,4},{9,15},{1... | collective-permute-start | bytes 393224 | tf_op jit(solution)/shard_map/ppermute | solution.py:358
  16.2 0.0 collective-permute-start.3
  16.2 1.7 %collective-permute-start.7 = (bf16[128,512]{1,0:T(8,128)(2,1)S(1)}, bf16[128,512]{1,0:T(8,128)(2,1)S(1)}, u32[]{:S(2)}, u32[]{:S(2)}) collective-permute-start(bf16[128,512]{1,0:T(8,128)(2,1)S(1)} %get-tuple-element.29), channel_id=1, source_target_pairs={{0,2},{1,13},{2,0},{3,15},{4,6},{5,9},{6,4},{7,11},{8,10},{9,5},{1... | collective-permute-start | bytes 393224 | tf_op jit(solution)/shard_map/ppermute | solution.py:358
  17.9 0.8 collective-permute-done.refs_0_
  18.7 4.0 %collective-permute-start.5 = (bf16[128,512]{1,0:T(8,128)(2,1)S(1)}, bf16[128,512]{1,0:T(8,128)(2,1)S(1)}, u32[]{:S(2)}, u32[]{:S(2)}) collective-permute-start(bf16[128,512]{1,0:T(8,128)(2,1)S(1)} %get-tuple-element.27), channel_id=1, source_target_pairs={{0,4},{1,9},{2,6},{3,11},{4,0},{5,13},{6,2},{7,15},{8,12},{9,1},{1... | collective-permute-start | bytes 393224 | tf_op jit(solution)/shard_map/ppermute | solution.py:358
  22.7 8.0 %collective-permute-done.1.refs_1_ = bf16[128,512]{1,0:T(8,128)(2,1)S(1)} collective-permute-done((bf16[128,512]{1,0:T(8,128)(2,1)S(1)}, bf16[128,512]{1,0:T(8,128)(2,1)S(1)}, u32[]{:S(2)}, u32[]{:S(2)}) %collective-permute-start.1) | collective-permute-done | bytes 131104 | tf_op jit(solution)/shard_map/ppermute | solution.py:358
  30.7 0.7 collective-permute-start.6
  31.4 0.0 collective-permute-done.2.refs_2_
  31.4 0.0 collective-permute-done.3.refs_3_
  31.4 0.1 collective-permute-start.4
  31.5 0.0 collective-permute-done.7.refs_3_
  31.5 5.0 %collective-permute-done.6.refs_2_ = bf16[128,512]{1,0:T(8,128)(2,1)S(1)} collective-permute-done((bf16[128,512]{1,0:T(8,128)(2,1)S(1)}, bf16[128,512]{1,0:T(8,128)(2,1)S(1)}, u32[]{:S(2)}, u32[]{:S(2)}) %collective-permute-start.6) | collective-permute-done | bytes 131104 | tf_op jit(solution)/shard_map/ppermute | solution.py:358
  36.6 0.1 collective-permute-start.8
  36.7 0.7 slab_source.1.slab_ref
  37.5 0.0 collective-permute-done.4.peer_ref.late_peer_ref
  37.5 1.1 %collective-permute-done.8.peer_ref = bf16[4,128,512]{2,1,0:T(8,128)(2,1)S(1)} collective-permute-done((bf16[4,128,512]{2,1,0:T(8,128)(2,1)S(1)}, bf16[4,128,512]{2,1,0:T(8,128)(2,1)S(1)}, u32[]{:S(2)}, u32[]{:S(2)}) %collective-permute-start.8) | collective-permute-done | bytes 524320 | tf_op jit(solution)/shard_map/ppermute | solution.py:369
  38.6 3.5 %finish_rest.1 = (bf16[128,512]{1,0:T(8,128)(2,1)S(1)}, bf16[128,512]{1,0:T(8,128)(2,1)S(1)}, bf16[128,512]{1,0:T(8,128)(2,1)S(1)}, bf16[128,512]{1,0:T(8,128)(2...) custom-call(bf16[2,128,4096]{2,1,0:T(8,128)(2,1)S(1)} %slab_source.1.slab_ref, ...), custom_call_target="tpu_custom_call" | custom-call | tf_op jit(solution)/shard_map/finish_rest/pallas_call | solution.py:420
  42.1 3.6 %collective-permute-start.11 = (bf16[128,512]{1,0:T(8,128)(2,1)S(1)}, bf16[128,512]{1,0:T(8,128)(2,1)S(1)}, u32[]{:S(2)}, u32[]{:S(2)}) collective-permute-start(bf16[128,512]{1,0:T(8,128)(2,1)S(1)} %get-tuple-element.32), channel_id=1, source_target_pairs={{0,12},{1,3},{2,14},{3,1},{4,8},{5,7},{6,10},{7,5},{8,4},{9,11},{1... | collective-permute-start | bytes 393224 | tf_op jit(solution)/shard_map/ppermute | solution.py:358
  45.7 0.8 collective-permute-start.12
  46.5 0.0 collective-permute-start.13
  46.5 2.4 %collective-permute-start.14 = (bf16[128,512]{1,0:T(8,128)(2,1)S(1)}, bf16[128,512]{1,0:T(8,128)(2,1)S(1)}, u32[]{:S(2)}, u32[]{:S(2)}) collective-permute-start(bf16[128,512]{1,0:T(8,128)(2,1)S(1)} %get-tuple-element.35), channel_id=1, source_target_pairs={{0,6},{1,13},{2,4},{3,15},{4,2},{5,9},{6,0},{7,11},{8,14},{9,5},{1... | collective-permute-start | bytes 393224 | tf_op jit(solution)/shard_map/ppermute | solution.py:358
  49.0 1.1 %collective-permute-start.15 = (bf16[128,512]{1,0:T(8,128)(2,1)S(1)}, bf16[128,512]{1,0:T(8,128)(2,1)S(1)}, u32[]{:S(2)}, u32[]{:S(2)}) collective-permute-start(bf16[128,512]{1,0:T(8,128)(2,1)S(1)} %get-tuple-element.36), channel_id=1, source_target_pairs={{0,2},{1,15},{2,0},{3,13},{4,6},{5,11},{6,4},{7,9},{8,10},{9,7},{1... | collective-permute-start | bytes 393224 | tf_op jit(solution)/shard_map/ppermute | solution.py:358
  50.0 0.7 begin_first.1.acc_ref
  50.7 0.0 copy-start
  50.8 0.7 finish_first.1
  51.5 7.6 %collective-permute-start.10 = (bf16[128,512]{1,0:T(8,128)(2,1)S(1)}, bf16[128,512]{1,0:T(8,128)(2,1)S(1)}, u32[]{:S(2)}, u32[]{:S(2)}) collective-permute-start(bf16[128,512]{1,0:T(8,128)(2,1)S(1)} %get-tuple-element.31), channel_id=1, source_target_pairs={{0,10},{1,7},{2,8},{3,5},{4,14},{5,3},{6,12},{7,1},{8,2},{9,15},{1... | collective-permute-start | bytes 393224 | tf_op jit(solution)/shard_map/ppermute | solution.py:358
  59.1 0.0 collective-permute-done.12.refs_3_
  59.1 3.5 %collective-permute-start.9 = (bf16[128,512]{1,0:T(8,128)(2,1)S(1)}, bf16[128,512]{1,0:T(8,128)(2,1)S(1)}, u32[]{:S(2)}, u32[]{:S(2)}) collective-permute-start(bf16[128,512]{1,0:T(8,128)(2,1)S(1)} %get-tuple-element.30), channel_id=1, source_target_pairs={{0,8},{1,5},{2,10},{3,7},{4,12},{5,1},{6,14},{7,3},{8,0},{9,13},{1... | collective-permute-start | bytes 393224 | tf_op jit(solution)/shard_map/ppermute | solution.py:358
  62.6 0.0 collective-permute-done.13.refs_4_
  62.6 2.0 %collective-permute-done.10.refs_1_ = bf16[128,512]{1,0:T(8,128)(2,1)S(1)} collective-permute-done((bf16[128,512]{1,0:T(8,128)(2,1)S(1)}, bf16[128,512]{1,0:T(8,128)(2,1)S(1)}, u32[]{:S(2)}, u32[]{:S(2)}) %collective-permute-start.10) | collective-permute-done | bytes 131104 | tf_op jit(solution)/shard_map/ppermute | solution.py:358
  64.6 4.4 %collective-permute-done.9.refs_0_ = bf16[128,512]{1,0:T(8,128)(2,1)S(1)} collective-permute-done((bf16[128,512]{1,0:T(8,128)(2,1)S(1)}, bf16[128,512]{1,0:T(8,128)(2,1)S(1)}, u32[]{:S(2)}, u32[]{:S(2)}) %collective-permute-start.9) | collective-permute-done | bytes 131104 | tf_op jit(solution)/shard_map/ppermute | solution.py:358
  69.0 0.7 fit.1
  69.7 0.1 collective-permute-start.16
  69.7 2.8 %collective-permute-start.17 = (f32[3,8,128]{2,1,0:T(8,128)S(1)}, f32[3,8,128]{2,1,0:T(8,128)S(1)}, u32[]{:S(2)}, u32[]{:S(2)}) collective-permute-start(f32[3,8,128]{2,1,0:T(8,128)S(1)} %fit.1), channel_id=1, source_target_pairs={{0,8},{1,9},{2,10},{3,11},{4,12},{5,13},{6,14},{7,15},{8,0},{9,1},... | collective-permute-start | bytes 36872 | tf_op jit(solution)/shard_map/ppermute | solution.py:134
  72.5 1.6 %collective-permute-start.18 = (f32[3,8,128]{2,1,0:T(8,128)S(1)}, f32[3,8,128]{2,1,0:T(8,128)S(1)}, u32[]{:S(2)}, u32[]{:S(2)}) collective-permute-start(f32[3,8,128]{2,1,0:T(8,128)S(1)} %fit.1), channel_id=1, source_target_pairs={{0,12},{1,13},{2,14},{3,15},{4,8},{5,9},{6,10},{7,11},{8,4},{9,5},... | collective-permute-start | bytes 36872 | tf_op jit(solution)/shard_map/ppermute | solution.py:134
  74.1 0.0 collective-permute-done.16
  74.1 0.4 collective-permute-done.17
  74.5 3.5 %collective-permute-done.18 = f32[3,8,128]{2,1,0:T(8,128)S(1)} collective-permute-done((f32[3,8,128]{2,1,0:T(8,128)S(1)}, f32[3,8,128]{2,1,0:T(8,128)S(1)}, u32[]{:S(2)}, u32[]{:S(2)}) %collective-permute-start.18) | collective-permute-done | bytes 12320 | tf_op jit(solution)/shard_map/ppermute | solution.py:134
  78.0 1.2 %collective-permute-start.20 = (f32[3,8,128]{2,1,0:T(8,128)S(1)}, f32[3,8,128]{2,1,0:T(8,128)S(1)}, u32[]{:S(2)}, u32[]{:S(2)}) collective-permute-start(f32[3,8,128]{2,1,0:T(8,128)S(1)} %add_add_fusion.refs_8_), channel_id=1, source_target_pairs={{0,2},{1,3},{2,0},{3,1},{4,6},{5,7},{6,4},{7,5},{8,10},{9,11},{10,... | collective-permute-start | bytes 36872 | tf_op jit(solution)/shard_map/ppermute | solution.py:134
  79.2 0.7 collective-permute-start.21
  79.9 1.9 %collective-permute-done.20.refs_10_ = f32[3,8,128]{2,1,0:T(8,128)S(1)} collective-permute-done((f32[3,8,128]{2,1,0:T(8,128)S(1)}, f32[3,8,128]{2,1,0:T(8,128)S(1)}, u32[]{:S(2)}, u32[]{:S(2)}) %collective-permute-start.20) | collective-permute-done | bytes 12320 | tf_op jit(solution)/shard_map/ppermute | solution.py:134
  81.8 0.5 collective-permute-done.21.refs_11_
  82.3 2.5 %subtract.1 = (f32[1,2,128,2048]{3,2,1,0:T(8,128)}, bf16[1,2,128,2048]{3,2,1,0:T(8,128)(2,1)}) custom-call(f32[1,2,128,2048]{3,2,1,0:T(8,128)S(1)} %copy-done, bf16[128,512]{1,0:T(8,128)(2,1)S(1)} %collective-permute-done.9.refs_0_, bf16[128,512]{1,0:T(8,128)(2,1)S(1)} %collective-permute-done.10.refs_1_, ...), custom_call_target="tpu_custom_call" | custom-call | tf_op jit(solution)/shard_map/subtract/pallas_call | solution.py:440
  (11 shorter events, 0.1 us)
Async XLA Ops:
  3.6 33.1 %copy-start.1 = (bf16[1,2,4095]{2,1,0:T(2,128)(2,1)S(1)}, bf16[1,2,4095]{2,1,0:T(2,128)(2,1)}, u32[]{:S(2)}) copy-start(bf16[1,2,4095]{2,1,0:T(2,128)(2,1)} %kernel_ref.1) | copy-start | bytes 49144
  7.2 11.5 %collective-permute-start = (bf16[128,512]{1,0:T(8,128)(2,1)S(1)}, bf16[128,512]{1,0:T(8,128)(2,1)S(1)}, u32[]{:S(2)}, u32[]{:S(2)}) collective-permute-start(bf16[128,512]{1,0:T(8,128)(2,1)S(1)} %get-tuple-element.22), channel_id=1, source_target_pairs={{0,8},{1,15},{2,10},{3,13},{4,12},{5,11},{6,14},{7,9},{8,0},{9,7},... | collective-permute-start | bytes 393224 | tf_op jit(solution)/shard_map/ppermute | solution.py:358
  11.3 19.4 %collective-permute-start.1 = (bf16[128,512]{1,0:T(8,128)(2,1)S(1)}, bf16[128,512]{1,0:T(8,128)(2,1)S(1)}, u32[]{:S(2)}, u32[]{:S(2)}) collective-permute-start(bf16[128,512]{1,0:T(8,128)(2,1)S(1)} %get-tuple-element.23), channel_id=1, source_target_pairs={{0,10},{1,5},{2,8},{3,7},{4,14},{5,1},{6,12},{7,3},{8,2},{9,13},{1... | collective-permute-start | bytes 393224 | tf_op jit(solution)/shard_map/ppermute | solution.py:358
  12.6 18.8 %collective-permute-start.2 = (bf16[128,512]{1,0:T(8,128)(2,1)S(1)}, bf16[128,512]{1,0:T(8,128)(2,1)S(1)}, u32[]{:S(2)}, u32[]{:S(2)}) collective-permute-start(bf16[128,512]{1,0:T(8,128)(2,1)S(1)} %get-tuple-element.24), channel_id=1, source_target_pairs={{0,12},{1,7},{2,14},{3,5},{4,8},{5,3},{6,10},{7,1},{8,4},{9,15},{1... | collective-permute-start | bytes 393224 | tf_op jit(solution)/shard_map/ppermute | solution.py:358
  16.2 15.2 %collective-permute-start.3 = (bf16[128,512]{1,0:T(8,128)(2,1)S(1)}, bf16[128,512]{1,0:T(8,128)(2,1)S(1)}, u32[]{:S(2)}, u32[]{:S(2)}) collective-permute-start(bf16[128,512]{1,0:T(8,128)(2,1)S(1)} %get-tuple-element.25), channel_id=1, source_target_pairs={{0,14},{1,3},{2,12},{3,1},{4,10},{5,7},{6,8},{7,5},{8,6},{9,11},{1... | collective-permute-start | bytes 393224 | tf_op jit(solution)/shard_map/ppermute | solution.py:358
  16.2 15.3 %collective-permute-start.7 = (bf16[128,512]{1,0:T(8,128)(2,1)S(1)}, bf16[128,512]{1,0:T(8,128)(2,1)S(1)}, u32[]{:S(2)}, u32[]{:S(2)}) collective-permute-start(bf16[128,512]{1,0:T(8,128)(2,1)S(1)} %get-tuple-element.29), channel_id=1, source_target_pairs={{0,2},{1,13},{2,0},{3,15},{4,6},{5,9},{6,4},{7,11},{8,10},{9,5},{1... | collective-permute-start | bytes 393224 | tf_op jit(solution)/shard_map/ppermute | solution.py:358
  18.7 12.8 %collective-permute-start.5 = (bf16[128,512]{1,0:T(8,128)(2,1)S(1)}, bf16[128,512]{1,0:T(8,128)(2,1)S(1)}, u32[]{:S(2)}, u32[]{:S(2)}) collective-permute-start(bf16[128,512]{1,0:T(8,128)(2,1)S(1)} %get-tuple-element.27), channel_id=1, source_target_pairs={{0,4},{1,9},{2,6},{3,11},{4,0},{5,13},{6,2},{7,15},{8,12},{9,1},{1... | collective-permute-start | bytes 393224 | tf_op jit(solution)/shard_map/ppermute | solution.py:358
  30.7 5.9 %collective-permute-start.6 = (bf16[128,512]{1,0:T(8,128)(2,1)S(1)}, bf16[128,512]{1,0:T(8,128)(2,1)S(1)}, u32[]{:S(2)}, u32[]{:S(2)}) collective-permute-start(bf16[128,512]{1,0:T(8,128)(2,1)S(1)} %get-tuple-element.28), channel_id=1, source_target_pairs={{0,6},{1,11},{2,4},{3,9},{4,2},{5,15},{6,0},{7,13},{8,14},{9,3},{1... | collective-permute-start | bytes 393224 | tf_op jit(solution)/shard_map/ppermute | solution.py:358
  31.4 6.0 %collective-permute-start.4 = (bf16[4,128,512]{2,1,0:T(8,128)(2,1)S(1)}, bf16[4,128,512]{2,1,0:T(8,128)(2,1)S(1)}, u32[]{:S(2)}, u32[]{:S(2)}) collective-permute-start(bf16[4,128,512]{2,1,0:T(8,128)(2,1)S(1)} %shard_map.50.own_ref.late_own_ref), channel_id=1, source_target_pairs={{0,1},{1,0},{2,3},{3,2},{4,5},{5,4},{6,7},{7,6},{8,9},{9,8},{10,11... | collective-permute-start | bytes 1572872 | tf_op jit(solution)/shard_map/ppermute | solution.py:369
  36.6 2.0 %collective-permute-start.8 = (bf16[4,128,512]{2,1,0:T(8,128)(2,1)S(1)}, bf16[4,128,512]{2,1,0:T(8,128)(2,1)S(1)}, u32[]{:S(2)}, u32[]{:S(2)}) collective-permute-start(bf16[4,128,512]{2,1,0:T(8,128)(2,1)S(1)} %shard_map.51.own_ref), channel_id=1, source_target_pairs={{0,1},{1,0},{2,3},{3,2},{4,5},{5,4},{6,7},{7,6},{8,9},{9,8},{10,11... | collective-permute-start | bytes 1572872 | tf_op jit(solution)/shard_map/ppermute | solution.py:369
  42.1 9.4 %collective-permute-start.11 = (bf16[128,512]{1,0:T(8,128)(2,1)S(1)}, bf16[128,512]{1,0:T(8,128)(2,1)S(1)}, u32[]{:S(2)}, u32[]{:S(2)}) collective-permute-start(bf16[128,512]{1,0:T(8,128)(2,1)S(1)} %get-tuple-element.32), channel_id=1, source_target_pairs={{0,12},{1,3},{2,14},{3,1},{4,8},{5,7},{6,10},{7,5},{8,4},{9,11},{1... | collective-permute-start | bytes 393224 | tf_op jit(solution)/shard_map/ppermute | solution.py:358
  45.7 13.4 %collective-permute-start.12 = (bf16[128,512]{1,0:T(8,128)(2,1)S(1)}, bf16[128,512]{1,0:T(8,128)(2,1)S(1)}, u32[]{:S(2)}, u32[]{:S(2)}) collective-permute-start(bf16[128,512]{1,0:T(8,128)(2,1)S(1)} %get-tuple-element.33), channel_id=1, source_target_pairs={{0,14},{1,9},{2,12},{3,11},{4,10},{5,13},{6,8},{7,15},{8,6},{9,1},... | collective-permute-start | bytes 393224 | tf_op jit(solution)/shard_map/ppermute | solution.py:358
  46.5 16.0 %collective-permute-start.13 = (bf16[128,512]{1,0:T(8,128)(2,1)S(1)}, bf16[128,512]{1,0:T(8,128)(2,1)S(1)}, u32[]{:S(2)}, u32[]{:S(2)}) collective-permute-start(bf16[128,512]{1,0:T(8,128)(2,1)S(1)} %get-tuple-element.34), channel_id=1, source_target_pairs={{0,4},{1,11},{2,6},{3,9},{4,0},{5,15},{6,2},{7,13},{8,12},{9,3},{1... | collective-permute-start | bytes 393224 | tf_op jit(solution)/shard_map/ppermute | solution.py:358
  46.5 16.0 %collective-permute-start.14 = (bf16[128,512]{1,0:T(8,128)(2,1)S(1)}, bf16[128,512]{1,0:T(8,128)(2,1)S(1)}, u32[]{:S(2)}, u32[]{:S(2)}) collective-permute-start(bf16[128,512]{1,0:T(8,128)(2,1)S(1)} %get-tuple-element.35), channel_id=1, source_target_pairs={{0,6},{1,13},{2,4},{3,15},{4,2},{5,9},{6,0},{7,11},{8,14},{9,5},{1... | collective-permute-start | bytes 393224 | tf_op jit(solution)/shard_map/ppermute | solution.py:358
  49.0 13.6 %collective-permute-start.15 = (bf16[128,512]{1,0:T(8,128)(2,1)S(1)}, bf16[128,512]{1,0:T(8,128)(2,1)S(1)}, u32[]{:S(2)}, u32[]{:S(2)}) collective-permute-start(bf16[128,512]{1,0:T(8,128)(2,1)S(1)} %get-tuple-element.36), channel_id=1, source_target_pairs={{0,2},{1,15},{2,0},{3,13},{4,6},{5,11},{6,4},{7,9},{8,10},{9,7},{1... | collective-permute-start | bytes 393224 | tf_op jit(solution)/shard_map/ppermute | solution.py:358
  50.7 18.2 %copy-start = (f32[1,2,128,2048]{3,2,1,0:T(8,128)S(1)}, f32[1,2,128,2048]{3,2,1,0:T(8,128)}, u32[]{:S(2)}) copy-start(f32[1,2,128,2048]{3,2,1,0:T(8,128)} %data_ref.3) | copy-start | bytes 6291460
  51.5 13.1 %collective-permute-start.10 = (bf16[128,512]{1,0:T(8,128)(2,1)S(1)}, bf16[128,512]{1,0:T(8,128)(2,1)S(1)}, u32[]{:S(2)}, u32[]{:S(2)}) collective-permute-start(bf16[128,512]{1,0:T(8,128)(2,1)S(1)} %get-tuple-element.31), channel_id=1, source_target_pairs={{0,10},{1,7},{2,8},{3,5},{4,14},{5,3},{6,12},{7,1},{8,2},{9,15},{1... | collective-permute-start | bytes 393224 | tf_op jit(solution)/shard_map/ppermute | solution.py:358
  59.1 9.9 %collective-permute-start.9 = (bf16[128,512]{1,0:T(8,128)(2,1)S(1)}, bf16[128,512]{1,0:T(8,128)(2,1)S(1)}, u32[]{:S(2)}, u32[]{:S(2)}) collective-permute-start(bf16[128,512]{1,0:T(8,128)(2,1)S(1)} %get-tuple-element.30), channel_id=1, source_target_pairs={{0,8},{1,5},{2,10},{3,7},{4,12},{5,1},{6,14},{7,3},{8,0},{9,13},{1... | collective-permute-start | bytes 393224 | tf_op jit(solution)/shard_map/ppermute | solution.py:358
  69.7 4.5 %collective-permute-start.16 = (f32[3,8,128]{2,1,0:T(8,128)S(1)}, f32[3,8,128]{2,1,0:T(8,128)S(1)}, u32[]{:S(2)}, u32[]{:S(2)}) collective-permute-start(f32[3,8,128]{2,1,0:T(8,128)S(1)} %fit.1), channel_id=1, source_target_pairs={{0,4},{1,5},{2,6},{3,7},{4,0},{5,1},{6,2},{7,3},{8,12},{9,13},{10,... | collective-permute-start | bytes 36872 | tf_op jit(solution)/shard_map/ppermute | solution.py:134
  69.7 4.8 %collective-permute-start.17 = (f32[3,8,128]{2,1,0:T(8,128)S(1)}, f32[3,8,128]{2,1,0:T(8,128)S(1)}, u32[]{:S(2)}, u32[]{:S(2)}) collective-permute-start(f32[3,8,128]{2,1,0:T(8,128)S(1)} %fit.1), channel_id=1, source_target_pairs={{0,8},{1,9},{2,10},{3,11},{4,12},{5,13},{6,14},{7,15},{8,0},{9,1},... | collective-permute-start | bytes 36872 | tf_op jit(solution)/shard_map/ppermute | solution.py:134
  72.5 5.5 %collective-permute-start.18 = (f32[3,8,128]{2,1,0:T(8,128)S(1)}, f32[3,8,128]{2,1,0:T(8,128)S(1)}, u32[]{:S(2)}, u32[]{:S(2)}) collective-permute-start(f32[3,8,128]{2,1,0:T(8,128)S(1)} %fit.1), channel_id=1, source_target_pairs={{0,12},{1,13},{2,14},{3,15},{4,8},{5,9},{6,10},{7,11},{8,4},{9,5},... | collective-permute-start | bytes 36872 | tf_op jit(solution)/shard_map/ppermute | solution.py:134
  78.0 1.9 %collective-permute-start.19 = (f32[3,8,128]{2,1,0:T(8,128)S(1)}, f32[3,8,128]{2,1,0:T(8,128)S(1)}, u32[]{:S(2)}, u32[]{:S(2)}) collective-permute-start(f32[3,8,128]{2,1,0:T(8,128)S(1)} %add_add_fusion.refs_8_), channel_id=1, source_target_pairs={{0,1},{1,0},{2,3},{3,2},{4,5},{5,4},{6,7},{7,6},{8,9},{9,8},{10,11... | collective-permute-start | bytes 36872 | tf_op jit(solution)/shard_map/ppermute | solution.py:134
  78.0 3.8 %collective-permute-start.20 = (f32[3,8,128]{2,1,0:T(8,128)S(1)}, f32[3,8,128]{2,1,0:T(8,128)S(1)}, u32[]{:S(2)}, u32[]{:S(2)}) collective-permute-start(f32[3,8,128]{2,1,0:T(8,128)S(1)} %add_add_fusion.refs_8_), channel_id=1, source_target_pairs={{0,2},{1,3},{2,0},{3,1},{4,6},{5,7},{6,4},{7,5},{8,10},{9,11},{10,... | collective-permute-start | bytes 36872 | tf_op jit(solution)/shard_map/ppermute | solution.py:134
  79.2 3.1 %collective-permute-start.21 = (f32[3,8,128]{2,1,0:T(8,128)S(1)}, f32[3,8,128]{2,1,0:T(8,128)S(1)}, u32[]{:S(2)}, u32[]{:S(2)}) collective-permute-start(f32[3,8,128]{2,1,0:T(8,128)S(1)} %add_add_fusion.refs_8_), channel_id=1, source_target_pairs={{0,3},{1,2},{2,1},{3,0},{4,7},{5,6},{6,5},{7,4},{8,11},{9,10},{10,... | collective-permute-start | bytes 36872 | tf_op jit(solution)/shard_map/ppermute | solution.py:134

commit v5 on v4

--- a/solution.py
+++ b/solution.py
@@ -250,8 +250,9 @@
 
 
 def stack_body(*refs):
-    for k, ref in enumerate(refs[:-1]):
-        refs[-1][k] = ref[...]
+    pieces, out_ref = refs[-1 - refs[-1].shape[0] : -1], refs[-1]
+    for k, ref in enumerate(pieces):
+        out_ref[k] = ref[...]
 
 
 def source_products(chips, slab_ref, stacks, outs):
@@ -278,27 +279,20 @@
     narrow_slab(kernel_ref, row_ref, slab_ref)
 
 
-def begin_first_body(chips, outs, early, slab_ref, own_ref, peer_ref, acc_ref):
-    re, im = source_products(chips, slab_ref, [(own_ref, peer_ref, early)], outs)
-    for h in range(2):
-        acc_ref[h, :, :256] = re[128 * h : 128 * h + 128]
-        acc_ref[h, :, 256:] = im[128 * h : 128 * h + 128]
-
-
-def finish_first_body(chips, outs, late, slab_ref, own_ref, peer_ref, acc_ref, *out_refs):
-    re, im = source_products(chips, slab_ref, [(own_ref, peer_ref, late)], outs)
-    for h in range(2):
-        out_refs[h][:, :256] = (acc_ref[h, :, :256] + re[128 * h : 128 * h + 128]).astype(BF16)
-        out_refs[h][:, 256:] = (acc_ref[h, :, 256:] + im[128 * h : 128 * h + 128]).astype(BF16)
-
-
-def finish_rest_body(chips, outs, early, late, slab_ref, own_ref, peer_ref, late_own_ref, late_peer_ref, *out_refs):
-    stacks = [(own_ref, peer_ref, early), (late_own_ref, late_peer_ref, late)]
+def begin_body(chips, outs, early, slab_ref, own_ref, peer_ref, acc_ref):
     for k in range(0, len(outs), 2):
-        re, im = source_products(chips, slab_ref, stacks, outs[k : k + 2])
+        re, im = source_products(chips, slab_ref, [(own_ref, peer_ref, early)], outs[k : k + 2])
         for h in range(2):
-            out_refs[k + h][:, :256] = re[128 * h : 128 * h + 128].astype(BF16)
-            out_refs[k + h][:, 256:] = im[128 * h : 128 * h + 128].astype(BF16)
+            acc_ref[k + h, :, :256] = re[128 * h : 128 * h + 128]
+            acc_ref[k + h, :, 256:] = im[128 * h : 128 * h + 128]
+
+
+def finish_body(chips, outs, late, slab_ref, own_ref, peer_ref, acc_ref, *out_refs):
+    for k in range(0, len(outs), 2):
+        re, im = source_products(chips, slab_ref, [(own_ref, peer_ref, late)], outs[k : k + 2])
+        for h in range(2):
+            out_refs[k + h][:, :256] = (acc_ref[k + h, :, :256] + re[128 * h : 128 * h + 128]).astype(BF16)
+            out_refs[k + h][:, 256:] = (acc_ref[k + h, :, 256:] + im[128 * h : 128 * h + 128]).astype(BF16)
 
 
 def fit_pieces_body(data_ref, *refs):
@@ -315,8 +309,18 @@
         sums_ref[k] = acc[k]
 
 
+def deliver_body(*refs):
+    piece_refs, mult_ref = refs[:-1], refs[-1]
+    bm = mult_ref.shape[2]
+    rows = pl.ds(pl.multiple_of(pl.program_id(0) * bm, bm), bm)
+    for offset, ref in enumerate(piece_refs):
+        at = aligned(256 * chip_at(len(piece_refs), offset, home=True), 256)
+        mult_ref[0, 0, :, at] = ref[rows, :256]
+        mult_ref[0, 1, :, at] = ref[rows, 256:]
+
+
 def subtract_pieces_body(chips, data_ref, *refs):
-    piece_refs, sums_refs, (out_ref, mult_ref) = refs[:chips], refs[chips:-2], refs[-2:]
+    piece_refs, sums_refs, out_ref = refs[:chips], refs[chips:-1], refs[-1]
     bm = out_ref.shape[2]
     sums = sums_refs[0][...]
     for ref in sums_refs[1:]:
@@ -327,8 +331,6 @@
     rows = pl.ds(pl.multiple_of(pl.program_id(0) * bm, bm), bm)
     for offset, ref in enumerate(piece_refs):
         at = aligned(256 * chip_at(len(piece_refs), offset, home=True), 256)
-        mult_ref[0, 0, :, at] = ref[rows, :256]
-        mult_ref[0, 1, :, at] = ref[rows, 256:]
         mr, mi = ref[rows, :256].astype(F32), ref[rows, 256:].astype(F32)
         out_ref[0, 0, :, at] = data_ref[0, 0, rows, at] - (fit_re * mr - fit_im * mi)
         out_ref[0, 1, :, at] = data_ref[0, 1, rows, at] - (fit_re * mi + fit_im * mr)
@@ -338,7 +340,7 @@
     rows, width = recorded.shape[2], recorded.shape[3]
     panels = lax.axis_size("panel")
     chips = panels // 2
-    own = chips - 1
+    half, own = chips // 2, chips - 1
     first, rest = (0, 1), (own, *range(2, own))
     early, late = (own, *range(chips // 2 - 1)), tuple(range(chips // 2 - 1, own))
     sources = rows * panels
@@ -363,7 +365,7 @@
         mine = pl.pallas_call(
             stack_body,
             in_specs=[resident] * len(pieces),
-            out_shape=pltpu.VMEM((len(pieces), rows, 512), BF16),
+            out_shape=pltpu.VMEM((half, rows, 512), BF16),
             compiler_params=small(),
         )(*pieces)
         return mine, lax.ppermute(mine, "panel", [(k, k ^ 1) for k in range(panels)])
@@ -401,30 +403,26 @@
         name="slab_source",
     )(source_kernel)
 
-    acc_first = pl.pallas_call(
-        functools.partial(begin_first_body, chips, first, early),
-        in_specs=[resident] * 3,
-        out_shape=pltpu.VMEM((len(first), rows, 512), F32),
-        compiler_params=medium(),
-        name="begin_first",
-    )(slab_s, early_own, early_peer)
-    late_own, late_peer = swap([got[o] for o in late])
-    pieces = pl.pallas_call(
-        functools.partial(finish_first_body, chips, first, late),
-        in_specs=[resident] * 4,
-        out_shape=[piece] * len(first),
-        compiler_params=medium(),
-        name="finish_first",
-    )(slab_s, late_own, late_peer, acc_first)
-    home = exchange(pieces, first, "home")
-    pieces = pl.pallas_call(
-        functools.partial(finish_rest_body, chips, rest, early, late),
-        in_specs=[resident] * 5,
-        out_shape=[piece] * len(rest),
-        compiler_params=medium(),
-        name="finish_rest",
-    )(slab_s, early_own, early_peer, late_own, late_peer)
-    home |= exchange(pieces, rest, "home")
+    def begin(outs):
+        return pl.pallas_call(
+            functools.partial(begin_body, chips, outs, early),
+            in_specs=[resident] * 3,
+            out_shape=pltpu.VMEM((len(outs), rows, 512), F32),
+            compiler_params=medium(),
+        )(slab_s, early_own, early_peer)
+
+    def finish(outs, acc):
+        return pl.pallas_call(
+            functools.partial(finish_body, chips, outs, late),
+            in_specs=[resident] * 4,
+            out_shape=[piece] * len(outs),
+            compiler_params=medium(),
+        )(slab_s, late_own, late_peer, acc)
+
+    acc_first, acc_rest = begin(first), begin(rest)
+    late_own, late_peer = swap([acc_rest] + [got[o] for o in late])
+    home = exchange(finish(first, acc_first), first, "home")
+    home |= exchange(finish(rest, acc_rest), rest, "home")
     back = [home[o] for o in range(chips)]
 
     sums = pl.pallas_call(
@@ -435,17 +433,27 @@
         name="fit",
     )(recorded, *back)
     terms = partials(sums, "panel")
-    bm = 32
+    bm = 64
     block = pl.BlockSpec((1, 2, bm, width), lambda i: (0, 0, i, 0))
-    return pl.pallas_call(
+    mult = pl.pallas_call(
+        deliver_body,
+        grid=(rows // bm,),
+        in_specs=[resident] * chips,
+        out_specs=block,
+        out_shape=shape((1, 2, rows, width), BF16),
+        compiler_params=small(),
+        name="deliver",
+    )(*back)
+    prim = pl.pallas_call(
         functools.partial(subtract_pieces_body, chips),
         grid=(rows // bm,),
         in_specs=[resident] * (1 + chips) + [pl.BlockSpec((3, 8, 128), lambda i: (0, 0, 0))] * len(terms),
-        out_specs=[block, block],
-        out_shape=[shape((1, 2, rows, width), F32), shape((1, 2, rows, width), BF16)],
+        out_specs=block,
+        out_shape=shape((1, 2, rows, width), F32),
         compiler_params=small(),
         name="subtract",
     )(recorded, *back, *terms)
+    return prim, mult
 
 
 def overlapping(panels):

time: 85.1 us -> 81.4 us (0.957)
  waiting for transfers between devices: 27.7 us -> 21.2 us
  starting transfers between devices: 40.8 us -> 43.2 us
    ppermute x2, starting transfers between devices: 0.14 us -> 3.79 us  [swap(): lax.ppermute(mine, 'panel', [(k, k ^ 1) for k in range(panels)])]
    ppermute x6, waiting for transfers between devices: 6.34 us -> 2.72 us  [partials(): lax.ppermute(x, axis, [(k, k ^ span * d) for k in range(n)])]
    ppermute x14, waiting for transfers between devices: 20.2 us -> 17 us  [exchange(): x = lax.ppermute(x, 'panel', pairs)]
    ppermute x14, starting transfers between devices: 34.3 us -> 33 us  [exchange(): x = lax.ppermute(x, 'panel', pairs)]
    pallas_call x3 -> x5, Pallas kernels: 4.99 us -> 6.2 us  [the longest x2 2.59 us: finish(): pl.pallas_call(functools.partial(finish_body, chips, outs, late), in_spec...]
  transfers between devices with their start and end apart: 22 -> 22, of which waited for: 10 -> 13; matrix products, arithmetic and copies ran while one was open for 0% -> 0% of each run, Pallas kernels for 3% -> 6%
where the time goes in v5:
time: 81.4 us; the launch traced here: 81.1 us
  starting transfers between devices  43.2 us (53%)
  waiting for transfers between devices  21.2 us (26%)
  Pallas kernels  15.9 us (20%)
    ppermute x14, starting transfers between devices, exchange(): x = lax.ppermute(x, 'panel', pairs)  33 us
    ppermute x14, waiting for transfers between devices, exchange(): x = lax.ppermute(x, 'panel', pairs)  17 us
    ppermute x6, starting transfers between devices, partials(): lax.ppermute(x, axis, [(k, k ^ span * d) for k in range(n)])  6.37 us
    ppermute x2, starting transfers between devices, swap(): lax.ppermute(mine, 'panel', [(k, k ^ 1) for k in range(panels)])  3.79 us
    pallas_call x1, Pallas kernels, piped(): pl.pallas_call(functools.partial(focus_rest_body, chips, rest), in_specs=...  3.57 us
    pallas_call x1, Pallas kernels, piped(): pl.pallas_call(functools.partial(focus_first_body, chips, first), in_spec...  2.98 us
    ppermute x6, waiting for transfers between devices, partials(): lax.ppermute(x, axis, [(k, k ^ span * d) for k in range(n)])  2.72 us
    pallas_call x2, Pallas kernels, finish(): pl.pallas_call(functools.partial(finish_body, chips, outs, late), in_spec...  2.59 us
  transfers between devices with their start and end apart: 22, of which 13 were waited for; matrix products, arithmetic and copies ran while one was open for 0% of the time, Pallas kernels for 6%

profile of v5, /device:TPU:0, one launch (start us, length us, event | category | flops | bytes accessed | tf_op | source)
XLA Modules:
  0.0 81.1 jit_solution(13822378940905593909)
XLA Ops:
  0.6 3.0 %focus_first.1 = (bf16[128,512]{1,0:T(8,128)(2,1)S(1)}, bf16[128,512]{1,0:T(8,128)(2,1)S(1)}, bf16[2,128,4096]{2,1,0:T(8,128)(2,1)S(1)}, bf16[256,2048]{1,0:T(8,128)(2,1)S(1)}) custom-call(f32[1,2,128,2048]{3,2,1,0:T(8,128)} %data_ref.3, bf16[1,2,4095]{2,1,0:T(2,128)(2,1)} %kernel_hbm.1), custom_call_target="tpu_custom_call" | custom-call | tf_op jit(solution)/shard_map/focus_first/pallas_call | solution.py:373
  3.6 0.0 copy-start.1
  3.6 3.6 %focus_rest.1 = (bf16[128,512]{1,0:T(8,128)(2,1)S(1)}, bf16[128,512]{1,0:T(8,128)(2,1)S(1)}, bf16[128,512]{1,0:T(8,128)(2,1)S(1)}, bf16[128,512]{1,0:T(8,128)(2,...) custom-call(bf16[2,128,4096]{2,1,0:T(8,128)(2,1)S(1)} %get-tuple-element.20.slab_ref, ...), custom_call_target="tpu_custom_call" | custom-call | tf_op jit(solution)/shard_map/focus_rest/pallas_call | solution.py:388
  7.2 3.0 %collective-permute-start.2 = (bf16[128,512]{1,0:T(8,128)(2,1)S(1)}, bf16[128,512]{1,0:T(8,128)(2,1)S(1)}, u32[]{:S(2)}, u32[]{:S(2)}) collective-permute-start(bf16[128,512]{1,0:T(8,128)(2,1)S(1)} %get-tuple-element.25), channel_id=1, source_target_pairs={{0,2},{1,13},{2,0},{3,15},{4,6},{5,9},{6,4},{7,11},{8,10},{9,5},{1... | collective-permute-start | bytes 393224 | tf_op jit(solution)/shard_map/ppermute | solution.py:360
  10.2 1.6 %collective-permute-start = (bf16[128,512]{1,0:T(8,128)(2,1)S(1)}, bf16[128,512]{1,0:T(8,128)(2,1)S(1)}, u32[]{:S(2)}, u32[]{:S(2)}) collective-permute-start(bf16[128,512]{1,0:T(8,128)(2,1)S(1)} %get-tuple-element.23), channel_id=1, source_target_pairs={{0,4},{1,9},{2,6},{3,11},{4,0},{5,13},{6,2},{7,15},{8,12},{9,1},{1... | collective-permute-start | bytes 393224 | tf_op jit(solution)/shard_map/ppermute | solution.py:360
  11.8 1.4 %collective-permute-done.2.refs_3_ = bf16[128,512]{1,0:T(8,128)(2,1)S(1)} collective-permute-done((bf16[128,512]{1,0:T(8,128)(2,1)S(1)}, bf16[128,512]{1,0:T(8,128)(2,1)S(1)}, u32[]{:S(2)}, u32[]{:S(2)}) %collective-permute-start.2) | collective-permute-done | bytes 131104 | tf_op jit(solution)/shard_map/ppermute | solution.py:360
  13.2 2.7 %collective-permute-done.refs_1_ = bf16[128,512]{1,0:T(8,128)(2,1)S(1)} collective-permute-done((bf16[128,512]{1,0:T(8,128)(2,1)S(1)}, bf16[128,512]{1,0:T(8,128)(2,1)S(1)}, u32[]{:S(2)}, u32[]{:S(2)}) %collective-permute-start) | collective-permute-done | bytes 131104 | tf_op jit(solution)/shard_map/ppermute | solution.py:360
  15.9 2.7 %collective-permute-done.1.refs_2_ = bf16[128,512]{1,0:T(8,128)(2,1)S(1)} collective-permute-done((bf16[128,512]{1,0:T(8,128)(2,1)S(1)}, bf16[128,512]{1,0:T(8,128)(2,1)S(1)}, u32[]{:S(2)}, u32[]{:S(2)}) %collective-permute-start.1) | collective-permute-done | bytes 131104 | tf_op jit(solution)/shard_map/ppermute | solution.py:360
  18.6 2.9 %collective-permute-start.3 = (bf16[4,128,512]{2,1,0:T(8,128)(2,1)S(1)}, bf16[4,128,512]{2,1,0:T(8,128)(2,1)S(1)}, u32[]{:S(2)}, u32[]{:S(2)}) collective-permute-start(bf16[4,128,512]{2,1,0:T(8,128)(2,1)S(1)} %shard_map.50.own_ref), channel_id=1, source_target_pairs={{0,1},{1,0},{2,3},{3,2},{4,5},{5,4},{6,7},{7,6},{8,9},{9,8},{10,11... | collective-permute-start | bytes 1572872 | tf_op jit(solution)/shard_map/ppermute | solution.py:371
  21.5 1.7 %collective-permute-start.4 = (bf16[128,512]{1,0:T(8,128)(2,1)S(1)}, bf16[128,512]{1,0:T(8,128)(2,1)S(1)}, u32[]{:S(2)}, u32[]{:S(2)}) collective-permute-start(bf16[128,512]{1,0:T(8,128)(2,1)S(1)} %get-tuple-element.26), channel_id=1, source_target_pairs={{0,8},{1,15},{2,10},{3,13},{4,12},{5,11},{6,14},{7,9},{8,0},{9,7},... | collective-permute-start | bytes 393224 | tf_op jit(solution)/shard_map/ppermute | solution.py:360
  23.2 1.2 %collective-permute-start.5 = (bf16[128,512]{1,0:T(8,128)(2,1)S(1)}, bf16[128,512]{1,0:T(8,128)(2,1)S(1)}, u32[]{:S(2)}, u32[]{:S(2)}) collective-permute-start(bf16[128,512]{1,0:T(8,128)(2,1)S(1)} %get-tuple-element.27), channel_id=1, source_target_pairs={{0,10},{1,5},{2,8},{3,7},{4,14},{5,1},{6,12},{7,3},{8,2},{9,13},{1... | collective-permute-start | bytes 393224 | tf_op jit(solution)/shard_map/ppermute | solution.py:360
  24.3 2.7 %collective-permute-start.6 = (bf16[128,512]{1,0:T(8,128)(2,1)S(1)}, bf16[128,512]{1,0:T(8,128)(2,1)S(1)}, u32[]{:S(2)}, u32[]{:S(2)}) collective-permute-start(bf16[128,512]{1,0:T(8,128)(2,1)S(1)} %get-tuple-element.28), channel_id=1, source_target_pairs={{0,12},{1,7},{2,14},{3,5},{4,8},{5,3},{6,10},{7,1},{8,4},{9,15},{1... | collective-permute-start | bytes 393224 | tf_op jit(solution)/shard_map/ppermute | solution.py:360
  27.1 2.1 %collective-permute-start.7 = (bf16[128,512]{1,0:T(8,128)(2,1)S(1)}, bf16[128,512]{1,0:T(8,128)(2,1)S(1)}, u32[]{:S(2)}, u32[]{:S(2)}) collective-permute-start(bf16[128,512]{1,0:T(8,128)(2,1)S(1)} %get-tuple-element.29), channel_id=1, source_target_pairs={{0,14},{1,3},{2,12},{3,1},{4,10},{5,7},{6,8},{7,5},{8,6},{9,11},{1... | collective-permute-start | bytes 393224 | tf_op jit(solution)/shard_map/ppermute | solution.py:360
  29.1 0.7 slab_source.1.slab_ref
  29.9 1.9 %shard_map.51.refs_0_.acc_ref = f32[6,128,512]{2,1,0:T(8,128)S(1)} custom-call(bf16[2,128,4096]{2,1,0:T(8,128)(2,1)S(1)} %slab_source.1.slab_ref, bf16[4,128,512]{2,1,0:T(8,128)(2,1)S(1)} %shard_map.50.own_ref, bf16[4,128,512]{2,1,0:T(8,128)(2,1)S(1)} %collective-permute-done.3.peer_ref), custom_call_target="tpu_custom_call" | custom-call | tf_op jit(solution)/shard_map/pallas_call | solution.py:407
  31.8 0.0 collective-permute-done.4.refs_1_
  31.8 1.7 %collective-permute-done.5.refs_2_ = bf16[128,512]{1,0:T(8,128)(2,1)S(1)} collective-permute-done((bf16[128,512]{1,0:T(8,128)(2,1)S(1)}, bf16[128,512]{1,0:T(8,128)(2,1)S(1)}, u32[]{:S(2)}, u32[]{:S(2)}) %collective-permute-start.5) | collective-permute-done | bytes 131104 | tf_op jit(solution)/shard_map/ppermute | solution.py:360
  33.5 0.7 collective-permute-done.6.refs_3_
  34.2 1.8 %collective-permute-done.7.refs_4_ = bf16[128,512]{1,0:T(8,128)(2,1)S(1)} collective-permute-done((bf16[128,512]{1,0:T(8,128)(2,1)S(1)}, bf16[128,512]{1,0:T(8,128)(2,1)S(1)}, u32[]{:S(2)}, u32[]{:S(2)}) %collective-permute-start.7) | collective-permute-done | bytes 131104 | tf_op jit(solution)/shard_map/ppermute | solution.py:360
  36.0 0.9 %collective-permute-start.8 = (bf16[4,128,512]{2,1,0:T(8,128)(2,1)S(1)}, bf16[4,128,512]{2,1,0:T(8,128)(2,1)S(1)}, u32[]{:S(2)}, u32[]{:S(2)}) collective-permute-start(bf16[4,128,512]{2,1,0:T(8,128)(2,1)S(1)} %shard_map.52.own_ref), channel_id=1, source_target_pairs={{0,1},{1,0},{2,3},{3,2},{4,5},{5,4},{6,7},{7,6},{8,9},{9,8},{10,11... | collective-permute-start | bytes 1572872 | tf_op jit(solution)/shard_map/ppermute | solution.py:371
  37.0 1.5 %collective-permute-done.8.peer_ref = bf16[4,128,512]{2,1,0:T(8,128)(2,1)S(1)} collective-permute-done((bf16[4,128,512]{2,1,0:T(8,128)(2,1)S(1)}, bf16[4,128,512]{2,1,0:T(8,128)(2,1)S(1)}, u32[]{:S(2)}, u32[]{:S(2)}) %collective-permute-start.8) | collective-permute-done | bytes 524320 | tf_op jit(solution)/shard_map/ppermute | solution.py:371
  38.5 1.9 %shard_map.55 = (bf16[128,512]{1,0:T(8,128)(2,1)S(1)}, bf16[128,512]{1,0:T(8,128)(2,1)S(1)}, bf16[128,512]{1,0:T(8,128)(2,1)S(1)}, bf16[128,512]{1,0:T(8,128)(2,...) custom-call(bf16[2,128,4096]{2,1,0:T(8,128)(2,1)S(1)} %slab_source.1.slab_ref, ...), custom_call_target="tpu_custom_call" | custom-call | tf_op jit(solution)/shard_map/pallas_call | solution.py:415
  40.4 2.5 %collective-permute-start.11 = (bf16[128,512]{1,0:T(8,128)(2,1)S(1)}, bf16[128,512]{1,0:T(8,128)(2,1)S(1)}, u32[]{:S(2)}, u32[]{:S(2)}) collective-permute-start(bf16[128,512]{1,0:T(8,128)(2,1)S(1)} %get-tuple-element.32), channel_id=1, source_target_pairs={{0,12},{1,3},{2,14},{3,1},{4,8},{5,7},{6,10},{7,5},{8,4},{9,11},{1... | collective-permute-start | bytes 393224 | tf_op jit(solution)/shard_map/ppermute | solution.py:360
  42.8 1.6 %collective-permute-start.12 = (bf16[128,512]{1,0:T(8,128)(2,1)S(1)}, bf16[128,512]{1,0:T(8,128)(2,1)S(1)}, u32[]{:S(2)}, u32[]{:S(2)}) collective-permute-start(bf16[128,512]{1,0:T(8,128)(2,1)S(1)} %get-tuple-element.33), channel_id=1, source_target_pairs={{0,14},{1,9},{2,12},{3,11},{4,10},{5,13},{6,8},{7,15},{8,6},{9,1},... | collective-permute-start | bytes 393224 | tf_op jit(solution)/shard_map/ppermute | solution.py:360
  44.5 0.7 shard_map.53.acc_ref
  45.2 0.0 copy-start
  45.2 1.6 %collective-permute-start.13 = (bf16[128,512]{1,0:T(8,128)(2,1)S(1)}, bf16[128,512]{1,0:T(8,128)(2,1)S(1)}, u32[]{:S(2)}, u32[]{:S(2)}) collective-permute-start(bf16[128,512]{1,0:T(8,128)(2,1)S(1)} %get-tuple-element.34), channel_id=1, source_target_pairs={{0,4},{1,11},{2,6},{3,9},{4,0},{5,15},{6,2},{7,13},{8,12},{9,3},{1... | collective-permute-start | bytes 393224 | tf_op jit(solution)/shard_map/ppermute | solution.py:360
  46.9 1.1 %collective-permute-start.14 = (bf16[128,512]{1,0:T(8,128)(2,1)S(1)}, bf16[128,512]{1,0:T(8,128)(2,1)S(1)}, u32[]{:S(2)}, u32[]{:S(2)}) collective-permute-start(bf16[128,512]{1,0:T(8,128)(2,1)S(1)} %get-tuple-element.35), channel_id=1, source_target_pairs={{0,6},{1,13},{2,4},{3,15},{4,2},{5,9},{6,0},{7,11},{8,14},{9,5},{1... | collective-permute-start | bytes 393224 | tf_op jit(solution)/shard_map/ppermute | solution.py:360
  48.0 0.8 collective-permute-start.15
  48.8 0.7 shard_map.54
  49.5 7.5 %collective-permute-start.9 = (bf16[128,512]{1,0:T(8,128)(2,1)S(1)}, bf16[128,512]{1,0:T(8,128)(2,1)S(1)}, u32[]{:S(2)}, u32[]{:S(2)}) collective-permute-start(bf16[128,512]{1,0:T(8,128)(2,1)S(1)} %get-tuple-element.30), channel_id=1, source_target_pairs={{0,8},{1,5},{2,10},{3,7},{4,12},{5,1},{6,14},{7,3},{8,0},{9,13},{1... | collective-permute-start | bytes 393224 | tf_op jit(solution)/shard_map/ppermute | solution.py:360
  57.0 5.6 %collective-permute-start.10 = (bf16[128,512]{1,0:T(8,128)(2,1)S(1)}, bf16[128,512]{1,0:T(8,128)(2,1)S(1)}, u32[]{:S(2)}, u32[]{:S(2)}) collective-permute-start(bf16[128,512]{1,0:T(8,128)(2,1)S(1)} %get-tuple-element.31), channel_id=1, source_target_pairs={{0,10},{1,7},{2,8},{3,5},{4,14},{5,3},{6,12},{7,1},{8,2},{9,15},{1... | collective-permute-start | bytes 393224 | tf_op jit(solution)/shard_map/ppermute | solution.py:360
  62.6 0.0 collective-permute-done.13.refs_4_
  62.6 0.0 collective-permute-done.14.refs_5_
  62.6 1.4 %collective-permute-done.9.refs_0_ = bf16[128,512]{1,0:T(8,128)(2,1)S(1)} collective-permute-done((bf16[128,512]{1,0:T(8,128)(2,1)S(1)}, bf16[128,512]{1,0:T(8,128)(2,1)S(1)}, u32[]{:S(2)}, u32[]{:S(2)}) %collective-permute-start.9) | collective-permute-done | bytes 131104 | tf_op jit(solution)/shard_map/ppermute | solution.py:360
  64.0 4.6 %collective-permute-done.10.refs_1_ = bf16[128,512]{1,0:T(8,128)(2,1)S(1)} collective-permute-done((bf16[128,512]{1,0:T(8,128)(2,1)S(1)}, bf16[128,512]{1,0:T(8,128)(2,1)S(1)}, u32[]{:S(2)}, u32[]{:S(2)}) %collective-permute-start.10) | collective-permute-done | bytes 131104 | tf_op jit(solution)/shard_map/ppermute | solution.py:360
  68.6 0.7 fit.1
  69.3 1.7 %collective-permute-start.18 = (f32[3,8,128]{2,1,0:T(8,128)S(1)}, f32[3,8,128]{2,1,0:T(8,128)S(1)}, u32[]{:S(2)}, u32[]{:S(2)}) collective-permute-start(f32[3,8,128]{2,1,0:T(8,128)S(1)} %fit.1), channel_id=1, source_target_pairs={{0,12},{1,13},{2,14},{3,15},{4,8},{5,9},{6,10},{7,11},{8,4},{9,5},... | collective-permute-start | bytes 36872 | tf_op jit(solution)/shard_map/ppermute | solution.py:134
  71.0 2.8 %collective-permute-start.16 = (f32[3,8,128]{2,1,0:T(8,128)S(1)}, f32[3,8,128]{2,1,0:T(8,128)S(1)}, u32[]{:S(2)}, u32[]{:S(2)}) collective-permute-start(f32[3,8,128]{2,1,0:T(8,128)S(1)} %fit.1), channel_id=1, source_target_pairs={{0,4},{1,5},{2,6},{3,7},{4,0},{5,1},{6,2},{7,3},{8,12},{9,13},{10,... | collective-permute-start | bytes 36872 | tf_op jit(solution)/shard_map/ppermute | solution.py:134
  73.8 1.1 %collective-permute-done.18 = f32[3,8,128]{2,1,0:T(8,128)S(1)} collective-permute-done((f32[3,8,128]{2,1,0:T(8,128)S(1)}, f32[3,8,128]{2,1,0:T(8,128)S(1)}, u32[]{:S(2)}, u32[]{:S(2)}) %collective-permute-start.18) | collective-permute-done | bytes 12320 | tf_op jit(solution)/shard_map/ppermute | solution.py:134
  74.9 0.7 collective-permute-done.17
  75.6 0.1 collective-permute-start.21
  75.7 1.5 %collective-permute-start.20 = (f32[3,8,128]{2,1,0:T(8,128)S(1)}, f32[3,8,128]{2,1,0:T(8,128)S(1)}, u32[]{:S(2)}, u32[]{:S(2)}) collective-permute-start(f32[3,8,128]{2,1,0:T(8,128)S(1)} %add_add_fusion.refs_8_), channel_id=1, source_target_pairs={{0,2},{1,3},{2,0},{3,1},{4,6},{5,7},{6,4},{7,5},{8,10},{9,11},{10,... | collective-permute-start | bytes 36872 | tf_op jit(solution)/shard_map/ppermute | solution.py:134
  77.3 0.3 collective-permute-start.19
  77.6 1.0 %deliver.1 = bf16[1,2,128,2048]{3,2,1,0:T(8,128)(2,1)} custom-call(bf16[128,512]{1,0:T(8,128)(2,1)S(1)} %collective-permute-done.9.refs_0_, bf16[128,512]{1,0:T(8,128)(2,1)S(1)} %collective-permute-done.10.refs_1_, bf16[128,512]{1,0:T(8,128)(2,1)S(1)} %collective-permute-done.11.refs_2_, bf16[128,512]{1,0:T(8,128)(2,1)S(1)} %collective-permute-done.12.refs_3_, ...), custom_call_target="tpu_custom_call" | custom-call | tf_op jit(solution)/shard_map/deliver/pallas_call | solution.py:438
  78.6 0.3 collective-permute-done.21.refs_11_
  78.9 0.5 collective-permute-done.20.refs_10_
  79.5 1.7 %subtract.1 = f32[1,2,128,2048]{3,2,1,0:T(8,128)} custom-call(f32[1,2,128,2048]{3,2,1,0:T(8,128)S(1)} %copy-done, bf16[128,512]{1,0:T(8,128)(2,1)S(1)} %collective-permute-done.9.refs_0_, bf16[128,512]{1,0:T(8,128)(2,1)S(1)} %collective-permute-done.10.refs_1_, bf16[128,512]{1,0:T(8,128)(2,1)S(1)} %collective-permute-done.11.refs_2_, ...), custom_call_target="tpu_custom_call" | custom-call | tf_op jit(solution)/shard_map/subtract/pallas_call | solution.py:447
  (13 shorter events, 0.1 us)
Async XLA Ops:
  3.6 25.5 %copy-start.1 = (bf16[1,2,4095]{2,1,0:T(2,128)(2,1)S(1)}, bf16[1,2,4095]{2,1,0:T(2,128)(2,1)}, u32[]{:S(2)}) copy-start(bf16[1,2,4095]{2,1,0:T(2,128)(2,1)} %kernel_ref.1) | copy-start | bytes 49144
  7.2 6.0 %collective-permute-start.2 = (bf16[128,512]{1,0:T(8,128)(2,1)S(1)}, bf16[128,512]{1,0:T(8,128)(2,1)S(1)}, u32[]{:S(2)}, u32[]{:S(2)}) collective-permute-start(bf16[128,512]{1,0:T(8,128)(2,1)S(1)} %get-tuple-element.25), channel_id=1, source_target_pairs={{0,2},{1,13},{2,0},{3,15},{4,6},{5,9},{6,4},{7,11},{8,10},{9,5},{1... | collective-permute-start | bytes 393224 | tf_op jit(solution)/shard_map/ppermute | solution.py:360
  10.2 5.7 %collective-permute-start = (bf16[128,512]{1,0:T(8,128)(2,1)S(1)}, bf16[128,512]{1,0:T(8,128)(2,1)S(1)}, u32[]{:S(2)}, u32[]{:S(2)}) collective-permute-start(bf16[128,512]{1,0:T(8,128)(2,1)S(1)} %get-tuple-element.23), channel_id=1, source_target_pairs={{0,4},{1,9},{2,6},{3,11},{4,0},{5,13},{6,2},{7,15},{8,12},{9,1},{1... | collective-permute-start | bytes 393224 | tf_op jit(solution)/shard_map/ppermute | solution.py:360
  11.8 6.8 %collective-permute-start.1 = (bf16[128,512]{1,0:T(8,128)(2,1)S(1)}, bf16[128,512]{1,0:T(8,128)(2,1)S(1)}, u32[]{:S(2)}, u32[]{:S(2)}) collective-permute-start(bf16[128,512]{1,0:T(8,128)(2,1)S(1)} %get-tuple-element.24), channel_id=1, source_target_pairs={{0,6},{1,11},{2,4},{3,9},{4,2},{5,15},{6,0},{7,13},{8,14},{9,3},{1... | collective-permute-start | bytes 393224 | tf_op jit(solution)/shard_map/ppermute | solution.py:360
  18.6 11.2 %collective-permute-start.3 = (bf16[4,128,512]{2,1,0:T(8,128)(2,1)S(1)}, bf16[4,128,512]{2,1,0:T(8,128)(2,1)S(1)}, u32[]{:S(2)}, u32[]{:S(2)}) collective-permute-start(bf16[4,128,512]{2,1,0:T(8,128)(2,1)S(1)} %shard_map.50.own_ref), channel_id=1, source_target_pairs={{0,1},{1,0},{2,3},{3,2},{4,5},{5,4},{6,7},{7,6},{8,9},{9,8},{10,11... | collective-permute-start | bytes 1572872 | tf_op jit(solution)/shard_map/ppermute | solution.py:371
  21.5 10.3 %collective-permute-start.4 = (bf16[128,512]{1,0:T(8,128)(2,1)S(1)}, bf16[128,512]{1,0:T(8,128)(2,1)S(1)}, u32[]{:S(2)}, u32[]{:S(2)}) collective-permute-start(bf16[128,512]{1,0:T(8,128)(2,1)S(1)} %get-tuple-element.26), channel_id=1, source_target_pairs={{0,8},{1,15},{2,10},{3,13},{4,12},{5,11},{6,14},{7,9},{8,0},{9,7},... | collective-permute-start | bytes 393224 | tf_op jit(solution)/shard_map/ppermute | solution.py:360
  23.2 10.3 %collective-permute-start.5 = (bf16[128,512]{1,0:T(8,128)(2,1)S(1)}, bf16[128,512]{1,0:T(8,128)(2,1)S(1)}, u32[]{:S(2)}, u32[]{:S(2)}) collective-permute-start(bf16[128,512]{1,0:T(8,128)(2,1)S(1)} %get-tuple-element.27), channel_id=1, source_target_pairs={{0,10},{1,5},{2,8},{3,7},{4,14},{5,1},{6,12},{7,3},{8,2},{9,13},{1... | collective-permute-start | bytes 393224 | tf_op jit(solution)/shard_map/ppermute | solution.py:360
  24.3 9.9 %collective-permute-start.6 = (bf16[128,512]{1,0:T(8,128)(2,1)S(1)}, bf16[128,512]{1,0:T(8,128)(2,1)S(1)}, u32[]{:S(2)}, u32[]{:S(2)}) collective-permute-start(bf16[128,512]{1,0:T(8,128)(2,1)S(1)} %get-tuple-element.28), channel_id=1, source_target_pairs={{0,12},{1,7},{2,14},{3,5},{4,8},{5,3},{6,10},{7,1},{8,4},{9,15},{1... | collective-permute-start | bytes 393224 | tf_op jit(solution)/shard_map/ppermute | solution.py:360
  27.1 8.9 %collective-permute-start.7 = (bf16[128,512]{1,0:T(8,128)(2,1)S(1)}, bf16[128,512]{1,0:T(8,128)(2,1)S(1)}, u32[]{:S(2)}, u32[]{:S(2)}) collective-permute-start(bf16[128,512]{1,0:T(8,128)(2,1)S(1)} %get-tuple-element.29), channel_id=1, source_target_pairs={{0,14},{1,3},{2,12},{3,1},{4,10},{5,7},{6,8},{7,5},{8,6},{9,11},{1... | collective-permute-start | bytes 393224 | tf_op jit(solution)/shard_map/ppermute | solution.py:360
  36.0 2.5 %collective-permute-start.8 = (bf16[4,128,512]{2,1,0:T(8,128)(2,1)S(1)}, bf16[4,128,512]{2,1,0:T(8,128)(2,1)S(1)}, u32[]{:S(2)}, u32[]{:S(2)}) collective-permute-start(bf16[4,128,512]{2,1,0:T(8,128)(2,1)S(1)} %shard_map.52.own_ref), channel_id=1, source_target_pairs={{0,1},{1,0},{2,3},{3,2},{4,5},{5,4},{6,7},{7,6},{8,9},{9,8},{10,11... | collective-permute-start | bytes 1572872 | tf_op jit(solution)/shard_map/ppermute | solution.py:371
  40.4 9.1 %collective-permute-start.11 = (bf16[128,512]{1,0:T(8,128)(2,1)S(1)}, bf16[128,512]{1,0:T(8,128)(2,1)S(1)}, u32[]{:S(2)}, u32[]{:S(2)}) collective-permute-start(bf16[128,512]{1,0:T(8,128)(2,1)S(1)} %get-tuple-element.32), channel_id=1, source_target_pairs={{0,12},{1,3},{2,14},{3,1},{4,8},{5,7},{6,10},{7,5},{8,4},{9,11},{1... | collective-permute-start | bytes 393224 | tf_op jit(solution)/shard_map/ppermute | solution.py:360
  42.8 14.2 %collective-permute-start.12 = (bf16[128,512]{1,0:T(8,128)(2,1)S(1)}, bf16[128,512]{1,0:T(8,128)(2,1)S(1)}, u32[]{:S(2)}, u32[]{:S(2)}) collective-permute-start(bf16[128,512]{1,0:T(8,128)(2,1)S(1)} %get-tuple-element.33), channel_id=1, source_target_pairs={{0,14},{1,9},{2,12},{3,11},{4,10},{5,13},{6,8},{7,15},{8,6},{9,1},... | collective-permute-start | bytes 393224 | tf_op jit(solution)/shard_map/ppermute | solution.py:360
  45.2 23.4 %copy-start = (f32[1,2,128,2048]{3,2,1,0:T(8,128)S(1)}, f32[1,2,128,2048]{3,2,1,0:T(8,128)}, u32[]{:S(2)}) copy-start(f32[1,2,128,2048]{3,2,1,0:T(8,128)} %data_ref.3) | copy-start | bytes 6291460
  45.2 17.4 %collective-permute-start.13 = (bf16[128,512]{1,0:T(8,128)(2,1)S(1)}, bf16[128,512]{1,0:T(8,128)(2,1)S(1)}, u32[]{:S(2)}, u32[]{:S(2)}) collective-permute-start(bf16[128,512]{1,0:T(8,128)(2,1)S(1)} %get-tuple-element.34), channel_id=1, source_target_pairs={{0,4},{1,11},{2,6},{3,9},{4,0},{5,15},{6,2},{7,13},{8,12},{9,3},{1... | collective-permute-start | bytes 393224 | tf_op jit(solution)/shard_map/ppermute | solution.py:360
  46.9 15.8 %collective-permute-start.14 = (bf16[128,512]{1,0:T(8,128)(2,1)S(1)}, bf16[128,512]{1,0:T(8,128)(2,1)S(1)}, u32[]{:S(2)}, u32[]{:S(2)}) collective-permute-start(bf16[128,512]{1,0:T(8,128)(2,1)S(1)} %get-tuple-element.35), channel_id=1, source_target_pairs={{0,6},{1,13},{2,4},{3,15},{4,2},{5,9},{6,0},{7,11},{8,14},{9,5},{1... | collective-permute-start | bytes 393224 | tf_op jit(solution)/shard_map/ppermute | solution.py:360
  48.0 14.6 %collective-permute-start.15 = (bf16[128,512]{1,0:T(8,128)(2,1)S(1)}, bf16[128,512]{1,0:T(8,128)(2,1)S(1)}, u32[]{:S(2)}, u32[]{:S(2)}) collective-permute-start(bf16[128,512]{1,0:T(8,128)(2,1)S(1)} %get-tuple-element.36), channel_id=1, source_target_pairs={{0,2},{1,15},{2,0},{3,13},{4,6},{5,11},{6,4},{7,9},{8,10},{9,7},{1... | collective-permute-start | bytes 393224 | tf_op jit(solution)/shard_map/ppermute | solution.py:360
  49.5 14.5 %collective-permute-start.9 = (bf16[128,512]{1,0:T(8,128)(2,1)S(1)}, bf16[128,512]{1,0:T(8,128)(2,1)S(1)}, u32[]{:S(2)}, u32[]{:S(2)}) collective-permute-start(bf16[128,512]{1,0:T(8,128)(2,1)S(1)} %get-tuple-element.30), channel_id=1, source_target_pairs={{0,8},{1,5},{2,10},{3,7},{4,12},{5,1},{6,14},{7,3},{8,0},{9,13},{1... | collective-permute-start | bytes 393224 | tf_op jit(solution)/shard_map/ppermute | solution.py:360
  57.0 11.6 %collective-permute-start.10 = (bf16[128,512]{1,0:T(8,128)(2,1)S(1)}, bf16[128,512]{1,0:T(8,128)(2,1)S(1)}, u32[]{:S(2)}, u32[]{:S(2)}) collective-permute-start(bf16[128,512]{1,0:T(8,128)(2,1)S(1)} %get-tuple-element.31), channel_id=1, source_target_pairs={{0,10},{1,7},{2,8},{3,5},{4,14},{5,3},{6,12},{7,1},{8,2},{9,15},{1... | collective-permute-start | bytes 393224 | tf_op jit(solution)/shard_map/ppermute | solution.py:360
  69.3 5.6 %collective-permute-start.18 = (f32[3,8,128]{2,1,0:T(8,128)S(1)}, f32[3,8,128]{2,1,0:T(8,128)S(1)}, u32[]{:S(2)}, u32[]{:S(2)}) collective-permute-start(f32[3,8,128]{2,1,0:T(8,128)S(1)} %fit.1), channel_id=1, source_target_pairs={{0,12},{1,13},{2,14},{3,15},{4,8},{5,9},{6,10},{7,11},{8,4},{9,5},... | collective-permute-start | bytes 36872 | tf_op jit(solution)/shard_map/ppermute | solution.py:134
  71.0 4.6 %collective-permute-start.17 = (f32[3,8,128]{2,1,0:T(8,128)S(1)}, f32[3,8,128]{2,1,0:T(8,128)S(1)}, u32[]{:S(2)}, u32[]{:S(2)}) collective-permute-start(f32[3,8,128]{2,1,0:T(8,128)S(1)} %fit.1), channel_id=1, source_target_pairs={{0,8},{1,9},{2,10},{3,11},{4,12},{5,13},{6,14},{7,15},{8,0},{9,1},... | collective-permute-start | bytes 36872 | tf_op jit(solution)/shard_map/ppermute | solution.py:134
  71.0 4.6 %collective-permute-start.16 = (f32[3,8,128]{2,1,0:T(8,128)S(1)}, f32[3,8,128]{2,1,0:T(8,128)S(1)}, u32[]{:S(2)}, u32[]{:S(2)}) collective-permute-start(f32[3,8,128]{2,1,0:T(8,128)S(1)} %fit.1), channel_id=1, source_target_pairs={{0,4},{1,5},{2,6},{3,7},{4,0},{5,1},{6,2},{7,3},{8,12},{9,13},{10,... | collective-permute-start | bytes 36872 | tf_op jit(solution)/shard_map/ppermute | solution.py:134
  75.6 3.3 %collective-permute-start.21 = (f32[3,8,128]{2,1,0:T(8,128)S(1)}, f32[3,8,128]{2,1,0:T(8,128)S(1)}, u32[]{:S(2)}, u32[]{:S(2)}) collective-permute-start(f32[3,8,128]{2,1,0:T(8,128)S(1)} %add_add_fusion.refs_8_), channel_id=1, source_target_pairs={{0,3},{1,2},{2,1},{3,0},{4,7},{5,6},{6,5},{7,4},{8,11},{9,10},{10,... | collective-permute-start | bytes 36872 | tf_op jit(solution)/shard_map/ppermute | solution.py:134
  75.7 3.8 %collective-permute-start.20 = (f32[3,8,128]{2,1,0:T(8,128)S(1)}, f32[3,8,128]{2,1,0:T(8,128)S(1)}, u32[]{:S(2)}, u32[]{:S(2)}) collective-permute-start(f32[3,8,128]{2,1,0:T(8,128)S(1)} %add_add_fusion.refs_8_), channel_id=1, source_target_pairs={{0,2},{1,3},{2,0},{3,1},{4,6},{5,7},{6,4},{7,5},{8,10},{9,11},{10,... | collective-permute-start | bytes 36872 | tf_op jit(solution)/shard_map/ppermute | solution.py:134
  77.3 2.2 %collective-permute-start.19 = (f32[3,8,128]{2,1,0:T(8,128)S(1)}, f32[3,8,128]{2,1,0:T(8,128)S(1)}, u32[]{:S(2)}, u32[]{:S(2)}) collective-permute-start(f32[3,8,128]{2,1,0:T(8,128)S(1)} %add_add_fusion.refs_8_), channel_id=1, source_target_pairs={{0,1},{1,0},{2,3},{3,2},{4,5},{5,4},{6,7},{7,6},{8,9},{9,8},{10,11... | collective-permute-start | bytes 36872 | tf_op jit(solution)/shard_map/ppermute | solution.py:134

commit v6 on v5

--- a/solution.py
+++ b/solution.py
@@ -204,7 +204,7 @@
 
 def turns(chips, parity, home=False):
     half = chips // 2
-    near, far = [*range(2, half), 1], [*range(half, chips)]
+    near, far = [*range(1, half)], [*range(half, chips, 2), *range(half + 1, chips, 2)]
     return far + near if bool(parity) != home else near + far
 
 
@@ -385,14 +385,14 @@
         name="focus_first",
     )(hbm(recorded), hbm(receiver_kernel))
     got = exchange(pieces, first, "away")
-    pieces = pl.pallas_call(
-        functools.partial(focus_rest_body, chips, rest),
-        in_specs=[resident] * 2,
-        out_shape=[piece] * len(rest),
-        compiler_params=medium(),
-        name="focus_rest",
-    )(slab_r, lhs)
-    got |= exchange(pieces, rest, "away")
+    for group in ((2, 3), (*range(4, own), own)):
+        pieces = pl.pallas_call(
+            functools.partial(focus_rest_body, chips, group),
+            in_specs=[resident] * 2,
+            out_shape=[piece] * len(group),
+            compiler_params=medium(),
+        )(slab_r, lhs)
+        got |= exchange(pieces, group, "away")
     early_own, early_peer = swap([got[o] for o in early])
     slab_s = pl.pallas_call(
         slab_body,
@@ -457,7 +457,7 @@
 
 
 def overlapping(panels):
-    return panels >= 8 and panels & (panels - 1) == 0
+    return panels >= 16 and panels & (panels - 1) == 0
 
 
 def per_device(recorded, receiver_kernel, source_kernel):

time: 81.4 us -> 76.7 us (0.942)
  starting transfers between devices: 43.2 us -> 35.2 us
  waiting for transfers between devices: 21.2 us -> 24.4 us
    ppermute x14, starting transfers between devices: 33 us -> 26.7 us  [exchange(): x = lax.ppermute(x, 'panel', pairs)]
    ppermute x2, starting transfers between devices: 3.79 us -> 1.55 us  [swap(): lax.ppermute(mine, 'panel', [(k, k ^ 1) for k in range(panels)])]
    ppermute x6, waiting for transfers between devices: 2.72 us -> 4.35 us  [partials(): lax.ppermute(x, axis, [(k, k ^ span * d) for k in range(n)])]
    ppermute x14, waiting for transfers between devices: 17 us -> 18.1 us  [exchange(): x = lax.ppermute(x, 'panel', pairs)]
    pallas_call x1 -> x2, Pallas kernels: 3.57 us -> 3.77 us  [piped(): pl.pallas_call(functools.partial(focus_rest_body, chips, group), in_specs...]
  transfers between devices with their start and end apart: 22 -> 22, of which waited for: 13 -> 12; matrix products, arithmetic and copies ran while one was open for 0% -> 0% of each run, Pallas kernels for 6% -> 12%
where the time goes in v6:
time: 76.7 us; the launch traced here: 76.5 us
  starting transfers between devices  35.2 us (46%)
  waiting for transfers between devices  24.4 us (32%)
  Pallas kernels  16.1 us (21%)
  between operations  0.79 us (1%)
    ppermute x14, starting transfers between devices, exchange(): x = lax.ppermute(x, 'panel', pairs)  26.7 us
    ppermute x14, waiting for transfers between devices, exchange(): x = lax.ppermute(x, 'panel', pairs)  18.1 us
    ppermute x6, starting transfers between devices, partials(): lax.ppermute(x, axis, [(k, k ^ span * d) for k in range(n)])  6.97 us
    ppermute x6, waiting for transfers between devices, partials(): lax.ppermute(x, axis, [(k, k ^ span * d) for k in range(n)])  4.35 us
    pallas_call x2, Pallas kernels, piped(): pl.pallas_call(functools.partial(focus_rest_body, chips, group), in_specs...  3.77 us
    pallas_call x1, Pallas kernels, piped(): pl.pallas_call(functools.partial(focus_first_body, chips, first), in_spec...  2.97 us
    pallas_call x2, Pallas kernels, finish(): pl.pallas_call(functools.partial(finish_body, chips, outs, late), in_spec...  2.59 us
    pallas_call x2, Pallas kernels, begin(): pl.pallas_call(functools.partial(begin_body, chips, outs, early), in_spec...  2.58 us
  transfers between devices with their start and end apart: 22, of which 12 were waited for; matrix products, arithmetic and copies ran while one was open for 0% of the time, Pallas kernels for 12%

profile of v6, /device:TPU:0, one launch (start us, length us, event | category | flops | bytes accessed | tf_op | source)
XLA Modules:
  0.0 76.5 jit_solution(11196638079314913794)
XLA Ops:
  0.6 3.0 %focus_first.1 = (bf16[128,512]{1,0:T(8,128)(2,1)S(1)}, bf16[128,512]{1,0:T(8,128)(2,1)S(1)}, bf16[2,128,4096]{2,1,0:T(8,128)(2,1)S(1)}, bf16[256,2048]{1,0:T(8,128)(2,1)S(1)}) custom-call(f32[1,2,128,2048]{3,2,1,0:T(8,128)} %data_ref.3, bf16[1,2,4095]{2,1,0:T(2,128)(2,1)} %kernel_hbm.1), custom_call_target="tpu_custom_call" | custom-call | tf_op jit(solution)/shard_map/focus_first/pallas_call | solution.py:373
  3.6 3.1 %collective-permute-start = (bf16[128,512]{1,0:T(8,128)(2,1)S(1)}, bf16[128,512]{1,0:T(8,128)(2,1)S(1)}, u32[]{:S(2)}, u32[]{:S(2)}) collective-permute-start(bf16[128,512]{1,0:T(8,128)(2,1)S(1)} %get-tuple-element.23), channel_id=1, source_target_pairs={{0,2},{1,9},{2,0},{3,11},{4,6},{5,13},{6,4},{7,15},{8,10},{9,1},{1... | collective-permute-start | bytes 393224 | tf_op jit(solution)/shard_map/ppermute | solution.py:360
  6.7 1.6 %collective-permute-start.1 = (bf16[128,512]{1,0:T(8,128)(2,1)S(1)}, bf16[128,512]{1,0:T(8,128)(2,1)S(1)}, u32[]{:S(2)}, u32[]{:S(2)}) collective-permute-start(bf16[128,512]{1,0:T(8,128)(2,1)S(1)} %get-tuple-element.24), channel_id=1, source_target_pairs={{0,4},{1,13},{2,6},{3,15},{4,0},{5,9},{6,2},{7,11},{8,12},{9,5},{1... | collective-permute-start | bytes 393224 | tf_op jit(solution)/shard_map/ppermute | solution.py:360
  8.2 1.3 %shard_map.51 = (bf16[128,512]{1,0:T(8,128)(2,1)S(1)}, bf16[128,512]{1,0:T(8,128)(2,1)S(1)}) custom-call(bf16[2,128,4096]{2,1,0:T(8,128)(2,1)S(1)} %get-tuple-element.20.slab_ref, bf16[256,2048]{1,0:T(8,128)(2,1)S(1)} %get-tuple-element.21.lhs_ref), custom_call_target="tpu_custom_call" | custom-call | tf_op jit(solution)/shard_map/pallas_call | solution.py:389
  9.6 0.0 copy-start.1
  9.6 0.1 collective-permute-start.2
  9.7 2.5 %shard_map.50 = (bf16[128,512]{1,0:T(8,128)(2,1)S(1)}, bf16[128,512]{1,0:T(8,128)(2,1)S(1)}, bf16[128,512]{1,0:T(8,128)(2,1)S(1)}, bf16[128,512]{1,0:T(8,128)(2,1)S(1)}) custom-call(bf16[2,128,4096]{2,1,0:T(8,128)(2,1)S(1)} %get-tuple-element.20.slab_ref, bf16[256,2048]{1,0:T(8,128)(2,1)S(1)} %get-tuple-element.21.lhs_ref), custom_call_target="tpu_custom_call" | custom-call | tf_op jit(solution)/shard_map/pallas_call | solution.py:389
  12.1 0.0 collective-permute-done.refs_1_
  12.1 0.5 collective-permute-done.1.refs_2_
  12.6 3.6 %collective-permute-done.2.refs_3_ = bf16[128,512]{1,0:T(8,128)(2,1)S(1)} collective-permute-done((bf16[128,512]{1,0:T(8,128)(2,1)S(1)}, bf16[128,512]{1,0:T(8,128)(2,1)S(1)}, u32[]{:S(2)}, u32[]{:S(2)}) %collective-permute-start.2) | collective-permute-done | bytes 131104 | tf_op jit(solution)/shard_map/ppermute | solution.py:360
  16.3 1.5 %collective-permute-start.3 = (bf16[4,128,512]{2,1,0:T(8,128)(2,1)S(1)}, bf16[4,128,512]{2,1,0:T(8,128)(2,1)S(1)}, u32[]{:S(2)}, u32[]{:S(2)}) collective-permute-start(bf16[4,128,512]{2,1,0:T(8,128)(2,1)S(1)} %shard_map.52.own_ref), channel_id=1, source_target_pairs={{0,1},{1,0},{2,3},{3,2},{4,5},{5,4},{6,7},{7,6},{8,9},{9,8},{10,11... | collective-permute-start | bytes 1572872 | tf_op jit(solution)/shard_map/ppermute | solution.py:371
  17.8 1.8 %collective-permute-start.4 = (bf16[128,512]{1,0:T(8,128)(2,1)S(1)}, bf16[128,512]{1,0:T(8,128)(2,1)S(1)}, u32[]{:S(2)}, u32[]{:S(2)}) collective-permute-start(bf16[128,512]{1,0:T(8,128)(2,1)S(1)} %get-tuple-element.26), channel_id=1, source_target_pairs={{0,8},{1,15},{2,10},{3,13},{4,12},{5,11},{6,14},{7,9},{8,0},{9,7},... | collective-permute-start | bytes 393224 | tf_op jit(solution)/shard_map/ppermute | solution.py:360
  19.6 1.7 %collective-permute-start.5 = (bf16[128,512]{1,0:T(8,128)(2,1)S(1)}, bf16[128,512]{1,0:T(8,128)(2,1)S(1)}, u32[]{:S(2)}, u32[]{:S(2)}) collective-permute-start(bf16[128,512]{1,0:T(8,128)(2,1)S(1)} %get-tuple-element.27), channel_id=1, source_target_pairs={{0,12},{1,3},{2,14},{3,1},{4,8},{5,7},{6,10},{7,5},{8,4},{9,11},{1... | collective-permute-start | bytes 393224 | tf_op jit(solution)/shard_map/ppermute | solution.py:360
  21.3 2.0 %collective-permute-start.6 = (bf16[128,512]{1,0:T(8,128)(2,1)S(1)}, bf16[128,512]{1,0:T(8,128)(2,1)S(1)}, u32[]{:S(2)}, u32[]{:S(2)}) collective-permute-start(bf16[128,512]{1,0:T(8,128)(2,1)S(1)} %get-tuple-element.28), channel_id=1, source_target_pairs={{0,10},{1,5},{2,8},{3,7},{4,14},{5,1},{6,12},{7,3},{8,2},{9,13},{1... | collective-permute-start | bytes 393224 | tf_op jit(solution)/shard_map/ppermute | solution.py:360
  23.3 1.9 %collective-permute-start.7 = (bf16[128,512]{1,0:T(8,128)(2,1)S(1)}, bf16[128,512]{1,0:T(8,128)(2,1)S(1)}, u32[]{:S(2)}, u32[]{:S(2)}) collective-permute-start(bf16[128,512]{1,0:T(8,128)(2,1)S(1)} %get-tuple-element.29), channel_id=1, source_target_pairs={{0,14},{1,7},{2,12},{3,5},{4,10},{5,3},{6,8},{7,1},{8,6},{9,15},{1... | collective-permute-start | bytes 393224 | tf_op jit(solution)/shard_map/ppermute | solution.py:360
  25.1 0.7 slab_source.1.slab_ref
  25.9 0.0 collective-permute-done.3.peer_ref
  25.9 1.9 %shard_map.53.refs_0_.acc_ref = f32[6,128,512]{2,1,0:T(8,128)S(1)} custom-call(bf16[2,128,4096]{2,1,0:T(8,128)(2,1)S(1)} %slab_source.1.slab_ref, bf16[4,128,512]{2,1,0:T(8,128)(2,1)S(1)} %shard_map.52.own_ref, bf16[4,128,512]{2,1,0:T(8,128)(2,1)S(1)} %collective-permute-done.3.peer_ref), custom_call_target="tpu_custom_call" | custom-call | tf_op jit(solution)/shard_map/pallas_call | solution.py:407
  27.8 0.7 collective-permute-done.5.refs_2_
  28.5 5.6 %collective-permute-done.6.refs_3_ = bf16[128,512]{1,0:T(8,128)(2,1)S(1)} collective-permute-done((bf16[128,512]{1,0:T(8,128)(2,1)S(1)}, bf16[128,512]{1,0:T(8,128)(2,1)S(1)}, u32[]{:S(2)}, u32[]{:S(2)}) %collective-permute-start.6) | collective-permute-done | bytes 131104 | tf_op jit(solution)/shard_map/ppermute | solution.py:360
  34.2 0.1 collective-permute-start.8
  34.2 1.9 %collective-permute-done.8.peer_ref = bf16[4,128,512]{2,1,0:T(8,128)(2,1)S(1)} collective-permute-done((bf16[4,128,512]{2,1,0:T(8,128)(2,1)S(1)}, bf16[4,128,512]{2,1,0:T(8,128)(2,1)S(1)}, u32[]{:S(2)}, u32[]{:S(2)}) %collective-permute-start.8) | collective-permute-done | bytes 524320 | tf_op jit(solution)/shard_map/ppermute | solution.py:371
  36.1 1.9 %shard_map.57 = (bf16[128,512]{1,0:T(8,128)(2,1)S(1)}, bf16[128,512]{1,0:T(8,128)(2,1)S(1)}, bf16[128,512]{1,0:T(8,128)(2,1)S(1)}, bf16[128,512]{1,0:T(8,128)(2,...) custom-call(bf16[2,128,4096]{2,1,0:T(8,128)(2,1)S(1)} %slab_source.1.slab_ref, ...), custom_call_target="tpu_custom_call" | custom-call | tf_op jit(solution)/shard_map/pallas_call | solution.py:415
  38.0 3.5 %collective-permute-start.11 = (bf16[128,512]{1,0:T(8,128)(2,1)S(1)}, bf16[128,512]{1,0:T(8,128)(2,1)S(1)}, u32[]{:S(2)}, u32[]{:S(2)}) collective-permute-start(bf16[128,512]{1,0:T(8,128)(2,1)S(1)} %get-tuple-element.32), channel_id=1, source_target_pairs={{0,10},{1,7},{2,8},{3,5},{4,14},{5,3},{6,12},{7,1},{8,2},{9,15},{1... | collective-permute-start | bytes 393224 | tf_op jit(solution)/shard_map/ppermute | solution.py:360
  41.5 1.8 %collective-permute-start.12 = (bf16[128,512]{1,0:T(8,128)(2,1)S(1)}, bf16[128,512]{1,0:T(8,128)(2,1)S(1)}, u32[]{:S(2)}, u32[]{:S(2)}) collective-permute-start(bf16[128,512]{1,0:T(8,128)(2,1)S(1)} %get-tuple-element.33), channel_id=1, source_target_pairs={{0,14},{1,9},{2,12},{3,11},{4,10},{5,13},{6,8},{7,15},{8,6},{9,1},... | collective-permute-start | bytes 393224 | tf_op jit(solution)/shard_map/ppermute | solution.py:360
  43.3 0.7 shard_map.55.acc_ref
  44.0 0.0 copy-start
  44.0 1.0 %collective-permute-start.13 = (bf16[128,512]{1,0:T(8,128)(2,1)S(1)}, bf16[128,512]{1,0:T(8,128)(2,1)S(1)}, u32[]{:S(2)}, u32[]{:S(2)}) collective-permute-start(bf16[128,512]{1,0:T(8,128)(2,1)S(1)} %get-tuple-element.34), channel_id=1, source_target_pairs={{0,2},{1,13},{2,0},{3,15},{4,6},{5,9},{6,4},{7,11},{8,10},{9,5},{1... | collective-permute-start | bytes 393224 | tf_op jit(solution)/shard_map/ppermute | solution.py:360
  45.0 2.6 %collective-permute-start.15 = (bf16[128,512]{1,0:T(8,128)(2,1)S(1)}, bf16[128,512]{1,0:T(8,128)(2,1)S(1)}, u32[]{:S(2)}, u32[]{:S(2)}) collective-permute-start(bf16[128,512]{1,0:T(8,128)(2,1)S(1)} %get-tuple-element.36), channel_id=1, source_target_pairs={{0,6},{1,15},{2,4},{3,13},{4,2},{5,11},{6,0},{7,9},{8,14},{9,7},{1... | collective-permute-start | bytes 393224 | tf_op jit(solution)/shard_map/ppermute | solution.py:360
  47.6 0.7 shard_map.56
  48.3 1.2 %collective-permute-start.9 = (bf16[128,512]{1,0:T(8,128)(2,1)S(1)}, bf16[128,512]{1,0:T(8,128)(2,1)S(1)}, u32[]{:S(2)}, u32[]{:S(2)}) collective-permute-start(bf16[128,512]{1,0:T(8,128)(2,1)S(1)} %get-tuple-element.30), channel_id=1, source_target_pairs={{0,8},{1,3},{2,10},{3,1},{4,12},{5,7},{6,14},{7,5},{8,0},{9,11},{1... | collective-permute-start | bytes 393224 | tf_op jit(solution)/shard_map/ppermute | solution.py:360
  49.6 1.2 %collective-permute-done.12.refs_3_ = bf16[128,512]{1,0:T(8,128)(2,1)S(1)} collective-permute-done((bf16[128,512]{1,0:T(8,128)(2,1)S(1)}, bf16[128,512]{1,0:T(8,128)(2,1)S(1)}, u32[]{:S(2)}, u32[]{:S(2)}) %collective-permute-start.12) | collective-permute-done | bytes 131104 | tf_op jit(solution)/shard_map/ppermute | solution.py:360
  50.8 4.5 %collective-permute-start.10 = (bf16[128,512]{1,0:T(8,128)(2,1)S(1)}, bf16[128,512]{1,0:T(8,128)(2,1)S(1)}, u32[]{:S(2)}, u32[]{:S(2)}) collective-permute-start(bf16[128,512]{1,0:T(8,128)(2,1)S(1)} %get-tuple-element.31), channel_id=1, source_target_pairs={{0,12},{1,5},{2,14},{3,7},{4,8},{5,1},{6,10},{7,3},{8,4},{9,13},{1... | collective-permute-start | bytes 393224 | tf_op jit(solution)/shard_map/ppermute | solution.py:360
  55.3 6.4 %collective-permute-done.9.refs_0_ = bf16[128,512]{1,0:T(8,128)(2,1)S(1)} collective-permute-done((bf16[128,512]{1,0:T(8,128)(2,1)S(1)}, bf16[128,512]{1,0:T(8,128)(2,1)S(1)}, u32[]{:S(2)}, u32[]{:S(2)}) %collective-permute-start.9) | collective-permute-done | bytes 131104 | tf_op jit(solution)/shard_map/ppermute | solution.py:360
  61.7 0.7 fit.1
  62.4 2.6 %collective-permute-start.18 = (f32[3,8,128]{2,1,0:T(8,128)S(1)}, f32[3,8,128]{2,1,0:T(8,128)S(1)}, u32[]{:S(2)}, u32[]{:S(2)}) collective-permute-start(f32[3,8,128]{2,1,0:T(8,128)S(1)} %fit.1), channel_id=1, source_target_pairs={{0,12},{1,13},{2,14},{3,15},{4,8},{5,9},{6,10},{7,11},{8,4},{9,5},... | collective-permute-start | bytes 36872 | tf_op jit(solution)/shard_map/ppermute | solution.py:134
  65.1 2.3 %collective-permute-start.17 = (f32[3,8,128]{2,1,0:T(8,128)S(1)}, f32[3,8,128]{2,1,0:T(8,128)S(1)}, u32[]{:S(2)}, u32[]{:S(2)}) collective-permute-start(f32[3,8,128]{2,1,0:T(8,128)S(1)} %fit.1), channel_id=1, source_target_pairs={{0,8},{1,9},{2,10},{3,11},{4,12},{5,13},{6,14},{7,15},{8,0},{9,1},... | collective-permute-start | bytes 36872 | tf_op jit(solution)/shard_map/ppermute | solution.py:134
  67.3 0.2 collective-permute-start.16
  67.6 0.4 collective-permute-done.18
  68.0 1.7 %collective-permute-done.17 = f32[3,8,128]{2,1,0:T(8,128)S(1)} collective-permute-done((f32[3,8,128]{2,1,0:T(8,128)S(1)}, f32[3,8,128]{2,1,0:T(8,128)S(1)}, u32[]{:S(2)}, u32[]{:S(2)}) %collective-permute-start.17) | collective-permute-done | bytes 12320 | tf_op jit(solution)/shard_map/ppermute | solution.py:134
  69.7 1.4 %collective-permute-done.16 = f32[3,8,128]{2,1,0:T(8,128)S(1)} collective-permute-done((f32[3,8,128]{2,1,0:T(8,128)S(1)}, f32[3,8,128]{2,1,0:T(8,128)S(1)}, u32[]{:S(2)}, u32[]{:S(2)}) %collective-permute-start.16) | collective-permute-done | bytes 12320 | tf_op jit(solution)/shard_map/ppermute | solution.py:134
  71.0 0.1 collective-permute-start.21
  71.1 1.1 %collective-permute-start.20 = (f32[3,8,128]{2,1,0:T(8,128)S(1)}, f32[3,8,128]{2,1,0:T(8,128)S(1)}, u32[]{:S(2)}, u32[]{:S(2)}) collective-permute-start(f32[3,8,128]{2,1,0:T(8,128)S(1)} %add_add_fusion.refs_8_), channel_id=1, source_target_pairs={{0,2},{1,3},{2,0},{3,1},{4,6},{5,7},{6,4},{7,5},{8,10},{9,11},{10,... | collective-permute-start | bytes 36872 | tf_op jit(solution)/shard_map/ppermute | solution.py:134
  72.2 0.7 collective-permute-start.19
  72.9 1.0 %deliver.1 = bf16[1,2,128,2048]{3,2,1,0:T(8,128)(2,1)} custom-call(bf16[128,512]{1,0:T(8,128)(2,1)S(1)} %collective-permute-done.9.refs_0_, bf16[128,512]{1,0:T(8,128)(2,1)S(1)} %collective-permute-done.10.refs_1_, bf16[128,512]{1,0:T(8,128)(2,1)S(1)} %collective-permute-done.11.refs_2_, bf16[128,512]{1,0:T(8,128)(2,1)S(1)} %collective-permute-done.12.refs_3_, ...), custom_call_target="tpu_custom_call" | custom-call | tf_op jit(solution)/shard_map/deliver/pallas_call | solution.py:438
  73.9 0.2 collective-permute-done.21.refs_11_
  74.2 0.6 collective-permute-done.20.refs_10_
  74.8 1.7 %subtract.1 = f32[1,2,128,2048]{3,2,1,0:T(8,128)} custom-call(f32[1,2,128,2048]{3,2,1,0:T(8,128)S(1)} %copy-done, bf16[128,512]{1,0:T(8,128)(2,1)S(1)} %collective-permute-done.9.refs_0_, bf16[128,512]{1,0:T(8,128)(2,1)S(1)} %collective-permute-done.10.refs_1_, bf16[128,512]{1,0:T(8,128)(2,1)S(1)} %collective-permute-done.11.refs_2_, ...), custom_call_target="tpu_custom_call" | custom-call | tf_op jit(solution)/shard_map/subtract/pallas_call | solution.py:447
  (14 shorter events, 0.1 us)
Async XLA Ops:
  3.6 8.5 %collective-permute-start = (bf16[128,512]{1,0:T(8,128)(2,1)S(1)}, bf16[128,512]{1,0:T(8,128)(2,1)S(1)}, u32[]{:S(2)}, u32[]{:S(2)}) collective-permute-start(bf16[128,512]{1,0:T(8,128)(2,1)S(1)} %get-tuple-element.23), channel_id=1, source_target_pairs={{0,2},{1,9},{2,0},{3,11},{4,6},{5,13},{6,4},{7,15},{8,10},{9,1},{1... | collective-permute-start | bytes 393224 | tf_op jit(solution)/shard_map/ppermute | solution.py:360
  6.7 6.0 %collective-permute-start.1 = (bf16[128,512]{1,0:T(8,128)(2,1)S(1)}, bf16[128,512]{1,0:T(8,128)(2,1)S(1)}, u32[]{:S(2)}, u32[]{:S(2)}) collective-permute-start(bf16[128,512]{1,0:T(8,128)(2,1)S(1)} %get-tuple-element.24), channel_id=1, source_target_pairs={{0,4},{1,13},{2,6},{3,15},{4,0},{5,9},{6,2},{7,11},{8,12},{9,5},{1... | collective-permute-start | bytes 393224 | tf_op jit(solution)/shard_map/ppermute | solution.py:360
  9.6 15.6 %copy-start.1 = (bf16[1,2,4095]{2,1,0:T(2,128)(2,1)S(1)}, bf16[1,2,4095]{2,1,0:T(2,128)(2,1)}, u32[]{:S(2)}) copy-start(bf16[1,2,4095]{2,1,0:T(2,128)(2,1)} %kernel_ref.1) | copy-start | bytes 49144
  9.6 6.7 %collective-permute-start.2 = (bf16[128,512]{1,0:T(8,128)(2,1)S(1)}, bf16[128,512]{1,0:T(8,128)(2,1)S(1)}, u32[]{:S(2)}, u32[]{:S(2)}) collective-permute-start(bf16[128,512]{1,0:T(8,128)(2,1)S(1)} %get-tuple-element.25), channel_id=1, source_target_pairs={{0,6},{1,11},{2,4},{3,9},{4,2},{5,15},{6,0},{7,13},{8,14},{9,3},{1... | collective-permute-start | bytes 393224 | tf_op jit(solution)/shard_map/ppermute | solution.py:360
  16.3 9.6 %collective-permute-start.3 = (bf16[4,128,512]{2,1,0:T(8,128)(2,1)S(1)}, bf16[4,128,512]{2,1,0:T(8,128)(2,1)S(1)}, u32[]{:S(2)}, u32[]{:S(2)}) collective-permute-start(bf16[4,128,512]{2,1,0:T(8,128)(2,1)S(1)} %shard_map.52.own_ref), channel_id=1, source_target_pairs={{0,1},{1,0},{2,3},{3,2},{4,5},{5,4},{6,7},{7,6},{8,9},{9,8},{10,11... | collective-permute-start | bytes 1572872 | tf_op jit(solution)/shard_map/ppermute | solution.py:371
  17.8 10.0 %collective-permute-start.4 = (bf16[128,512]{1,0:T(8,128)(2,1)S(1)}, bf16[128,512]{1,0:T(8,128)(2,1)S(1)}, u32[]{:S(2)}, u32[]{:S(2)}) collective-permute-start(bf16[128,512]{1,0:T(8,128)(2,1)S(1)} %get-tuple-element.26), channel_id=1, source_target_pairs={{0,8},{1,15},{2,10},{3,13},{4,12},{5,11},{6,14},{7,9},{8,0},{9,7},... | collective-permute-start | bytes 393224 | tf_op jit(solution)/shard_map/ppermute | solution.py:360
  19.6 8.9 %collective-permute-start.5 = (bf16[128,512]{1,0:T(8,128)(2,1)S(1)}, bf16[128,512]{1,0:T(8,128)(2,1)S(1)}, u32[]{:S(2)}, u32[]{:S(2)}) collective-permute-start(bf16[128,512]{1,0:T(8,128)(2,1)S(1)} %get-tuple-element.27), channel_id=1, source_target_pairs={{0,12},{1,3},{2,14},{3,1},{4,8},{5,7},{6,10},{7,5},{8,4},{9,11},{1... | collective-permute-start | bytes 393224 | tf_op jit(solution)/shard_map/ppermute | solution.py:360
  21.3 12.8 %collective-permute-start.6 = (bf16[128,512]{1,0:T(8,128)(2,1)S(1)}, bf16[128,512]{1,0:T(8,128)(2,1)S(1)}, u32[]{:S(2)}, u32[]{:S(2)}) collective-permute-start(bf16[128,512]{1,0:T(8,128)(2,1)S(1)} %get-tuple-element.28), channel_id=1, source_target_pairs={{0,10},{1,5},{2,8},{3,7},{4,14},{5,1},{6,12},{7,3},{8,2},{9,13},{1... | collective-permute-start | bytes 393224 | tf_op jit(solution)/shard_map/ppermute | solution.py:360
  23.3 10.8 %collective-permute-start.7 = (bf16[128,512]{1,0:T(8,128)(2,1)S(1)}, bf16[128,512]{1,0:T(8,128)(2,1)S(1)}, u32[]{:S(2)}, u32[]{:S(2)}) collective-permute-start(bf16[128,512]{1,0:T(8,128)(2,1)S(1)} %get-tuple-element.29), channel_id=1, source_target_pairs={{0,14},{1,7},{2,12},{3,5},{4,10},{5,3},{6,8},{7,1},{8,6},{9,15},{1... | collective-permute-start | bytes 393224 | tf_op jit(solution)/shard_map/ppermute | solution.py:360
  34.2 2.0 %collective-permute-start.8 = (bf16[4,128,512]{2,1,0:T(8,128)(2,1)S(1)}, bf16[4,128,512]{2,1,0:T(8,128)(2,1)S(1)}, u32[]{:S(2)}, u32[]{:S(2)}) collective-permute-start(bf16[4,128,512]{2,1,0:T(8,128)(2,1)S(1)} %shard_map.54.own_ref), channel_id=1, source_target_pairs={{0,1},{1,0},{2,3},{3,2},{4,5},{5,4},{6,7},{7,6},{8,9},{9,8},{10,11... | collective-permute-start | bytes 1572872 | tf_op jit(solution)/shard_map/ppermute | solution.py:371
  38.0 10.3 %collective-permute-start.11 = (bf16[128,512]{1,0:T(8,128)(2,1)S(1)}, bf16[128,512]{1,0:T(8,128)(2,1)S(1)}, u32[]{:S(2)}, u32[]{:S(2)}) collective-permute-start(bf16[128,512]{1,0:T(8,128)(2,1)S(1)} %get-tuple-element.32), channel_id=1, source_target_pairs={{0,10},{1,7},{2,8},{3,5},{4,14},{5,3},{6,12},{7,1},{8,2},{9,15},{1... | collective-permute-start | bytes 393224 | tf_op jit(solution)/shard_map/ppermute | solution.py:360
  41.5 9.2 %collective-permute-start.12 = (bf16[128,512]{1,0:T(8,128)(2,1)S(1)}, bf16[128,512]{1,0:T(8,128)(2,1)S(1)}, u32[]{:S(2)}, u32[]{:S(2)}) collective-permute-start(bf16[128,512]{1,0:T(8,128)(2,1)S(1)} %get-tuple-element.33), channel_id=1, source_target_pairs={{0,14},{1,9},{2,12},{3,11},{4,10},{5,13},{6,8},{7,15},{8,6},{9,1},... | collective-permute-start | bytes 393224 | tf_op jit(solution)/shard_map/ppermute | solution.py:360
  44.0 17.7 %copy-start = (f32[1,2,128,2048]{3,2,1,0:T(8,128)S(1)}, f32[1,2,128,2048]{3,2,1,0:T(8,128)}, u32[]{:S(2)}) copy-start(f32[1,2,128,2048]{3,2,1,0:T(8,128)} %data_ref.3) | copy-start | bytes 6291460
  44.0 11.2 %collective-permute-start.13 = (bf16[128,512]{1,0:T(8,128)(2,1)S(1)}, bf16[128,512]{1,0:T(8,128)(2,1)S(1)}, u32[]{:S(2)}, u32[]{:S(2)}) collective-permute-start(bf16[128,512]{1,0:T(8,128)(2,1)S(1)} %get-tuple-element.34), channel_id=1, source_target_pairs={{0,2},{1,13},{2,0},{3,15},{4,6},{5,9},{6,4},{7,11},{8,10},{9,5},{1... | collective-permute-start | bytes 393224 | tf_op jit(solution)/shard_map/ppermute | solution.py:360
  45.0 10.3 %collective-permute-start.14 = (bf16[128,512]{1,0:T(8,128)(2,1)S(1)}, bf16[128,512]{1,0:T(8,128)(2,1)S(1)}, u32[]{:S(2)}, u32[]{:S(2)}) collective-permute-start(bf16[128,512]{1,0:T(8,128)(2,1)S(1)} %get-tuple-element.35), channel_id=1, source_target_pairs={{0,4},{1,11},{2,6},{3,9},{4,0},{5,15},{6,2},{7,13},{8,12},{9,3},{1... | collective-permute-start | bytes 393224 | tf_op jit(solution)/shard_map/ppermute | solution.py:360
  45.0 10.3 %collective-permute-start.15 = (bf16[128,512]{1,0:T(8,128)(2,1)S(1)}, bf16[128,512]{1,0:T(8,128)(2,1)S(1)}, u32[]{:S(2)}, u32[]{:S(2)}) collective-permute-start(bf16[128,512]{1,0:T(8,128)(2,1)S(1)} %get-tuple-element.36), channel_id=1, source_target_pairs={{0,6},{1,15},{2,4},{3,13},{4,2},{5,11},{6,0},{7,9},{8,14},{9,7},{1... | collective-permute-start | bytes 393224 | tf_op jit(solution)/shard_map/ppermute | solution.py:360
  48.3 13.4 %collective-permute-start.9 = (bf16[128,512]{1,0:T(8,128)(2,1)S(1)}, bf16[128,512]{1,0:T(8,128)(2,1)S(1)}, u32[]{:S(2)}, u32[]{:S(2)}) collective-permute-start(bf16[128,512]{1,0:T(8,128)(2,1)S(1)} %get-tuple-element.30), channel_id=1, source_target_pairs={{0,8},{1,3},{2,10},{3,1},{4,12},{5,7},{6,14},{7,5},{8,0},{9,11},{1... | collective-permute-start | bytes 393224 | tf_op jit(solution)/shard_map/ppermute | solution.py:360
  50.8 11.0 %collective-permute-start.10 = (bf16[128,512]{1,0:T(8,128)(2,1)S(1)}, bf16[128,512]{1,0:T(8,128)(2,1)S(1)}, u32[]{:S(2)}, u32[]{:S(2)}) collective-permute-start(bf16[128,512]{1,0:T(8,128)(2,1)S(1)} %get-tuple-element.31), channel_id=1, source_target_pairs={{0,12},{1,5},{2,14},{3,7},{4,8},{5,1},{6,10},{7,3},{8,4},{9,13},{1... | collective-permute-start | bytes 393224 | tf_op jit(solution)/shard_map/ppermute | solution.py:360
  62.4 5.6 %collective-permute-start.18 = (f32[3,8,128]{2,1,0:T(8,128)S(1)}, f32[3,8,128]{2,1,0:T(8,128)S(1)}, u32[]{:S(2)}, u32[]{:S(2)}) collective-permute-start(f32[3,8,128]{2,1,0:T(8,128)S(1)} %fit.1), channel_id=1, source_target_pairs={{0,12},{1,13},{2,14},{3,15},{4,8},{5,9},{6,10},{7,11},{8,4},{9,5},... | collective-permute-start | bytes 36872 | tf_op jit(solution)/shard_map/ppermute | solution.py:134
  65.1 4.6 %collective-permute-start.17 = (f32[3,8,128]{2,1,0:T(8,128)S(1)}, f32[3,8,128]{2,1,0:T(8,128)S(1)}, u32[]{:S(2)}, u32[]{:S(2)}) collective-permute-start(f32[3,8,128]{2,1,0:T(8,128)S(1)} %fit.1), channel_id=1, source_target_pairs={{0,8},{1,9},{2,10},{3,11},{4,12},{5,13},{6,14},{7,15},{8,0},{9,1},... | collective-permute-start | bytes 36872 | tf_op jit(solution)/shard_map/ppermute | solution.py:134
  67.3 3.7 %collective-permute-start.16 = (f32[3,8,128]{2,1,0:T(8,128)S(1)}, f32[3,8,128]{2,1,0:T(8,128)S(1)}, u32[]{:S(2)}, u32[]{:S(2)}) collective-permute-start(f32[3,8,128]{2,1,0:T(8,128)S(1)} %fit.1), channel_id=1, source_target_pairs={{0,4},{1,5},{2,6},{3,7},{4,0},{5,1},{6,2},{7,3},{8,12},{9,13},{10,... | collective-permute-start | bytes 36872 | tf_op jit(solution)/shard_map/ppermute | solution.py:134
  71.0 3.1 %collective-permute-start.21 = (f32[3,8,128]{2,1,0:T(8,128)S(1)}, f32[3,8,128]{2,1,0:T(8,128)S(1)}, u32[]{:S(2)}, u32[]{:S(2)}) collective-permute-start(f32[3,8,128]{2,1,0:T(8,128)S(1)} %add_add_fusion.refs_8_), channel_id=1, source_target_pairs={{0,3},{1,2},{2,1},{3,0},{4,7},{5,6},{6,5},{7,4},{8,11},{9,10},{10,... | collective-permute-start | bytes 36872 | tf_op jit(solution)/shard_map/ppermute | solution.py:134
  71.1 3.7 %collective-permute-start.20 = (f32[3,8,128]{2,1,0:T(8,128)S(1)}, f32[3,8,128]{2,1,0:T(8,128)S(1)}, u32[]{:S(2)}, u32[]{:S(2)}) collective-permute-start(f32[3,8,128]{2,1,0:T(8,128)S(1)} %add_add_fusion.refs_8_), channel_id=1, source_target_pairs={{0,2},{1,3},{2,0},{3,1},{4,6},{5,7},{6,4},{7,5},{8,10},{9,11},{10,... | collective-permute-start | bytes 36872 | tf_op jit(solution)/shard_map/ppermute | solution.py:134
  72.2 2.6 %collective-permute-start.19 = (f32[3,8,128]{2,1,0:T(8,128)S(1)}, f32[3,8,128]{2,1,0:T(8,128)S(1)}, u32[]{:S(2)}, u32[]{:S(2)}) collective-permute-start(f32[3,8,128]{2,1,0:T(8,128)S(1)} %add_add_fusion.refs_8_), channel_id=1, source_target_pairs={{0,1},{1,0},{2,3},{3,2},{4,5},{5,4},{6,7},{7,6},{8,9},{9,8},{10,11... | collective-permute-start | bytes 36872 | tf_op jit(solution)/shard_map/ppermute | solution.py:134
